TPU v7x, 128 devices: a whole 4x4x4 slice. The times are simulated.
128 devices in a mesh: seq: 16 (over y_lo, z, core), mp: 8 (over y_hi, x).
Axes of the slice: x: 4, y: 4 (y_hi: 2, y_lo: 2; y = y_hi * 2 + y_lo), z: 4, core: 2. Of those that a mesh axis runs over, the one named last changes fastest.
Arguments:
- hidden_in: bfloat16 [8192, 4096], P('seq', 'mp'), may hold values from -30 to 30
- norm_gain: float32 [4096], replicated, may hold values from 0.1 to 1.9
- w_z: bfloat16 [4096, 8192], P('seq', 'mp'), may hold values from -0.09375 to 0.09375
- w_x: bfloat16 [4096, 8192], P('seq', 'mp'), may hold values from -0.09375 to 0.09375
- w_b: bfloat16 [4096, 1024], P('seq', 'mp'), may hold values from -0.09375 to 0.09375
- w_c: bfloat16 [4096, 1024], P('seq', 'mp'), may hold values from -0.09375 to 0.09375
- w_dt: bfloat16 [4096, 128], P('seq', 'mp'), may hold values from -0.0625 to 0.0625
- conv_x: float32 [4, 8192], P(None, 'mp'), may hold values from -3 to 3
- conv_b: float32 [4, 1024], P(None, 'mp'), may hold values from -3 to 3
- conv_c: float32 [4, 1024], P(None, 'mp'), may hold values from -3 to 3
- dt_bias: float32 [128], P('mp'), may hold values from -9 to -5
- a_rate: float32 [128], P('mp'), may hold values from 0.5 to 16
- skip_gain: float32 [128], P('mp'), may hold values from -3 to 3
- group_gain: float32 [8192], P('mp'), may hold values from 0.1 to 1.9
- w_out: bfloat16 [8192, 4096], P('mp', 'seq'), may hold values from -0.0625 to 0.0625
- attn_gain: float32 [4096], replicated, may hold values from 0.1 to 1.9
- w_q: bfloat16 [4096, 4096], P(None, 'mp'), may hold values from -0.125 to 0.125
- w_k: bfloat16 [4096, 1024], P(None, 'mp'), may hold values from -0.125 to 0.125
- w_v: bfloat16 [4096, 1024], P(None, 'mp'), may hold values from -0.09375 to 0.09375
Outputs:
- mixed: float32 [8192, 4096], P('seq', 'mp')
- context: float32 [8192, 4096], P('seq', 'mp')
All inputs are finite; a program needn't handle non-finite values.
Results may differ from a plain program's by a relative error of at most 0.017.
Values may be sent and summed in bfloat16 or wider, within the bound.
A program may use at most 128 MiB of HBM per device.

v0:
```python
import jax
import jax.numpy as jnp
from jax import lax
from jax.sharding import PartitionSpec as P

P_SIZE = 64
N = 128
HD = 128
WINDOW = 4096
QB = 128


def side_by_side(arrays, axis, dim, along):
    widths = [a.shape[along] for a in arrays]
    both = jnp.concatenate(arrays, axis=along)
    whole = lax.all_gather(both, axis, axis=dim, tiled=True)
    return tuple(jnp.split(whole, [sum(widths[:k]) for k in range(1, len(widths))], axis=along))


def from_behind(block, axis, distance):
    devices = range(lax.axis_size(axis))
    route = [(i - distance, i) for i in devices if i - distance in devices]
    return lax.ppermute(block, axis, route)


def carried_in(part, axis, combine, identity):
    place = lax.axis_index(axis)
    gathered = jax.tree.map(lambda a: lax.all_gather(a, axis), part)
    state = jax.tree.map(lambda a, e: jnp.zeros_like(a) + jnp.asarray(e, a.dtype), part, identity)

    def one(lap, state):
        return combine(
            state, jax.tree.map(lambda a: lax.dynamic_index_in_dim(a, lap, 0, False), gathered)
        )

    return lax.fori_loop(0, place, one, state)


def in_order(parts, dim):
    dims = list(parts.shape[1:])
    dims[dim] *= parts.shape[0]
    return jnp.moveaxis(parts, 0, dim).reshape(dims)


def work_in_pieces(array, axis, dim, apply, out_dim):
    size, rows = (lax.axis_size(axis), array.shape[dim])
    count = 2 if rows % 2 == 0 else 1
    finished, length = ([], rows // count)
    for k in range(count):
        piece = lax.slice_in_dim(array, k * length, (k + 1) * length, axis=dim)
        starts = jnp.arange(size) * rows + k * length
        finished.append(jax.vmap(apply)(lax.all_gather(piece, axis), starts))
    return in_order(jnp.concatenate(finished, axis=out_dim + 1), out_dim)


def rms_norm(values, gain):
    return values * lax.rsqrt(jnp.mean(values * values, axis=-1, keepdims=True) + 1e-05) * gain


def causal_conv(values, rim, device_routine):
    padded = jnp.concatenate([rim, values], axis=0)
    length = values.shape[0]
    summed = jnp.zeros(values.shape, jnp.float32)
    for offset in range(device_routine.shape[0]):
        summed = summed + device_routine[offset][None, :] * padded[offset : offset + length]
    return jax.nn.silu(summed)


def ssd_block(carry_state, pieces):
    inputs, step_sizes, decays, keys_b, reads_c = pieces
    per_group = inputs.shape[1] // keys_b.shape[1]
    b_heads = jnp.repeat(keys_b, per_group, axis=1)
    c_heads = jnp.repeat(reads_c, per_group, axis=1)
    cumulative = jnp.cumsum(decays, axis=0)
    length = inputs.shape[0]
    causal_mask = jnp.arange(length)[:, None] >= jnp.arange(length)[None, :]
    spread = cumulative[:, None, :] - cumulative[None, :, :]
    within = jnp.exp(jnp.where(causal_mask[:, :, None], spread, -jnp.inf))
    affinity = jnp.einsum("tgn,sgn->gts", reads_c, keys_b)
    affinity = jnp.repeat(affinity, per_group, axis=0)
    mixing = affinity * jnp.transpose(within, (2, 0, 1)) * jnp.transpose(step_sizes)[:, None, :]
    inside = jnp.einsum("hts,shp->thp", mixing, inputs)
    carried = jnp.exp(cumulative)[:, :, None] * jnp.einsum("thn,hpn->thp", c_heads, carry_state)
    tail_weight = jnp.exp(cumulative[-1][None, :] - cumulative) * step_sizes
    fresh_state = jnp.einsum("sh,shp,shn->hpn", tail_weight, inputs, b_heads)
    updated = jnp.exp(cumulative[-1])[:, None, None] * carry_state + fresh_state
    return (updated, inside + carried)


def run_ssd(inputs, step_sizes, decays, keys_b, reads_c, block, carry_state):
    total_rows = inputs.shape[0]
    block_count = total_rows // block

    def blocked(values):
        return values.reshape((block_count, block) + values.shape[1:])

    final_state, outputs = lax.scan(
        ssd_block,
        carry_state,
        (blocked(inputs), blocked(step_sizes), blocked(decays), blocked(keys_b), blocked(reads_c)),
    )
    return (final_state, outputs.reshape((total_rows,) + outputs.shape[2:]))


def window_attention(asking_vectors, keys, values, shift_rows, first_key):
    per_kv = asking_vectors.shape[1] // keys.shape[1]
    keys_all = jnp.repeat(keys, per_kv, axis=1)
    values_all = jnp.repeat(values, per_kv, axis=1)
    query_rows = asking_vectors.shape[0]
    key_count = keys.shape[0]
    scale = asking_vectors.shape[2] ** (-0.5)
    index_offsets = jnp.arange(key_count)[None, :] - shift_rows - jnp.arange(query_rows)[:, None]
    allowed = (
        (index_offsets <= 0)
        & (index_offsets > -WINDOW)
        & (first_key + jnp.arange(key_count) >= 0)[None, :]
    )

    def one_head(operands):
        query_h, key_h, value_h = operands
        scores = (
            lax.dot_general(
                query_h, key_h, (((1,), (1,)), ((), ())), preferred_element_type=jnp.float32
            )
            * scale
        )
        scores = jnp.where(allowed, scores, -jnp.inf)
        row_peak = jnp.max(scores, axis=1, keepdims=True)
        exp_scores = jnp.exp(scores - row_peak)
        weights = (exp_scores / jnp.sum(exp_scores, axis=1, keepdims=True)).astype(jnp.bfloat16)
        return jnp.dot(weights, value_h, preferred_element_type=jnp.float32)

    outputs = lax.map(
        one_head,
        (
            jnp.transpose(asking_vectors, (1, 0, 2)),
            jnp.transpose(keys_all, (1, 0, 2)),
            jnp.transpose(values_all, (1, 0, 2)),
        ),
    )
    return jnp.transpose(outputs, (1, 0, 2)).reshape(query_rows, -1)


def on_device(
    hidden_in,
    norm_gain,
    w_z,
    w_x,
    w_b,
    w_c,
    w_dt,
    conv_x,
    conv_b,
    conv_c,
    dt_bias,
    a_rate,
    skip_gain,
    group_gain,
    w_out,
    attn_gain,
    w_q,
    w_k,
    w_v,
):
    rows_here = hidden_in.shape[0]
    whole_rows = lax.all_gather(hidden_in, "mp", axis=1, tiled=True)
    normed = rms_norm(whole_rows.astype(jnp.float32), norm_gain).astype(jnp.bfloat16)

    def add_rows(piece):
        return jnp.dot(normed, piece, preferred_element_type=jnp.float32)

    pieces = side_by_side((w_x, w_b, w_c, w_dt), "seq", 0, 1)
    input_mapped, b_proj, c_proj, delta_time_unscaled = tuple((add_rows(piece) for piece in pieces))
    rim_rows = conv_x.shape[0] - 1
    rims = from_behind(
        (
            input_mapped[rows_here - rim_rows :],
            b_proj[rows_here - rim_rows :],
            c_proj[rows_here - rim_rows :],
        ),
        "seq",
        1,
    )
    conv_in = causal_conv(input_mapped, rims[0], conv_x)
    conv_bv = causal_conv(b_proj, rims[1], conv_b)
    conv_cv = causal_conv(c_proj, rims[2], conv_c)
    step_sizes = jax.nn.softplus(delta_time_unscaled + dt_bias[None, :])
    decays = -a_rate[None, :] * step_sizes
    heads_here = dt_bias.shape[0]
    groups_here = conv_b.shape[1] // N
    inputs = conv_in.reshape(rows_here, heads_here, P_SIZE)
    keys_b = conv_bv.reshape(rows_here, groups_here, N)
    reads_c = conv_cv.reshape(rows_here, groups_here, N)
    start_state = jnp.zeros((heads_here, P_SIZE, N), jnp.float32)
    local_state, ssd_out = run_ssd(inputs, step_sizes, decays, keys_b, reads_c, QB, start_state)
    cumulative = jnp.cumsum(decays, axis=0)
    decay_total = jnp.exp(cumulative[-1])

    def combine(earlier, later):
        return (earlier[0] * later[0], later[0][:, None, None] * earlier[1] + later[1])

    identity = (jnp.ones_like(decay_total), jnp.zeros_like(local_state))
    incoming = carried_in((decay_total, local_state), "seq", combine, identity)[1]
    c_heads = jnp.repeat(reads_c, heads_here // groups_here, axis=1)
    ssd_out = ssd_out + jnp.exp(cumulative)[:, :, None] * jnp.einsum(
        "thn,hpn->thp", c_heads, incoming
    )
    gate_proj = add_rows(lax.all_gather(w_z, "seq", axis=0, tiled=True))
    full = ssd_out + skip_gain[None, :, None] * inputs
    gated = full.reshape(rows_here, -1) * jax.nn.silu(gate_proj)
    grouped = gated.reshape(rows_here, groups_here, -1)
    y_normed = (
        rms_norm(grouped, group_gain.reshape(groups_here, -1))
        .reshape(rows_here, -1)
        .astype(jnp.bfloat16)
    )

    def project(piece, start):
        return jnp.dot(y_normed, piece, preferred_element_type=jnp.float32)

    terms = work_in_pieces(w_out, "seq", 1, project, 1)
    rounded = lax.optimization_barrier(terms.astype(jnp.bfloat16)).astype(jnp.float32)
    summed = lax.psum_scatter(
        rounded.astype(jnp.bfloat16), "mp", scatter_dimension=1, tiled=True
    ).astype(jnp.float32)
    mixed = hidden_in.astype(jnp.float32) + summed
    mixed_low = mixed.astype(jnp.bfloat16)
    stream_rows = lax.all_gather(mixed_low, "mp", axis=1, tiled=True)
    normed_two = rms_norm(stream_rows.astype(jnp.float32), attn_gain).astype(jnp.bfloat16)
    asking_vectors = jnp.dot(normed_two, w_q, preferred_element_type=jnp.float32).astype(
        jnp.bfloat16
    )
    own_keys = jnp.dot(normed_two, w_k, preferred_element_type=jnp.float32).astype(jnp.bfloat16)
    own_values = jnp.dot(normed_two, w_v, preferred_element_type=jnp.float32).astype(jnp.bfloat16)
    reach = WINDOW // rows_here
    key_parts = [own_keys]
    value_parts = [own_values]
    for distance in range(1, reach + 1):
        arrived = from_behind((own_keys, own_values), "seq", distance)
        key_parts.insert(0, arrived[0])
        value_parts.insert(0, arrived[1])
    kv_heads = own_keys.shape[1] // HD
    key_rows = jnp.concatenate(key_parts, axis=0).reshape(-1, kv_heads, HD)
    value_rows = jnp.concatenate(value_parts, axis=0).reshape(-1, kv_heads, HD)
    first_key = lax.axis_index("seq") * rows_here - reach * rows_here
    context = window_attention(
        asking_vectors.reshape(rows_here, -1, HD),
        key_rows,
        value_rows,
        reach * rows_here,
        first_key,
    )
    return (mixed, context)


def solution(mesh):
    placed = (
        P("seq", "mp"),
        P(),
        P("seq", "mp"),
        P("seq", "mp"),
        P("seq", "mp"),
        P("seq", "mp"),
        P("seq", "mp"),
        P(None, "mp"),
        P(None, "mp"),
        P(None, "mp"),
        P("mp"),
        P("mp"),
        P("mp"),
        P("mp"),
        P("mp", "seq"),
        P(),
        P(None, "mp"),
        P(None, "mp"),
        P(None, "mp"),
    )
    return jax.shard_map(
        on_device,
        mesh=mesh,
        in_specs=placed,
        out_specs=(P("seq", "mp"), P("seq", "mp")),
        check_vma=False,
    )
```

profile of v0, /device:TPU:8, one launch (start us, length us, event | category | flops | bytes accessed | tf_op | source)
XLA Modules:
  0.0 659.0 jit_solution(6856268379291212277)
XLA Ops:
  13.2 75.5 %all-gather.12.cloned.1.call-done = bf16[512,4096]{1,0:T(8,128)(2,1)} async-done(((bf16[512,512]{1,0:T(8,128)(2,1)}), bf16[512,4096]{1,0:T(8,128)(2,1)}) %all-gather.12.cloned.1.call-update) | async-done | bytes 4194320 | tf_op jit(solution)/shard_map/all_gather | solution.py:166
  95.8 61.8 %all-gather.14.cloned.1.call-done = bf16[4096,1296]{1,0:T(8,128)(2,1)} async-done(((bf16[256,1296]{1,0:T(8,128)(2,1)}), bf16[4096,1296]{1,0:T(8,128)(2,1)}) %all-gather.14.cloned.1.call-update) | async-done | bytes 10616848 | tf_op jit(solution)/shard_map/all_gather | solution.py:16
  157.5 9.2 %fusion.55 = f32[512,1024]{1,0:T(8,128)S(1)} fusion(bf16[512,4096]{1,0:T(8,128)(2,1)} %fusion.51, bf16[4096,1296]{1,0:T(8,128)(2,1)} %all-gather.14.cloned.1.call-done), kind=kOutput, calls=%fused_computation.71 | convolution fusion | flops 4294967296 | bytes 14680064 | tf_op jit(solution)/shard_map/dot_general | solution.py:170
  185.3 5.6 divide_multiply_fusion
  190.9 4.5 reshape.170
  199.5 75.0 %while.38 = (s32[]{:T(128)}, f32[16,64,128]{2,1,0:T(8,128)S(1)}, f32[4,128,16,64]{1,0,3,2:T(4,128)}, f32[4,128,16]{2,1,0:T(8,128)S(1)}, f32[4,128,16]{2,1,0:T(8,...) while((s32[]{:T(128)}, f32[16,64,128]{2,1,0:T(8,128)S(1)}, ...), condition=%wide.region_3.4_spmd.clone, body=%wide.region_1.3_spmd.clone.sunk | while | flops 107104256 | bytes 5596684 | solution.py:97
  202.9 13.9 %dynamic_update_slice.14 = f32[4,128,16,64]{1,0,3,2:T(4,128)} dynamic-update-slice(f32[4,128,16,64]{1,0,3,2:T(4,128)} %get-tuple-element.426, f32[1,128,16,64]{1,0,3,2:T(1,128)S(1)} %bitcast.207, s32[]{:T(128)} %get-tuple-element.424, s32[]{:T(128)} %constant.90.clone.1..sunk.1, s32[]{:T(128)} %constant.90.clone.1..sunk.1, s32[]{:T(128)} %constant.90.clone.1..sunk.1) | dynamic-update-slice | bytes 1048580 | tf_op jit(solution)/shard_map/while/body/jit(dynamic_update_index_in_dim)/dynamic_update_slice | solution.py:97
  221.7 13.9 %dynamic_update_slice.14 = f32[4,128,16,64]{1,0,3,2:T(4,128)} dynamic-update-slice(f32[4,128,16,64]{1,0,3,2:T(4,128)} %get-tuple-element.426, f32[1,128,16,64]{1,0,3,2:T(1,128)S(1)} %bitcast.207, s32[]{:T(128)} %get-tuple-element.424, s32[]{:T(128)} %constant.90.clone.1..sunk.1, s32[]{:T(128)} %constant.90.clone.1..sunk.1, s32[]{:T(128)} %constant.90.clone.1..sunk.1) | dynamic-update-slice | bytes 1048580 | tf_op jit(solution)/shard_map/while/body/jit(dynamic_update_index_in_dim)/dynamic_update_slice | solution.py:97
  240.4 13.9 %dynamic_update_slice.14 = f32[4,128,16,64]{1,0,3,2:T(4,128)} dynamic-update-slice(f32[4,128,16,64]{1,0,3,2:T(4,128)} %get-tuple-element.426, f32[1,128,16,64]{1,0,3,2:T(1,128)S(1)} %bitcast.207, s32[]{:T(128)} %get-tuple-element.424, s32[]{:T(128)} %constant.90.clone.1..sunk.1, s32[]{:T(128)} %constant.90.clone.1..sunk.1, s32[]{:T(128)} %constant.90.clone.1..sunk.1) | dynamic-update-slice | bytes 1048580 | tf_op jit(solution)/shard_map/while/body/jit(dynamic_update_index_in_dim)/dynamic_update_slice | solution.py:97
  259.2 13.9 %dynamic_update_slice.14 = f32[4,128,16,64]{1,0,3,2:T(4,128)} dynamic-update-slice(f32[4,128,16,64]{1,0,3,2:T(4,128)} %get-tuple-element.426, f32[1,128,16,64]{1,0,3,2:T(1,128)S(1)} %bitcast.207, s32[]{:T(128)} %get-tuple-element.424, s32[]{:T(128)} %constant.90.clone.1..sunk.1, s32[]{:T(128)} %constant.90.clone.1..sunk.1, s32[]{:T(128)} %constant.90.clone.1..sunk.1) | dynamic-update-slice | bytes 1048580 | tf_op jit(solution)/shard_map/while/body/jit(dynamic_update_index_in_dim)/dynamic_update_slice | solution.py:97
  275.4 6.5 copy.101
  281.8 6.4 copy.102
  290.6 10.8 %fusion.109 = f32[512,1024]{1,0:T(8,128)} fusion(bf16[512,4096]{1,0:T(8,128)(2,1)} %fusion.51, bf16[4096,1024]{1,0:T(8,128)(2,1)} %all-gather.16.cloned.1.call-done), kind=kOutput, calls=%fused_computation.189 | convolution fusion | flops 4294967296 | bytes 14680064 | tf_op jit(solution)/shard_map/dot_general | solution.py:170
  303.0 19.4 %all-gather.3 = f32[16,1,16]{2,1,0:T(1,128)S(1)} all-gather(f32[1,1,16]{2,1,0:T(1,128)S(1)} %bitcast.230), channel_id=1, replica_groups=mesh['seq'=16,'mp'=8] {'seq'}, dimensions={0}, use_global_device_ids=true | all-gather | bytes 1088 | tf_op jit(solution)/shard_map/all_gather | solution.py:28
  327.5 18.5 %all-gather.20.cloned.1.call-done = f32[256,64,128]{2,1,0:T(8,128)} async-done(((f32[16,64,128]{2,1,0:T(8,128)}), f32[256,64,128]{2,1,0:T(8,128)}) %all-gather.20.cloned.1.call-update) | async-done | bytes 8388624 | tf_op jit(solution)/shard_map/all_gather | solution.py:28
  346.0 10.1 %while.36 = (s32[]{:T(128)}, f32[16,64,128]{2,1,0:T(8,128)S(1)}, s32[]{:T(128)}, f32[16,16]{1,0:T(8,128)S(1)}, f32[16,16,64,128]{3,2,1,0:T(8,128)}, /*index=5*/s32[]{:T(128)}, s32[]{:T(128)}, s32[]{:T(128)}) while((s32[]{:T(128)}, f32[16,64,128]{2,1,0:T(8,128)S(1)}, s32[]{:T(128)}, f32[16,16]{1,0:T(8,128)S(1)}, f32[16,16,64,128]{3,2,1,0:T(8,128)}, ...), condition=%wide.region_7.8_spmd, body=%wide.region_6.7_spmd.sunk | while | flops 262149 | bytes 1573183 | solution.py:36
  373.2 6.4 copy.103
  379.7 93.1 %reduce-scatter.2.cloned.1.call-done = bf16[512,512]{1,0:T(8,128)(2,1)} async-done(((bf16[512,4096]{1,0:T(8,128)(2,1)}), bf16[512,512]{1,0:T(8,128)(2,1)}) %reduce-scatter.2.cloned.1.call-update) | async-done | bytes 524304 | tf_op jit(solution)/shard_map/reduce_scatter | solution.py:223
  475.3 76.2 %all-gather.18.cloned.1.call-done = bf16[512,4096]{1,0:T(8,128)(2,1)} async-done(((bf16[512,512]{1,0:T(8,128)(2,1)}), bf16[512,4096]{1,0:T(8,128)(2,1)}) %all-gather.18.cloned.1.call-update) | async-done | bytes 4194320 | tf_op jit(solution)/shard_map/all_gather | solution.py:228
  612.9 37.2 %while.37 = (s32[]{:T(128)}, f32[4,512,128]{2,1,0:T(8,128)S(1)}, bf16[4,512,128]{2,1,0:T(8,128)(2,1)S(1)}, bf16[4,4608,128]{2,1,0:T(8,128)(2,1)}, bf16[4,4608,12...) while((s32[]{:T(128)}, f32[4,512,128]{2,1,0:T(8,128)S(1)}, ...), condition=%wide.region_14.15_spmd.clone, body=%wide.region_11.14_spmd.clone.sunk | while | flops 1238629376 | bytes 31102036 | solution.py:133
  612.9 5.0 fusion.142
  622.2 5.0 fusion.142
  631.5 5.0 fusion.142
  640.8 5.0 fusion.142
  (262 shorter events, 173.4 us)
Async XLA Ops:
  7.2 81.5 %all-gather.12.cloned.1.call-start = ((), (), s32[]{:S(2)}) async-start(), calls=%async_computation.1 | async-start | bytes 4718592 | tf_op jit(solution)/shard_map/all_gather | solution.py:166
  7.9 149.6 %all-gather.14.cloned.1.call-start = ((), (), s32[]{:S(2)}) async-start(), calls=%async_computation.2 | async-start | bytes 12255232 | tf_op jit(solution)/shard_map/all_gather | solution.py:16
  10.9 264.4 %all-gather.22.cloned.1.call-start = ((), (), s32[]{:S(2)}) async-start(), calls=%async_computation.7 | async-start | bytes 4456448 | tf_op jit(solution)/shard_map/all_gather | solution.py:52
  11.8 270.0 %all-gather.24.cloned.1.call-start = ((), (), s32[]{:S(2)}) async-start(), calls=%async_computation.8 | async-start | bytes 4456448 | tf_op jit(solution)/shard_map/all_gather | solution.py:52
  12.4 278.2 %all-gather.16.cloned.1.call-start = ((), (), s32[]{:S(2)}) async-start(), calls=%async_computation.3 | async-start | bytes 8912896 | tf_op jit(solution)/shard_map/all_gather | solution.py:208
  13.0 332.9 %all-gather.20.cloned.1.call-start = ((), (), s32[]{:S(2)}) async-start(), calls=%async_computation.6 | async-start | bytes 8912896 | tf_op jit(solution)/shard_map/all_gather | solution.py:28
  166.7 18.6 %collective-permute-start = (f32[3,1024]{1,0:T(4,128)S(1)}, f32[3,1024]{1,0:T(4,128)S(1)}, u32[]{:S(2)}, u32[]{:S(2)}) collective-permute-start(f32[3,1024]{1,0:T(4,128)S(1)} %slice.122), channel_id=1, source_target_pairs={{0,8},{8,16},{16,24},{24,32},{32,40},{40,48},{48,56},{56,64},{64,7... | collective-permute-start | bytes 36872 | tf_op jit(solution)/shard_map/ppermute | solution.py:23
  171.4 11.5 %collective-permute-start.2 = (f32[3,128]{1,0:T(4,128)S(1)}, f32[3,128]{1,0:T(4,128)S(1)}, u32[]{:S(2)}, u32[]{:S(2)}) collective-permute-start(f32[3,128]{1,0:T(4,128)S(1)} %slice.132), channel_id=1, source_target_pairs={{0,8},{8,16},{16,24},{24,32},{32,40},{40,48},{48,56},{56,64},{64,7... | collective-permute-start | bytes 4616 | tf_op jit(solution)/shard_map/ppermute | solution.py:23
  275.3 197.5 %reduce-scatter.2.cloned.1.call-start = ((), (), s32[]{:S(2)}) async-start(), calls=%async_computation.4 | async-start | bytes 4718592 | tf_op jit(solution)/shard_map/reduce_scatter | solution.py:223
  379.7 171.8 %all-gather.18.cloned.1.call-start = ((), (), s32[]{:S(2)}) async-start(), calls=%async_computation.5 | async-start | bytes 4718592 | tf_op jit(solution)/shard_map/all_gather | solution.py:228
  556.3 15.9 %collective-permute-start.11 = (bf16[512,128]{1,0:T(8,128)(2,1)S(1)}, bf16[512,128]{1,0:T(8,128)(2,1)S(1)}, u32[]{:S(2)}, u32[]{:S(2)}) collective-permute-start(bf16[512,128]{1,0:T(8,128)(2,1)S(1)} %convolution_convert_fusion.1), channel_id=1, source_target_pairs={{0,64},{8,72},{16,80},{24,88},{32,96},{40,104},{48,112},{56,120},{... | collective-permute-start | bytes 393224 | tf_op jit(solution)/shard_map/ppermute | solution.py:23
  557.7 16.5 %collective-permute-start.12 = (bf16[512,128]{1,0:T(8,128)(2,1)S(1)}, bf16[512,128]{1,0:T(8,128)(2,1)S(1)}, u32[]{:S(2)}, u32[]{:S(2)}) collective-permute-start(bf16[512,128]{1,0:T(8,128)(2,1)S(1)} %convolution_convert_fusion.1), channel_id=1, source_target_pairs={{0,56},{8,64},{16,72},{24,80},{32,88},{40,96},{48,104},{56,112},{6... | collective-permute-start | bytes 393224 | tf_op jit(solution)/shard_map/ppermute | solution.py:23
  560.7 15.5 %collective-permute-start.13 = (bf16[512,128]{1,0:T(8,128)(2,1)S(1)}, bf16[512,128]{1,0:T(8,128)(2,1)S(1)}, u32[]{:S(2)}, u32[]{:S(2)}) collective-permute-start(bf16[512,128]{1,0:T(8,128)(2,1)S(1)} %convolution_convert_fusion.1), channel_id=1, source_target_pairs={{0,48},{8,56},{16,64},{24,72},{32,80},{40,88},{48,96},{56,104},{64... | collective-permute-start | bytes 393224 | tf_op jit(solution)/shard_map/ppermute | solution.py:23
  563.9 14.2 %collective-permute-start.14 = (bf16[512,128]{1,0:T(8,128)(2,1)S(1)}, bf16[512,128]{1,0:T(8,128)(2,1)S(1)}, u32[]{:S(2)}, u32[]{:S(2)}) collective-permute-start(bf16[512,128]{1,0:T(8,128)(2,1)S(1)} %convolution_convert_fusion.1), channel_id=1, source_target_pairs={{0,40},{8,48},{16,56},{24,64},{32,72},{40,80},{48,88},{56,96},{64,... | collective-permute-start | bytes 393224 | tf_op jit(solution)/shard_map/ppermute | solution.py:23
  565.8 13.6 %collective-permute-start.15 = (bf16[512,128]{1,0:T(8,128)(2,1)S(1)}, bf16[512,128]{1,0:T(8,128)(2,1)S(1)}, u32[]{:S(2)}, u32[]{:S(2)}) collective-permute-start(bf16[512,128]{1,0:T(8,128)(2,1)S(1)} %convolution_convert_fusion.1), channel_id=1, source_target_pairs={{0,32},{8,40},{16,48},{24,56},{32,64},{40,72},{48,80},{56,88},{64,... | collective-permute-start | bytes 393224 | tf_op jit(solution)/shard_map/ppermute | solution.py:23
  574.2 11.3 %collective-permute-start.17 = (bf16[512,128]{1,0:T(8,128)(2,1)S(1)}, bf16[512,128]{1,0:T(8,128)(2,1)S(1)}, u32[]{:S(2)}, u32[]{:S(2)}) collective-permute-start(bf16[512,128]{1,0:T(8,128)(2,1)S(1)} %convolution_convert_fusion.1), channel_id=1, source_target_pairs={{0,16},{8,24},{16,32},{24,40},{32,48},{40,56},{48,64},{56,72},{64,... | collective-permute-start | bytes 393224 | tf_op jit(solution)/shard_map/ppermute | solution.py:23
  576.2 11.3 %collective-permute-start.18 = (bf16[512,128]{1,0:T(8,128)(2,1)S(1)}, bf16[512,128]{1,0:T(8,128)(2,1)S(1)}, u32[]{:S(2)}, u32[]{:S(2)}) collective-permute-start(bf16[512,128]{1,0:T(8,128)(2,1)S(1)} %convolution_convert_fusion.1), channel_id=1, source_target_pairs={{0,8},{8,16},{16,24},{24,32},{32,40},{40,48},{48,56},{56,64},{64,7... | collective-permute-start | bytes 393224 | tf_op jit(solution)/shard_map/ppermute | solution.py:23
  578.1 11.3 %collective-permute-start.3 = (bf16[512,128]{1,0:T(8,128)(2,1)S(1)}, bf16[512,128]{1,0:T(8,128)(2,1)S(1)}, u32[]{:S(2)}, u32[]{:S(2)}) collective-permute-start(bf16[512,128]{1,0:T(8,128)(2,1)S(1)} %convolution_convert_fusion.2), channel_id=1, source_target_pairs={{0,64},{8,72},{16,80},{24,88},{32,96},{40,104},{48,112},{56,120},{... | collective-permute-start | bytes 393224 | tf_op jit(solution)/shard_map/ppermute | solution.py:23
  579.5 11.9 %collective-permute-start.4 = (bf16[512,128]{1,0:T(8,128)(2,1)S(1)}, bf16[512,128]{1,0:T(8,128)(2,1)S(1)}, u32[]{:S(2)}, u32[]{:S(2)}) collective-permute-start(bf16[512,128]{1,0:T(8,128)(2,1)S(1)} %convolution_convert_fusion.2), channel_id=1, source_target_pairs={{0,56},{8,64},{16,72},{24,80},{32,88},{40,96},{48,104},{56,112},{6... | collective-permute-start | bytes 393224 | tf_op jit(solution)/shard_map/ppermute | solution.py:23
  582.1 11.8 %collective-permute-start.5 = (bf16[512,128]{1,0:T(8,128)(2,1)S(1)}, bf16[512,128]{1,0:T(8,128)(2,1)S(1)}, u32[]{:S(2)}, u32[]{:S(2)}) collective-permute-start(bf16[512,128]{1,0:T(8,128)(2,1)S(1)} %convolution_convert_fusion.2), channel_id=1, source_target_pairs={{0,48},{8,56},{16,64},{24,72},{32,80},{40,88},{48,96},{56,104},{64... | collective-permute-start | bytes 393224 | tf_op jit(solution)/shard_map/ppermute | solution.py:23
  587.5 12.0 %collective-permute-start.7 = (bf16[512,128]{1,0:T(8,128)(2,1)S(1)}, bf16[512,128]{1,0:T(8,128)(2,1)S(1)}, u32[]{:S(2)}, u32[]{:S(2)}) collective-permute-start(bf16[512,128]{1,0:T(8,128)(2,1)S(1)} %convolution_convert_fusion.2), channel_id=1, source_target_pairs={{0,32},{8,40},{16,48},{24,56},{32,64},{40,72},{48,80},{56,88},{64,... | collective-permute-start | bytes 393224 | tf_op jit(solution)/shard_map/ppermute | solution.py:23
  589.4 12.6 %collective-permute-start.8 = (bf16[512,128]{1,0:T(8,128)(2,1)S(1)}, bf16[512,128]{1,0:T(8,128)(2,1)S(1)}, u32[]{:S(2)}, u32[]{:S(2)}) collective-permute-start(bf16[512,128]{1,0:T(8,128)(2,1)S(1)} %convolution_convert_fusion.2), channel_id=1, source_target_pairs={{0,24},{8,32},{16,40},{24,48},{32,56},{40,64},{48,72},{56,80},{64,... | collective-permute-start | bytes 393224 | tf_op jit(solution)/shard_map/ppermute | solution.py:23
  591.4 13.7 %collective-permute-start.9 = (bf16[512,128]{1,0:T(8,128)(2,1)S(1)}, bf16[512,128]{1,0:T(8,128)(2,1)S(1)}, u32[]{:S(2)}, u32[]{:S(2)}) collective-permute-start(bf16[512,128]{1,0:T(8,128)(2,1)S(1)} %convolution_convert_fusion.2), channel_id=1, source_target_pairs={{0,16},{8,24},{16,32},{24,40},{32,48},{40,56},{48,64},{56,72},{64,... | collective-permute-start | bytes 393224 | tf_op jit(solution)/shard_map/ppermute | solution.py:23
  593.8 13.5 %collective-permute-start.10 = (bf16[512,128]{1,0:T(8,128)(2,1)S(1)}, bf16[512,128]{1,0:T(8,128)(2,1)S(1)}, u32[]{:S(2)}, u32[]{:S(2)}) collective-permute-start(bf16[512,128]{1,0:T(8,128)(2,1)S(1)} %convolution_convert_fusion.2), channel_id=1, source_target_pairs={{0,8},{8,16},{16,24},{24,32},{32,40},{40,48},{48,56},{56,64},{64,7... | collective-permute-start | bytes 393224 | tf_op jit(solution)/shard_map/ppermute | solution.py:23
  (27 other events, 973.7 us)
Sparse Core Ops, SparseCore 0:
  10.2 78.4 all-gather.11
  91.0 66.4 all-gather.13
  159.8 38.3 all-gather.21
  199.7 37.0 all-gather.23
  238.4 52.1 all-gather.15
  292.7 53.1 all-gather.19
  379.8 92.9 reduce-scatter.1
  475.6 75.8 all-gather.17
where the time goes:
time: 668 us; the launch traced here: 659 us
  waiting for transfers between devices  345 us (52%)
  local copies, waits for them, and re-layouts  106 us (16%)
  matrix products  88.3 us (13%)
  other arithmetic  44.1 us (7%)
  starting transfers between devices  40.2 us (6%)
  blocking collectives  19.4 us (3%)
  between operations  15.4 us (2%)
    reduce_scatter x1, waiting for transfers between devices, on_device(): lax.psum_scatter(rounded.astype(jnp.bfloat16), 'mp', scatter_dimension=1,...  93.1 us
    all_gather x1, waiting for transfers between devices, on_device(): stream_rows = lax.all_gather(mixed_low, 'mp', axis=1, tiled=True)  76.2 us
    all_gather x1, waiting for transfers between devices, on_device(): whole_rows = lax.all_gather(hidden_in, 'mp', axis=1, tiled=True)  75.5 us
    all_gather x1, waiting for transfers between devices, side_by_side(): whole = lax.all_gather(both, axis, axis=dim, tiled=True)  61.8 us
    dynamic_update_slice x4, local copies, waits for them, and re-layouts, run_ssd(): lax.scan(ssd_block, carry_state, (blocked(inputs), blocked(step_sizes), b...  55.5 us
    ppermute x19, starting transfers between devices, from_behind(): return lax.ppermute(block, axis, route)  39.9 us
    dot_general x5, matrix products, add_rows(): return jnp.dot(normed, piece, preferred_element_type=jnp.float32)  28 us
    dot_general x4, matrix products, one_head(): lax.dot_general(query_h, key_h, (((1,), (1,)), ((), ())), preferred_eleme...  20.1 us
  transfers between devices with their start and end apart: 27, of which 14 were waited for; matrix products, arithmetic and copies ran while one was open for 23% of the time, Pallas kernels for 0%

commit v1 on v0

v1 whole, which is shorter than its diff:
```python
import functools
import jax
import jax.numpy as jnp
from jax import lax
from jax.experimental import pallas as pl
from jax.experimental.pallas import tpu as pltpu
from jax.sharding import PartitionSpec as P

MESH = pl.DeviceIdType.MESH
P_SIZE = 64
N = 128
HD = 128
WINDOW = 4096
QB = 128
VM = pl.BlockSpec(memory_space=pltpu.VMEM)


def rows(start, size):
    return pl.ds(start, size)


def mp_places():
    me = lax.axis_index("mp")
    high, low = me // 4, me % 4
    return high, low


def mp_greet(others):
    barrier = pltpu.get_barrier_semaphore()
    for other in others:
        pl.semaphore_signal(barrier, inc=1, device_id={"mp": other}, device_id_type=MESH)
    pl.semaphore_wait(barrier, len(others))


def gather_kernel(chunks, x_ref, gain_ref, normed_ref, out_ref, own_sem, ysend, yrecv, xsend, xrecv, fsend, frecv):
    high, low = mp_places()
    right, left = (low + 1) % 4, (low + 3) % 4
    me, partner = high * 4 + low, (1 - high) * 4 + low
    mp_greet((high * 4 + right, high * 4 + left, partner))
    count = x_ref.shape[0] // chunks
    half = x_ref.shape[0] // 2

    def send(src, block, piece, target, ssem, rsem):
        copy = pltpu.make_async_remote_copy(
            src_ref=src, dst_ref=out_ref.at[block, piece], send_sem=ssem, recv_sem=rsem,
            device_id={"mp": target}, device_id_type=MESH)
        copy.start()
        return copy

    sides = ((right, left), (left, right))
    started = []
    ycopies, own = [], []
    for c in range(chunks):
        piece = rows(c * count, count)
        ycopies.append(send(x_ref.at[piece], me, piece, partner, ysend.at[c], yrecv.at[c]))
        own.append([
            send(x_ref.at[piece], me, piece, high * 4 + to, xsend.at[0, d, c], xrecv.at[0, d, c])
            for d, (to, _) in enumerate(sides)])
    local = pltpu.make_async_copy(x_ref, out_ref.at[me], own_sem)
    local.start()
    other = []
    for c in range(chunks):
        piece = rows(c * count, count)
        ycopies[c].wait_recv()
        other.append([
            send(out_ref.at[partner, piece], partner, piece, high * 4 + to, xsend.at[1, d, c], xrecv.at[1, d, c])
            for d, (to, _) in enumerate(sides)])
    forwards = []
    for k, copies in enumerate((own, other)):
        for c in range(chunks):
            for d, (to, origin) in enumerate(sides):
                copies[c][d].wait_recv()
                if (c * count < half) == (d == 0):
                    block = (high if k == 0 else 1 - high) * 4 + origin
                    piece = rows(c * count, count)
                    forwards.append(send(out_ref.at[block, piece], block, piece, high * 4 + to,
                                         fsend.at[k, c], frecv.at[k, c]))
    for copy in forwards:
        copy.wait()
    local.wait()
    for c in range(chunks):
        ycopies[c].wait_send()
        for copies in (own, other):
            for d in range(2):
                copies[c][d].wait_send()
    wide = x_ref.shape[1]

    def norm(c, _):
        piece = rows(pl.multiple_of(c * 32, 32), 32)
        square = jnp.zeros((32, wide), jnp.float32)
        for b in range(8):
            value = out_ref[b, piece, :].astype(jnp.float32)
            square = square + value * value
        scale = lax.rsqrt(jnp.sum(square, axis=1, keepdims=True) / (8 * wide) + 1e-05)
        for b in range(8):
            lanes = slice(b * wide, (b + 1) * wide)
            normed_ref[piece, lanes] = (out_ref[b, piece, :].astype(jnp.float32) * scale
                                        * gain_ref[:, lanes]).astype(normed_ref.dtype)
        return 0

    lax.fori_loop(0, x_ref.shape[0] // 32, norm, 0)


def mp_gather_norm(x, gain, cid, chunks=4):
    n, w = x.shape
    D = pltpu.SemaphoreType.DMA
    return pl.pallas_call(
        functools.partial(gather_kernel, chunks),
        out_shape=jax.ShapeDtypeStruct((n, 8 * w), x.dtype),
        in_specs=[VM, VM], out_specs=VM,
        scratch_shapes=[pltpu.VMEM((8, n, w), x.dtype), D, D((chunks,)), D((chunks,)), D((2, 2, chunks)), D((2, 2, chunks)), D((2, chunks)), D((2, chunks))],
        compiler_params=pltpu.CompilerParams(collective_id=cid, has_side_effects=True, vmem_limit_bytes=24 << 20),
    )(x, gain)


def reduce_kernel(p_ref, out_ref, tmp, d1, d2, ysrc, ydst, s1, r1, s2, r2, sy, ry, sraw, rraw):
    high, low = mp_places()
    right, left = (low + 1) % 4, (low + 3) % 4
    far = (low + 2) % 4
    partner = (1 - high) * 4 + low
    mp_greet((high * 4 + right, high * 4 + left, partner))
    n = p_ref.shape[1]
    half = n // 2
    order = (1 - high, high)
    sides = ((right, left), (left, right))

    def send(src, dst, target, ssem, rsem):
        copy = pltpu.make_async_remote_copy(src_ref=src, dst_ref=dst, send_sem=ssem, recv_sem=rsem,
                                            device_id={"mp": target}, device_id_type=MESH)
        copy.start()
        return copy

    first = [[send(p_ref.at[order[k] * 4 + far, rows(d * half, half)], d1.at[k, d], high * 4 + sides[d][0],
                   s1.at[k, d], r1.at[k, d]) for d in range(2)] for k in range(2)]
    raw = [[send(p_ref.at[order[k] * 4 + sides[d][0], rows((1 - d) * half, half)],
                 d2.at[k, d, rows((1 - d) * half, half)], high * 4 + sides[d][0],
                 sraw.at[k, d], rraw.at[k, d]) for d in range(2)] for k in range(2)]
    second = []
    for k in range(2):
        for d in range(2):
            first[k][d].wait_recv()
            tmp[k, d] = (d1[k, d].astype(jnp.float32)
                         + p_ref[order[k] * 4 + sides[d][0], d * half:(d + 1) * half].astype(jnp.float32)).astype(tmp.dtype)
            second.append(send(tmp.at[k, d], d2.at[k, d, rows(d * half, half)], high * 4 + sides[d][0],
                               s2.at[k, d], r2.at[k, d]))
    totals = None
    for k in range(2):
        for d in range(2):
            raw[k][d].wait_recv()
            second[k * 2 + d].wait_recv()
        total = (p_ref[order[k] * 4 + low].astype(jnp.float32) + d2[k, 0].astype(jnp.float32)
                 + d2[k, 1].astype(jnp.float32))
        if k == 0:
            ysrc[...] = total.astype(ysrc.dtype)
            ycopy = send(ysrc, ydst, partner, sy, ry)
        else:
            ycopy.wait_recv()
            out_ref[...] = total + ydst[...].astype(jnp.float32)
    ycopy.wait_send()
    for k in range(2):
        for d in range(2):
            first[k][d].wait_send()
            raw[k][d].wait_send()
            second[k * 2 + d].wait_send()


def mp_reduce(p, cid):
    _, n, w = p.shape
    D = pltpu.SemaphoreType.DMA
    half = n // 2
    return pl.pallas_call(
        reduce_kernel,
        out_shape=jax.ShapeDtypeStruct((n, w), jnp.float32),
        in_specs=[VM], out_specs=VM,
        scratch_shapes=[pltpu.VMEM((2, 2, half, w), p.dtype), pltpu.VMEM((2, 2, half, w), p.dtype),
                        pltpu.VMEM((2, 2, n, w), p.dtype), pltpu.VMEM((n, w), p.dtype), pltpu.VMEM((n, w), p.dtype),
                        D((2, 2)), D((2, 2)), D((2, 2)), D((2, 2)), D, D, D((2, 2)), D((2, 2))],
        compiler_params=pltpu.CompilerParams(collective_id=cid, has_side_effects=True, vmem_limit_bytes=32 << 20),
    )(p)


def ssd_kernel(xp_ref, bcd_ref, rimx_ref, rimbc_ref, cx_ref, cbc_ref, bias_ref, rate_ref, skip_ref,
               y_ref, cc_ref, cum_ref, send_ref, padx, padbc, state):
    n = xp_ref.shape[0]
    count = n // QB
    padx[pl.ds(0, 8), :] = rimx_ref[...]
    padbc[pl.ds(0, 8), :] = rimbc_ref[...]
    padx[pl.ds(8, n), :] = xp_ref[...]
    padbc[pl.ds(8, n), :] = bcd_ref[:, 0:2 * N]
    state[...] = jnp.zeros_like(state)
    row = lax.broadcasted_iota(jnp.int32, (QB, QB), 0)
    col = lax.broadcasted_iota(jnp.int32, (QB, QB), 1)
    causal = row >= col
    tri = jnp.where(causal, 1.0, 0.0).astype(jnp.float32)
    low = col < P_SIZE
    bf = jnp.bfloat16

    def silu(v):
        return v / (1.0 + jnp.exp(-v))

    def conv(pad, taps, start, lanes):
        whole = pad[pl.ds(start, QB + 8), lanes]
        total = taps[0:1, lanes] * whole[5:5 + QB]
        for j in range(1, 4):
            total = total + taps[j:j + 1, lanes] * whole[5 + j:5 + j + QB]
        return silu(total)

    def one(c, before):
        start = pl.multiple_of(c * QB, QB)
        here = pl.ds(start, QB)
        bv = conv(padbc, cbc_ref, start, slice(0, N))
        cv = conv(padbc, cbc_ref, start, slice(N, 2 * N)).astype(bf)
        cc_ref[here, :] = cv
        raw = bcd_ref[here, 2 * N:3 * N] + bias_ref[...]
        step = jnp.maximum(raw, 0.0) + jnp.log1p(jnp.exp(-jnp.abs(raw)))
        decay = -rate_ref[...] * step
        cum = jnp.dot(tri, decay, precision=lax.Precision.HIGHEST, preferred_element_type=jnp.float32)
        cum_ref[here, :] = cum + before
        cum_t, step_t = cum.T, step.T
        last = cum[QB - 1:QB, :]
        bt = bv.T.astype(bf)
        affinity = jnp.dot(cv, bt, preferred_element_type=jnp.float32)
        for p in range(xp_ref.shape[1] // 128):
            lanes = slice(p * 128, (p + 1) * 128)
            xv = conv(padx, cx_ref, start, lanes)
            mixes, grown, tails, ends = [], [], [], []
            for h in (2 * p, 2 * p + 1):
                ct = jnp.broadcast_to(cum[:, h:h + 1], (QB, QB))
                st = jnp.broadcast_to(step[:, h:h + 1], (QB, QB))
                end = jnp.broadcast_to(last[:, h:h + 1], (1, QB))
                spread = jnp.where(causal, ct - cum_t[h:h + 1, :], -jnp.inf)
                mixes.append((affinity * jnp.exp(spread) * step_t[h:h + 1, :]).astype(bf))
                grown.append(ct)
                tails.append(jnp.exp(end - ct) * st)
                ends.append(end)
            lowhalf = low[0:1]
            mixed = jnp.concatenate(mixes, axis=1)
            xs = jnp.concatenate([jnp.where(low, xv, 0.0).astype(bf), jnp.where(low, 0.0, xv).astype(bf)], axis=0)
            out = jnp.dot(mixed, xs, preferred_element_type=jnp.float32)
            old = state[:, lanes]
            carried = jnp.dot(cv, old.astype(bf), preferred_element_type=jnp.float32)
            out = out + jnp.exp(jnp.where(low, grown[0], grown[1])) * carried
            y_ref[here, lanes] = out + skip_ref[0:1, lanes] * xv
            weighted = (xv * jnp.where(low, tails[0], tails[1])).astype(bf)
            fresh = jnp.dot(bt, weighted, preferred_element_type=jnp.float32)
            state[:, lanes] = jnp.exp(jnp.where(lowhalf, ends[0], ends[1])) * old + fresh
        return before + last

    total = lax.fori_loop(0, count, one, jnp.zeros((1, 128), jnp.float32))
    send_ref[0:N, :] = state[...].astype(bf)
    for p in range(xp_ref.shape[1] // 128):
        lanes = slice(p * 128, (p + 1) * 128)
        ends = [jnp.broadcast_to(total[:, h:h + 1], (16, 128)) for h in (2 * p, 2 * p + 1)]
        decay = jnp.exp(jnp.where(low[0:16], ends[0], ends[1]))
        big = decay.astype(bf)
        rest = decay - big.astype(jnp.float32)
        middle = rest.astype(bf)
        small = (rest - middle.astype(jnp.float32)).astype(bf)
        which = row[0:16]
        send_ref[N:N + 16, lanes] = jnp.where(which == 0, big.astype(jnp.float32), jnp.where(
            which == 1, middle.astype(jnp.float32), small.astype(jnp.float32))).astype(bf)


def run_ssd(xp, bcd, rimx, rimbc, conv_x, conv_bc, bias, rate, skip):
    n, width = xp.shape
    f32, bf = jnp.float32, jnp.bfloat16
    return pl.pallas_call(
        ssd_kernel,
        out_shape=(jax.ShapeDtypeStruct((n, width), f32), jax.ShapeDtypeStruct((n, N), bf),
                   jax.ShapeDtypeStruct((n, 128), f32), jax.ShapeDtypeStruct((N + 16, width), bf)),
        in_specs=[VM] * 9, out_specs=(VM,) * 4,
        scratch_shapes=[pltpu.VMEM((n + 8, width), f32), pltpu.VMEM((n + 8, 2 * N), f32), pltpu.VMEM((N, width), f32)],
        compiler_params=pltpu.CompilerParams(vmem_limit_bytes=32 << 20),
        cost_estimate=pl.CostEstimate(flops=4_000_000_000, bytes_accessed=8 << 20, transcendentals=0),
    )(xp, bcd, rimx, rimbc, conv_x, conv_bc, bias, rate, skip)


def gate_kernel(y_ref, cc_ref, cum_ref, states_ref, gate_ref, gain_ref, out_ref, incoming, full):
    place = lax.axis_index("seq")
    n, width = y_ref.shape
    bf, f32 = jnp.bfloat16, jnp.float32
    incoming[...] = jnp.zeros_like(incoming)

    def add(k, _):
        tail = states_ref[k, N:N + 16, :].astype(f32)
        decay = tail[0:1] + (tail[1:2] + tail[2:3])
        incoming[...] = decay * incoming[...] + states_ref[k, 0:N, :].astype(f32)
        return 0

    lax.fori_loop(0, place, add, 0)
    low = lax.broadcasted_iota(jnp.int32, (QB, 128), 1) < P_SIZE

    def one(c, _):
        here = pl.ds(pl.multiple_of(c * QB, QB), QB)
        cv = cc_ref[here, :]
        cum = cum_ref[here, :]
        square = jnp.zeros((QB, 128), f32)
        for p in range(width // 128):
            lanes = slice(p * 128, (p + 1) * 128)
            ct = jnp.where(low, jnp.broadcast_to(cum[:, 2 * p:2 * p + 1], (QB, 128)),
                           jnp.broadcast_to(cum[:, 2 * p + 1:2 * p + 2], (QB, 128)))
            carried = jnp.dot(cv, incoming[:, lanes].astype(bf), preferred_element_type=f32)
            g = gate_ref[here, lanes]
            value = (y_ref[here, lanes] + jnp.exp(ct) * carried) * (g / (1.0 + jnp.exp(-g)))
            full[:, lanes] = value
            square = square + value * value
        scale = lax.rsqrt(jnp.sum(square, axis=1, keepdims=True) / width + 1e-05)
        out_ref[here, :] = (full[...] * scale * gain_ref[...]).astype(bf)
        return 0

    lax.fori_loop(0, n // QB, one, 0)


def run_gate(y, cc, cum, states, gate, gain):
    n, width = y.shape
    return pl.pallas_call(
        gate_kernel,
        out_shape=jax.ShapeDtypeStruct((n, width), jnp.bfloat16),
        in_specs=[VM] * 6, out_specs=VM,
        scratch_shapes=[pltpu.VMEM((N, width), jnp.float32), pltpu.VMEM((QB, width), jnp.float32)],
        compiler_params=pltpu.CompilerParams(vmem_limit_bytes=32 << 20),
        cost_estimate=pl.CostEstimate(flops=2_000_000_000, bytes_accessed=8 << 20, transcendentals=0),
    )(y, cc, cum, states, gate, gain)


def out_kernel(y_ref, w_ref, out_ref):
    out_ref[0] = jnp.dot(y_ref[...], w_ref[0], preferred_element_type=jnp.float32).astype(out_ref.dtype)


def run_out(y, w):
    n, width = y.shape
    cols = w.shape[2]
    return pl.pallas_call(
        out_kernel,
        out_shape=jax.ShapeDtypeStruct((8, n, 2 * cols), jnp.bfloat16),
        grid=(w.shape[0],),
        in_specs=[pl.BlockSpec((n, width), lambda j: (0, 0)), pl.BlockSpec((1, width, cols), lambda j: (j, 0, 0))],
        out_specs=pl.BlockSpec((1, n, cols), lambda j: (j // 2, 0, j % 2)),
        compiler_params=pltpu.CompilerParams(vmem_limit_bytes=16 << 20),
        cost_estimate=pl.CostEstimate(flops=2 * n * width * 4096, bytes_accessed=16 << 20, transcendentals=0),
    )(y, w)


def attention_kernel(q_ref, kv_ref, out_ref, peak, total):
    place = lax.axis_index("seq")
    j = pl.program_id(0)
    reach = pl.num_programs(0) - 1
    n = q_ref.shape[0]
    heads = q_ref.shape[1] // HD
    scale = HD ** -0.5 * 1.4426950408889634

    @pl.when(j == 0)
    def _():
        peak[...] = jnp.full_like(peak, -1e30)
        total[...] = jnp.zeros_like(total)

    def work(edge):
        keys = kv_ref[0, :, 0:HD]
        both = jnp.concatenate([kv_ref[0, :, HD:2 * HD], jnp.ones((n, HD), jnp.bfloat16)], axis=1)
        for h in range(heads):
            scores = lax.dot_general(q_ref[:, h * HD:(h + 1) * HD], keys, (((1,), (1,)), ((), ())),
                                     preferred_element_type=jnp.float32) * scale
            if edge is not None:
                t = lax.broadcasted_iota(jnp.int32, (n, n), 0)
                s = lax.broadcasted_iota(jnp.int32, (n, n), 1)
                scores = jnp.where(s > t if edge == 0 else s <= t, scores, -1e30)
            old = peak[h]
            new = jnp.maximum(old, jnp.max(scores, axis=1, keepdims=True))
            weights = jnp.exp2(scores - new[:, 0:1])
            if edge == 0:
                weights = jnp.where(s > t, weights, 0.0)
            shrink = jnp.exp2(old - new)
            peak[h] = new
            total[h] = jnp.concatenate([shrink, shrink], axis=1) * total[h] + jnp.dot(
                weights.astype(jnp.bfloat16), both, preferred_element_type=jnp.float32)

    @pl.when((j == 0) & (place >= reach))
    def _():
        work(0)

    @pl.when((j > 0) & (j < reach) & (place + j >= reach))
    def _():
        work(None)

    @pl.when(j == reach)
    def _():
        work(1)
        for h in range(heads):
            out_ref[:, h * HD:(h + 1) * HD] = total[h, :, 0:HD] / total[h, :, HD:2 * HD]


def run_attention(q, kv):
    n, width = q.shape
    reach = WINDOW // n
    heads = width // HD
    return pl.pallas_call(
        attention_kernel,
        out_shape=jax.ShapeDtypeStruct((n, width), jnp.float32),
        grid=(reach + 1,),
        in_specs=[pl.BlockSpec((n, width), lambda j: (0, 0)),
                  pl.BlockSpec((1, n, 2 * HD), lambda j: (jnp.maximum(lax.axis_index("seq") + j - reach, 0), 0, 0))],
        out_specs=pl.BlockSpec((n, width), lambda j: (0, 0)),
        scratch_shapes=[pltpu.VMEM((heads, n, HD), jnp.float32), pltpu.VMEM((heads, n, 2 * HD), jnp.float32)],
        compiler_params=pltpu.CompilerParams(vmem_limit_bytes=32 << 20),
        cost_estimate=pl.CostEstimate(flops=8 * n * width * WINDOW, bytes_accessed=8 << 20, transcendentals=0),
    )(q, kv)


def rms_norm(values, gain):
    return values * lax.rsqrt(jnp.mean(values * values, axis=-1, keepdims=True) + 1e-05) * gain


def padded(vector):
    return jnp.pad(vector, (0, 128 - vector.shape[0]))[None, :]


def on_device(hidden_in, norm_gain, w_z, w_x, w_b, w_c, w_dt, conv_x, conv_b, conv_c, dt_bias, a_rate,
              skip_gain, group_gain, w_out, attn_gain, w_q, w_k, w_v):
    f32, bf = jnp.float32, jnp.bfloat16
    n = hidden_in.shape[0]
    w_bcd = jnp.concatenate([w_b, w_c, jnp.pad(w_dt, ((0, 0), (0, 128 - w_dt.shape[1])))], axis=1)
    w_x_all = lax.all_gather(w_x, "seq", axis=0, tiled=True)
    w_bcd_all = lax.all_gather(w_bcd, "seq", axis=0, tiled=True)
    w_z_all = lax.all_gather(w_z, "seq", axis=0, tiled=True)
    w_out_all = lax.all_gather(w_out, "seq")
    normed = mp_gather_norm(hidden_in, norm_gain[None, :], 0)
    bcd = jnp.dot(normed, w_bcd_all, preferred_element_type=f32)
    xp = jnp.dot(normed, w_x_all, preferred_element_type=f32)
    route = [(i, i + 1) for i in range(lax.axis_size("seq") - 1)]
    rims = lax.ppermute(jnp.concatenate([xp[n - 8:], bcd[n - 8:, 0:2 * N]], axis=1), "seq", route)
    width = xp.shape[1]
    y, cc, cum, send = run_ssd(
        xp, bcd, rims[:, 0:width], rims[:, width:], conv_x, jnp.concatenate([conv_b, conv_c], axis=1),
        padded(dt_bias), padded(a_rate), jnp.repeat(skip_gain, P_SIZE)[None, :])
    states = lax.all_gather(send, "seq")
    gate = jnp.dot(normed, w_z_all, preferred_element_type=f32)
    y_normed = run_gate(y, cc, cum, states, gate, group_gain[None, :])
    parts = run_out(y_normed, w_out_all)
    mixed = hidden_in.astype(f32) + mp_reduce(parts, 1)
    normed_two = mp_gather_norm(mixed.astype(bf), attn_gain[None, :], 2)
    keys = jnp.dot(normed_two, w_k, preferred_element_type=f32).astype(bf)
    values = jnp.dot(normed_two, w_v, preferred_element_type=f32).astype(bf)
    kv = lax.all_gather(jnp.concatenate([keys, values], axis=1), "seq")
    queries = jnp.dot(normed_two, w_q, preferred_element_type=f32).astype(bf)
    return (mixed, run_attention(queries, kv))


def solution(mesh):
    tile, cols = P("seq", "mp"), P(None, "mp")
    placed = (tile, P(), tile, tile, tile, tile, tile, cols, cols, cols, P("mp"), P("mp"), P("mp"), P("mp"),
              P("mp", "seq"), P(), cols, cols, cols)
    return jax.shard_map(on_device, mesh=mesh, in_specs=placed, out_specs=(tile, tile), check_vma=False)
```

time: 668 us -> 438 us (0.66); the launches traced: 659 us -> 437 us
  Pallas kernels: 0 us -> 168 us
  waiting for transfers between devices: 345 us -> 186 us
  local copies, waits for them, and re-layouts: 106 us -> 30.2 us
  matrix products: 88.3 us -> 32.9 us
  other arithmetic: 44.1 us -> 3.28 us
  starting transfers between devices: 40.2 us -> 2.36 us
  blocking collectives: 19.4 us -> 0 us
    pallas_call x0 -> x7, Pallas kernels: none -> 168 us  [the longest x2 80.9 us: mp_gather_norm(): pl.pallas_call(functools.partial(gather_kernel, chunks), out_shape=jax.Sh...]
    reduce_scatter x1 -> x0, waiting for transfers between devices: 93.1 us -> none  [on_device(): lax.psum_scatter(rounded.astype(jnp.bfloat16), 'mp', scatter_dimension=1,...]
    all_gather x7 -> x6, waiting for transfers between devices: 234 us -> 178 us  [the longest x1 46.4 us: on_device(): w_out_all = lax.all_gather(w_out, 'seq')]
    dynamic_update_slice x4 -> x0, local copies, waits for them, and re-layouts: 55.5 us -> none  [run_ssd(): lax.scan(ssd_block, carry_state, (blocked(inputs), blocked(step_sizes), b...]
    dot_general x33 -> x6, matrix products: 83.3 us -> 32.9 us  [the longest x1 10.5 us: on_device(): gate = jnp.dot(normed, w_z_all, preferred_element_type=f32)]
    ppermute x19 -> x1, starting transfers between devices: 39.9 us -> 2.12 us  [on_device(): lax.ppermute(jnp.concatenate([xp[n - 8:], bcd[n - 8:, 0:2 * N]], axis=1),...]
    all_gather x1 -> x0, blocking collectives: 19.4 us -> none  [carried_in(): gathered = jax.tree.map(lambda a: lax.all_gather(a, axis), part)]
    unnamed x68 -> x52, local copies, waits for them, and re-layouts: 7.55 us -> 23.6 us
  transfers between devices with their start and end apart: 27 -> 7, of which waited for: 14 -> 6; matrix products, arithmetic and copies ran while one was open for 23% -> 7% of each run, Pallas kernels for 0% -> 12%
where the time goes in v1:
time: 438 us; the launch traced here: 437 us
  waiting for transfers between devices  186 us (42%)
  Pallas kernels  168 us (38%)
  matrix products  32.9 us (8%)
  local copies, waits for them, and re-layouts  30.2 us (7%)
  between operations  14.4 us (3%)
    pallas_call x2, Pallas kernels, mp_gather_norm(): pl.pallas_call(functools.partial(gather_kernel, chunks), out_shape=jax.Sh...  80.9 us
    pallas_call x1, Pallas kernels, mp_reduce(): pl.pallas_call(reduce_kernel, out_shape=jax.ShapeDtypeStruct((n, w), jnp....  47.2 us
    all_gather x1, waiting for transfers between devices, on_device(): w_out_all = lax.all_gather(w_out, 'seq')  46.4 us
    all_gather x1, waiting for transfers between devices, on_device(): w_x_all = lax.all_gather(w_x, 'seq', axis=0, tiled=True)  45.8 us
    all_gather x1, waiting for transfers between devices, on_device(): kv = lax.all_gather(jnp.concatenate([keys, values], axis=1), 'seq')  31 us
    all_gather x1, waiting for transfers between devices, on_device(): states = lax.all_gather(send, 'seq')  30.5 us
    all_gather x1, waiting for transfers between devices, on_device(): w_z_all = lax.all_gather(w_z, 'seq', axis=0, tiled=True)  24.3 us
    unnamed x52, local copies, waits for them, and re-layouts  23.6 us
  transfers between devices with their start and end apart: 7, of which 6 were waited for; matrix products, arithmetic and copies ran while one was open for 7% of the time, Pallas kernels for 12%

profile of v1, /device:TPU:8, one launch (start us, length us, event | category | flops | bytes accessed | tf_op | source)
XLA Modules:
  0.0 437.3 jit_solution(16090065946346578758)
XLA Ops:
  13.9 42.3 %shard_map.194 = bf16[512,4096]{1,0:T(8,128)(2,1)S(1)} custom-call(bf16[512,512]{1,0:T(8,128)(2,1)S(1)} %copy-done.5, f32[1,4096]{1,0:T(1,128)S(1)} %bitcast.24), custom_call_target="tpu_custom_call" | custom-call | tf_op jit(solution)/shard_map/pallas_call | solution.py:107
  56.2 2.0 copy-done.3
  58.3 5.5 %fusion.4.bcd_ref = f32[512,384]{1,0:T(8,128)S(1)} fusion(bf16[512,4096]{1,0:T(8,128)(2,1)} %copy-done.3, bf16[4096,384]{0,1:T(8,128)(2,1)} %all-gather.12.cloned.1.call-done), kind=kOutput, calls=%fused_computation.14 | convolution fusion | flops 1610612736 | bytes 8126464 | tf_op jit(solution)/shard_map/dot_general | solution.py:427
  64.7 45.8 %all-gather.10.cloned.1.call-done = bf16[4096,1024]{1,0:T(8,128)(2,1)} async-done(((bf16[256,1024]{1,0:T(8,128)(2,1)}), bf16[4096,1024]{1,0:T(8,128)(2,1)}) %all-gather.10.cloned.1.call-update) | async-done | bytes 8388624 | tf_op jit(solution)/shard_map/all_gather | solution.py:422
  110.5 8.1 %fusion.3.xp_ref = f32[512,1024]{1,0:T(8,128)S(1)} fusion(bf16[512,4096]{1,0:T(8,128)(2,1)} %copy-done.3, bf16[4096,1024]{1,0:T(8,128)(2,1)} %all-gather.10.cloned.1.call-done), kind=kOutput, calls=%fused_computation.13 | convolution fusion | flops 4294967296 | bytes 14680064 | tf_op jit(solution)/shard_map/dot_general | solution.py:428
  119.9 2.1 collective-permute-start
  122.3 5.9 %collective-permute-done = f32[8,1280]{1,0:T(8,128)S(1)} collective-permute-done((f32[8,1280]{1,0:T(8,128)S(1)}, f32[8,1280]{1,0:T(8,128)S(1)}, u32[]{:S(2)}, u32[]{:S(2)}) %collective-permute-start) | collective-permute-done | bytes 40992 | tf_op jit(solution)/shard_map/ppermute | solution.py:430
  128.2 1.6 copy-done.14
  131.7 8.6 %shard_map.195 = (f32[512,1024]{1,0:T(8,128)S(1)}, bf16[512,128]{1,0:T(8,128)(2,1)S(1)}, f32[512,128]{1,0:T(8,128)S(1)}, bf16[144,1024]{1,0:T(8,128)(2,1)}) custom-call(f32[512,1024]{1,0:T(8,128)S(1)} %copy-done.14, f32[512,384]{1,0:T(8,128)S(1)} %copy-done.16, f32[8,1024]{1,0:T(8,128)S(1)} %slice.18.rimx_ref, f32[8,256]{1,0:T(8,128)S(1)} %slice.19.rimbc_ref, ...), custom_call_target="tpu_custom_call" | custom-call | flops 4000000000 | bytes 8388608 | tf_op jit(solution)/shard_map/pallas_call | solution.py:267
  140.9 24.3 %all-gather.14.cloned.1.call-done = bf16[4096,1024]{1,0:T(8,128)(2,1)} async-done(((bf16[256,1024]{1,0:T(8,128)(2,1)}), bf16[4096,1024]{1,0:T(8,128)(2,1)}) %all-gather.14.cloned.1.call-update) | async-done | bytes 8388624 | tf_op jit(solution)/shard_map/all_gather | solution.py:424
  165.3 10.5 %fusion.5.gate_ref = f32[512,1024]{1,0:T(8,128)} fusion(bf16[512,4096]{1,0:T(8,128)(2,1)} %copy-done.3, bf16[4096,1024]{1,0:T(8,128)(2,1)} %all-gather.14.cloned.1.call-done), kind=kOutput, calls=%fused_computation.15 | convolution fusion | flops 4294967296 | bytes 14680064 | tf_op jit(solution)/shard_map/dot_general | solution.py:436
  175.7 30.5 %all-gather.16.cloned.1.call-done = bf16[2304,1024]{1,0:T(8,128)(2,1)} async-done(((bf16[144,1024]{1,0:T(8,128)(2,1)}), bf16[2304,1024]{1,0:T(8,128)(2,1)}) %all-gather.16.cloned.1.call-update) | async-done | bytes 4718608 | tf_op jit(solution)/shard_map/all_gather | solution.py:435
  206.2 2.3 copy-done.2
  210.2 2.8 shard_map.196.y_ref
  213.9 46.4 %all-gather.18.cloned.1.call-done = bf16[16384,256]{1,0:T(8,128)(2,1)} async-done(((bf16[1024,256]{1,0:T(8,128)(2,1)}), bf16[16384,256]{1,0:T(8,128)(2,1)}) %all-gather.18.cloned.1.call-update) | async-done | bytes 8388624 | tf_op jit(solution)/shard_map/all_gather | solution.py:425
  261.6 3.4 copy-done.17
  264.9 7.7 %shard_map.197.p_ref = bf16[8,512,512]{2,1,0:T(8,128)(2,1)S(1)} custom-call(bf16[512,1024]{1,0:T(8,128)(2,1)S(1)} %copy-done.9, bf16[16,1024,256]{2,1,0:T(8,128)(2,1)S(1)} %bitcast.27), custom_call_target="tpu_custom_call" | custom-call | flops 4294967296 | bytes 16777216 | tf_op jit(solution)/shard_map/pallas_call | solution.py:333
  272.7 47.2 %shard_map.198 = f32[512,512]{1,0:T(8,128)S(1)} custom-call(bf16[8,512,512]{2,1,0:T(8,128)(2,1)S(1)} %shard_map.197.p_ref), custom_call_target="tpu_custom_call" | custom-call | tf_op jit(solution)/shard_map/pallas_call | solution.py:171
  321.1 38.7 %shard_map.199 = bf16[512,4096]{1,0:T(8,128)(2,1)S(1)} custom-call(bf16[512,512]{1,0:T(8,128)(2,1)S(1)} %get-tuple-element.10.x_ref, f32[1,4096]{1,0:T(1,128)S(1)} %bitcast.25), custom_call_target="tpu_custom_call" | custom-call | tf_op jit(solution)/shard_map/pallas_call | solution.py:107
  364.1 5.8 %convolution_convert_fusion.q_ref = bf16[512,512]{1,0:T(8,128)(2,1)S(1)} fusion(bf16[512,4096]{1,0:T(8,128)(2,1)} %copy-done.1, bf16[4096,512]{1,0:T(8,128)(2,1)} %param.35), kind=kOutput, calls=%fused_computation | convolution fusion | flops 2147745792 | bytes 8912896 | tf_op jit(solution)/shard_map/dot_general | solution.py:444
  369.8 31.0 %all-gather.20.cloned.1.call-done = bf16[8192,256]{0,1:T(8,128)(2,1)} async-done(((bf16[512,256]{0,1:T(8,128)(2,1)}), bf16[8192,256]{0,1:T(8,128)(2,1)}) %all-gather.20.cloned.1.call-update) | async-done | bytes 4194320 | tf_op jit(solution)/shard_map/all_gather | solution.py:443
  400.9 6.4 %copy.23 = bf16[8192,256]{1,0:T(8,128)(2,1)} copy(bf16[8192,256]{0,1:T(8,128)(2,1)} %all-gather.20.cloned.1.call-done) | data formatting | bytes 8388608 | tf_op jit(solution)/shard_map/all_gather | solution.py:443
  407.3 2.2 copy-done.4
  409.4 21.0 %shard_map.200 = f32[512,512]{1,0:T(8,128)} custom-call(bf16[512,512]{1,0:T(8,128)(2,1)S(1)} %convolution_convert_fusion.q_ref, bf16[16,512,256]{2,1,0:T(8,128)(2,1)S(1)} %bitcast.23), custom_call_target="tpu_custom_call" | custom-call | flops 8589934592 | bytes 8388608 | tf_op jit(solution)/shard_map/pallas_call | solution.py:396
  (74 shorter events, 20.8 us)
Async XLA Ops:
  7.2 352.6 %copy-start = (bf16[4096,128]{1,0:T(8,128)(2,1)S(1)}, bf16[4096,128]{1,0:T(8,128)(2,1)}, u32[]{:S(2)}) copy-start(bf16[4096,128]{1,0:T(8,128)(2,1)} %param.37) | copy-start | bytes 3145732
  7.2 51.0 %copy-start.21 = (f32[4,128]{1,0:T(4,128)S(1)}, f32[4,128]{1,0:T(4,128)}, u32[]{:S(2)}) copy-start(f32[4,128]{1,0:T(4,128)} %param.27) | copy-start | bytes 6148
  7.2 51.0 %copy-start.20 = (f32[4,128]{1,0:T(4,128)S(1)}, f32[4,128]{1,0:T(4,128)}, u32[]{:S(2)}) copy-start(f32[4,128]{1,0:T(4,128)} %param.28) | copy-start | bytes 6148
  7.2 51.1 %all-gather.12.cloned.1.call-start = ((), (), s32[]{:S(2)}) async-start(), calls=%async_computation.1 | async-start | bytes 3342336 | tf_op jit(solution)/shard_map/all_gather | solution.py:423
  10.6 99.8 %all-gather.10.cloned.1.call-start = ((), (), s32[]{:S(2)}) async-start(), calls=%async_computation | async-start | bytes 8912896 | tf_op jit(solution)/shard_map/all_gather | solution.py:422
  11.4 153.9 %all-gather.14.cloned.1.call-start = ((), (), s32[]{:S(2)}) async-start(), calls=%async_computation.2 | async-start | bytes 8912896 | tf_op jit(solution)/shard_map/all_gather | solution.py:424
  12.1 194.1 %all-gather.16.cloned.1.call-start = ((), (), s32[]{:S(2)}) async-start(), calls=%async_computation.3 | async-start | bytes 5013504 | tf_op jit(solution)/shard_map/all_gather | solution.py:435
  56.2 2.0 copy-start.3
  64.7 57.4 %copy-start.23 = (f32[16]{0:T(128)S(1)}, f32[16]{0:T(128)}, u32[]{:S(2)}) copy-start(f32[16]{0:T(128)} %param.30) | copy-start | bytes 196
  64.7 57.4 %copy-start.24 = (f32[16]{0:T(128)S(1)}, f32[16]{0:T(128)}, u32[]{:S(2)}) copy-start(f32[16]{0:T(128)} %param.29) | copy-start | bytes 196
  64.7 57.4 %copy-start.22 = (f32[16]{0:T(128)S(1)}, f32[16]{0:T(128)}, u32[]{:S(2)}) copy-start(f32[16]{0:T(128)} %param.31) | copy-start | bytes 196
  119.9 8.2 %collective-permute-start = (f32[8,1280]{1,0:T(8,128)S(1)}, f32[8,1280]{1,0:T(8,128)S(1)}, u32[]{:S(2)}, u32[]{:S(2)}) collective-permute-start(f32[8,1280]{1,0:T(8,128)S(1)} %pad_maximum_fusion.1), channel_id=1, source_target_pairs={{0,8},{8,16},{16,24},{24,32},{32,40},{40,48},{48,56},{56,64},{64,7... | collective-permute-start | bytes 122888 | tf_op jit(solution)/shard_map/ppermute | solution.py:430
  128.2 1.6 copy-start.14
  140.3 120.0 %all-gather.18.cloned.1.call-start = ((), (), s32[]{:S(2)}) async-start(), calls=%async_computation.4 | async-start | bytes 8912896 | tf_op jit(solution)/shard_map/all_gather | solution.py:425
  140.9 65.3 %copy-start.12 = (f32[1024]{0:T(1024)S(1)}, f32[1024]{0:T(1024)}, u32[]{:S(2)}) copy-start(f32[1024]{0:T(1024)} %param.32) | copy-start | bytes 12292
  140.9 260.0 %all-gather.20.cloned.1.call-start = ((), (), s32[]{:S(2)}) async-start(), calls=%async_computation.5 | async-start | bytes 4456448 | tf_op jit(solution)/shard_map/all_gather | solution.py:443
  206.2 2.3 copy-start.2
  208.6 1.6 copy-start.7
  261.6 3.4 copy-start.17
  272.7 47.2 %copy-start.6 = (bf16[512,512]{1,0:T(8,128)(2,1)S(1)}, bf16[512,512]{1,0:T(8,128)(2,1)}, u32[]{:S(2)}) copy-start(bf16[512,512]{1,0:T(8,128)(2,1)} %x_ref.1) | copy-start | bytes 1572868
  272.7 48.4 %copy-start.11 = (f32[4096]{0:T(1024)S(1)}, f32[4096]{0:T(1024)}, u32[]{:S(2)}) copy-start(f32[4096]{0:T(1024)} %param.34) | copy-start | bytes 49156
  359.8 3.5 copy-start.1
  359.8 2.0 copy-start.19
  407.3 2.2 copy-start.4
  (8 other events, 8.0 us)
Sparse Core Ops, SparseCore 0:
  10.7 45.3 all-gather.11
  57.9 52.5 all-gather.9
  112.2 53.0 all-gather.13
  167.4 38.7 all-gather.15
  207.8 52.5 all-gather.17
  364.2 36.6 all-gather.19

commit v2 on v1

--- a/solution.py
+++ b/solution.py
@@ -1,4 +1,3 @@
-import functools
 import jax
 import jax.numpy as jnp
 from jax import lax
@@ -7,118 +6,228 @@
 from jax.sharding import PartitionSpec as P
 
 MESH = pl.DeviceIdType.MESH
+VM = pl.BlockSpec(memory_space=pltpu.VMEM)
 P_SIZE = 64
 N = 128
 HD = 128
 WINDOW = 4096
 QB = 128
-VM = pl.BlockSpec(memory_space=pltpu.VMEM)
 
 
 def rows(start, size):
     return pl.ds(start, size)
 
 
-def mp_places():
+class Gather:
+    def __init__(self, view, own, names, pair, ring, core, sends, recvs, base, pieces, fan):
+        self.view, self.own, self.names = view, own, names
+        self.pair, self.ring, self.core = pair, ring, core
+        self.sends, self.recvs, self.next, self.pieces, self.fan = sends, recvs, base, pieces, fan
+        self.right, self.left, self.far = (ring + 1) % 4, (ring + 3) % 4, (ring + 2) % 4
+        self.started, self.across = [], []
+        self.y, self.a, self.b, self.f = {}, {}, {}, []
+
+    def send(self, src, block, piece, pair, ring, core):
+        copy = pltpu.make_async_remote_copy(
+            src_ref=src, dst_ref=self.view(*block, piece), send_sem=self.sends.at[self.next], recv_sem=self.recvs.at[self.next],
+            device_id=self.names(pair, ring, core), device_id_type=MESH)
+        self.next += 1
+        copy.start()
+        self.started.append(copy)
+        return copy
+
+    def over(self, src, block, piece):
+        if self.fan:
+            self.across.append(self.send(src, block, piece, self.pair, self.ring, 1 - self.core))
+
+    def begin(self):
+        me = (self.pair, self.ring, self.core)
+        for k, piece in enumerate(self.pieces):
+            src = self.own(piece)
+            self.y[k] = self.send(src, me, piece, 1 - self.pair, self.ring, self.core)
+            self.a[k] = [self.send(src, me, piece, self.pair, to, self.core) for to in (self.right, self.left)]
+            self.over(src, me, piece)
+
+    def second(self, k):
+        piece, block = self.pieces[k], (1 - self.pair, self.ring, self.core)
+        self.y[k].wait_recv()
+        src = self.view(*block, piece)
+        self.b[k] = [self.send(src, block, piece, self.pair, to, self.core) for to in (self.right, self.left)]
+        self.over(src, block, piece)
+
+    def forward(self, which, k):
+        pair = self.pair if which == 0 else 1 - self.pair
+        piece, first = self.pieces[k], k < len(self.pieces) // 2
+        for d, (to, origin) in enumerate(((self.right, self.left), (self.left, self.right))):
+            (self.a, self.b)[which][k][d].wait_recv()
+            block = (pair, origin, self.core)
+            src = self.view(*block, piece)
+            if first == (d == 0):
+                self.f.append((self.send(src, block, piece, self.pair, to, self.core), (pair, self.far, self.core), piece))
+            self.over(src, block, piece)
+
+    def last(self):
+        for copy, block, piece in self.f:
+            copy.wait_recv()
+            self.over(self.view(*block, piece), block, piece)
+
+    def finish(self):
+        for copy in self.across:
+            copy.wait_recv()
+        for copy in self.started:
+            copy.wait_send()
+
+
+def copies_of(pieces, fan):
+    return pieces * (7 + (8 if fan else 0))
+
+
+def seq_names(pair, ring, core):
+    return {"seq": (pair * 4 + ring) * 2 + core}
+
+
+def mp_names(pair, ring, core):
+    return {"mp": pair * 4 + ring}
+
+
+def greet(ids):
+    barrier = pltpu.get_barrier_semaphore()
+    for other in ids:
+        pl.semaphore_signal(barrier, inc=1, device_id=other, device_id_type=MESH)
+    pl.semaphore_wait(barrier, len(ids))
+
+
+def seq_place():
+    me = lax.axis_index("seq")
+    return me // 8, (me // 2) % 4, me % 2
+
+
+def mp_place():
     me = lax.axis_index("mp")
-    high, low = me // 4, me % 4
-    return high, low
-
-
-def mp_greet(others):
-    barrier = pltpu.get_barrier_semaphore()
-    for other in others:
-        pl.semaphore_signal(barrier, inc=1, device_id={"mp": other}, device_id_type=MESH)
-    pl.semaphore_wait(barrier, len(others))
-
-
-def gather_kernel(chunks, x_ref, gain_ref, normed_ref, out_ref, own_sem, ysend, yrecv, xsend, xrecv, fsend, frecv):
-    high, low = mp_places()
-    right, left = (low + 1) % 4, (low + 3) % 4
-    me, partner = high * 4 + low, (1 - high) * 4 + low
-    mp_greet((high * 4 + right, high * 4 + left, partner))
-    count = x_ref.shape[0] // chunks
-    half = x_ref.shape[0] // 2
-
-    def send(src, block, piece, target, ssem, rsem):
-        copy = pltpu.make_async_remote_copy(
-            src_ref=src, dst_ref=out_ref.at[block, piece], send_sem=ssem, recv_sem=rsem,
-            device_id={"mp": target}, device_id_type=MESH)
-        copy.start()
-        return copy
-
-    sides = ((right, left), (left, right))
-    started = []
-    ycopies, own = [], []
-    for c in range(chunks):
-        piece = rows(c * count, count)
-        ycopies.append(send(x_ref.at[piece], me, piece, partner, ysend.at[c], yrecv.at[c]))
-        own.append([
-            send(x_ref.at[piece], me, piece, high * 4 + to, xsend.at[0, d, c], xrecv.at[0, d, c])
-            for d, (to, _) in enumerate(sides)])
-    local = pltpu.make_async_copy(x_ref, out_ref.at[me], own_sem)
-    local.start()
-    other = []
-    for c in range(chunks):
-        piece = rows(c * count, count)
-        ycopies[c].wait_recv()
-        other.append([
-            send(out_ref.at[partner, piece], partner, piece, high * 4 + to, xsend.at[1, d, c], xrecv.at[1, d, c])
-            for d, (to, _) in enumerate(sides)])
-    forwards = []
-    for k, copies in enumerate((own, other)):
-        for c in range(chunks):
-            for d, (to, origin) in enumerate(sides):
-                copies[c][d].wait_recv()
-                if (c * count < half) == (d == 0):
-                    block = (high if k == 0 else 1 - high) * 4 + origin
-                    piece = rows(c * count, count)
-                    forwards.append(send(out_ref.at[block, piece], block, piece, high * 4 + to,
-                                         fsend.at[k, c], frecv.at[k, c]))
-    for copy in forwards:
-        copy.wait()
-    local.wait()
-    for c in range(chunks):
-        ycopies[c].wait_send()
-        for copies in (own, other):
-            for d in range(2):
-                copies[c][d].wait_send()
-    wide = x_ref.shape[1]
+    return me // 4, me % 4
+
+
+def neighbours(names, pair, ring, core, fan):
+    ids = [names(1 - pair, ring, core), names(pair, (ring + 1) % 4, core), names(pair, (ring + 3) % 4, core)]
+    return ids + ([names(pair, ring, 1 - core)] if fan else [])
+
+
+def cut(total, count):
+    return [pl.ds(k * (total // count), total // count) for k in range(count)]
+
+
+def write_normed(whole, gain_ref, normed_ref):
+    blocks, n, wide = whole.shape
 
     def norm(c, _):
         piece = rows(pl.multiple_of(c * 32, 32), 32)
         square = jnp.zeros((32, wide), jnp.float32)
-        for b in range(8):
-            value = out_ref[b, piece, :].astype(jnp.float32)
+        for b in range(blocks):
+            value = whole[b, piece, :].astype(jnp.float32)
             square = square + value * value
-        scale = lax.rsqrt(jnp.sum(square, axis=1, keepdims=True) / (8 * wide) + 1e-05)
-        for b in range(8):
+        scale = lax.rsqrt(jnp.sum(square, axis=1, keepdims=True) / (blocks * wide) + 1e-05)
+        for b in range(blocks):
             lanes = slice(b * wide, (b + 1) * wide)
-            normed_ref[piece, lanes] = (out_ref[b, piece, :].astype(jnp.float32) * scale
-                                        * gain_ref[:, lanes]).astype(normed_ref.dtype)
+            normed_ref[piece, lanes] = (whole[b, piece, :].astype(jnp.float32) * scale * gain_ref[:, lanes]).astype(normed_ref.dtype)
         return 0
 
-    lax.fori_loop(0, x_ref.shape[0] // 32, norm, 0)
-
-
-def mp_gather_norm(x, gain, cid, chunks=4):
+    lax.fori_loop(0, n // 32, norm, 0)
+
+
+def first_kernel(x_ref, wx_ref, wb_ref, gain_ref, normed_ref, wxa_ref, wba_ref, whole, local, ms, mr, bs, br, xs, xr):
+    mpair, mring = mp_place()
+    spair, sring, score = seq_place()
+    greet(neighbours(mp_names, mpair, mring, 0, False) + neighbours(seq_names, spair, sring, score, True))
+    depth = wx_ref.shape[0]
+
+    def wide_view(ref):
+        return lambda pair, ring, core, piece: ref.at[pl.ds(((pair * 4 + ring) * 2 + core) * depth + piece.start, piece.size), :]
+
+    hidden = Gather(lambda pair, ring, core, piece: whole.at[pair * 4 + ring, piece], lambda piece: x_ref.at[piece], mp_names,
+                    mpair, mring, 0, ms, mr, 0, cut(x_ref.shape[0], 2), False)
+    small = Gather(wide_view(wba_ref), lambda piece: wb_ref.at[piece], seq_names, spair, sring, score, bs, br, 0, cut(depth, 2), True)
+    big = Gather(wide_view(wxa_ref), lambda piece: wx_ref.at[piece], seq_names, spair, sring, score, xs, xr, 0, cut(depth, 2), True)
+    here = (spair * 4 + sring) * 2 + score
+    mine = [pltpu.make_async_copy(x_ref, whole.at[mpair * 4 + mring], local.at[0]),
+            pltpu.make_async_copy(wx_ref, wxa_ref.at[pl.ds(here * depth, depth), :], local.at[1]),
+            pltpu.make_async_copy(wb_ref, wba_ref.at[pl.ds(here * depth, depth), :], local.at[2])]
+    everything = (hidden, small, big)
+    for g in everything:
+        g.begin()
+    for copy in mine:
+        copy.start()
+    for k in range(2):
+        for g in (small, hidden, big):
+            g.second(k)
+    for which in range(2):
+        for k in range(2):
+            for g in (small, hidden, big):
+                g.forward(which, k)
+    hidden.last()
+    mine[0].wait()
+    write_normed(whole, gain_ref, normed_ref)
+    small.last()
+    big.last()
+    for g in everything:
+        g.finish()
+    for copy in mine[1:]:
+        copy.wait()
+
+
+def run_first(x, wx, wb, gain, cid):
+    n, w = x.shape
+    depth = wx.shape[0]
+    D = pltpu.SemaphoreType.DMA
+    few, many = copies_of(2, False), copies_of(2, True)
+    bf = jnp.bfloat16
+    return pl.pallas_call(
+        first_kernel,
+        out_shape=(jax.ShapeDtypeStruct((n, 8 * w), bf), jax.ShapeDtypeStruct((16 * depth, wx.shape[1]), bf),
+                   jax.ShapeDtypeStruct((16 * depth, wb.shape[1]), bf)),
+        in_specs=[VM] * 4, out_specs=(VM,) * 3,
+        scratch_shapes=[pltpu.VMEM((8, n, w), bf), D((3,)), D((few,)), D((few,)), D((many,)), D((many,)), D((many,)), D((many,))],
+        compiler_params=pltpu.CompilerParams(collective_id=cid, has_side_effects=True, vmem_limit_bytes=40 << 20),
+    )(x, wx, wb, gain)
+
+
+def norm_kernel(x_ref, gain_ref, normed_ref, whole, local, ms, mr):
+    pair, ring = mp_place()
+    greet(neighbours(mp_names, pair, ring, 0, False))
+    hidden = Gather(lambda pair, ring, core, piece: whole.at[pair * 4 + ring, piece], lambda piece: x_ref.at[piece], mp_names,
+                    pair, ring, 0, ms, mr, 0, cut(x_ref.shape[0], 4), False)
+    mine = pltpu.make_async_copy(x_ref, whole.at[pair * 4 + ring], local)
+    hidden.begin()
+    mine.start()
+    for k in range(4):
+        hidden.second(k)
+    for which in range(2):
+        for k in range(4):
+            hidden.forward(which, k)
+    hidden.last()
+    hidden.finish()
+    mine.wait()
+    write_normed(whole, gain_ref, normed_ref)
+
+
+def run_norm(x, gain, cid):
     n, w = x.shape
     D = pltpu.SemaphoreType.DMA
-    return pl.pallas_call(
-        functools.partial(gather_kernel, chunks),
+    few = copies_of(4, False)
+    return pl.pallas_call(
+        norm_kernel,
         out_shape=jax.ShapeDtypeStruct((n, 8 * w), x.dtype),
         in_specs=[VM, VM], out_specs=VM,
-        scratch_shapes=[pltpu.VMEM((8, n, w), x.dtype), D, D((chunks,)), D((chunks,)), D((2, 2, chunks)), D((2, 2, chunks)), D((2, chunks)), D((2, chunks))],
+        scratch_shapes=[pltpu.VMEM((8, n, w), x.dtype), D, D((few,)), D((few,))],
         compiler_params=pltpu.CompilerParams(collective_id=cid, has_side_effects=True, vmem_limit_bytes=24 << 20),
     )(x, gain)
 
 
 def reduce_kernel(p_ref, out_ref, tmp, d1, d2, ysrc, ydst, s1, r1, s2, r2, sy, ry, sraw, rraw):
-    high, low = mp_places()
+    high, low = mp_place()
     right, left = (low + 1) % 4, (low + 3) % 4
     far = (low + 2) % 4
     partner = (1 - high) * 4 + low
-    mp_greet((high * 4 + right, high * 4 + left, partner))
+    greet(neighbours(mp_names, high, low, 0, False))
     n = p_ref.shape[1]
     half = n // 2
     order = (1 - high, high)
@@ -275,16 +384,46 @@
     )(xp, bcd, rimx, rimbc, conv_x, conv_bc, bias, rate, skip)
 
 
-def gate_kernel(y_ref, cc_ref, cum_ref, states_ref, gate_ref, gain_ref, out_ref, incoming, full):
+def gate_kernel(normed_ref, wz_ref, send_ref, y_ref, cc_ref, cum_ref, gain_ref, out_ref, states, incoming, gate, local, ss, sr):
     place = lax.axis_index("seq")
+    pair, ring, core = seq_place()
+    greet(neighbours(seq_names, pair, ring, core, True))
     n, width = y_ref.shape
     bf, f32 = jnp.bfloat16, jnp.float32
+    tall = send_ref.shape[0]
+    every = Gather(lambda pair, ring, core, piece: states.at[(pair * 4 + ring) * 2 + core, piece], lambda piece: send_ref.at[piece],
+                   seq_names, pair, ring, core, ss, sr, 0, [pl.ds(0, 80), pl.ds(80, tall - 80)], True)
+    mine = pltpu.make_async_copy(send_ref, states.at[place], local)
+    every.begin()
+    mine.start()
+
+    def matmul(part):
+        lanes = slice(part * 128, (part + 1) * 128)
+        gate[:, lanes] = jnp.dot(normed_ref[...], wz_ref[:, lanes], preferred_element_type=f32)
+
+    matmul(0)
+    matmul(1)
+    every.second(0)
+    every.second(1)
+    matmul(2)
+    every.forward(0, 0)
+    every.forward(0, 1)
+    matmul(3)
+    matmul(4)
+    every.forward(1, 0)
+    every.forward(1, 1)
+    matmul(5)
+    matmul(6)
+    matmul(7)
+    every.last()
+    every.finish()
+    mine.wait()
     incoming[...] = jnp.zeros_like(incoming)
 
     def add(k, _):
-        tail = states_ref[k, N:N + 16, :].astype(f32)
+        tail = states[k, N:N + 16, :].astype(f32)
         decay = tail[0:1] + (tail[1:2] + tail[2:3])
-        incoming[...] = decay * incoming[...] + states_ref[k, 0:N, :].astype(f32)
+        incoming[...] = decay * incoming[...] + states[k, 0:N, :].astype(f32)
         return 0
 
     lax.fori_loop(0, place, add, 0)
@@ -300,27 +439,29 @@
             ct = jnp.where(low, jnp.broadcast_to(cum[:, 2 * p:2 * p + 1], (QB, 128)),
                            jnp.broadcast_to(cum[:, 2 * p + 1:2 * p + 2], (QB, 128)))
             carried = jnp.dot(cv, incoming[:, lanes].astype(bf), preferred_element_type=f32)
-            g = gate_ref[here, lanes]
+            g = gate[here, lanes]
             value = (y_ref[here, lanes] + jnp.exp(ct) * carried) * (g / (1.0 + jnp.exp(-g)))
-            full[:, lanes] = value
+            gate[here, lanes] = value
             square = square + value * value
         scale = lax.rsqrt(jnp.sum(square, axis=1, keepdims=True) / width + 1e-05)
-        out_ref[here, :] = (full[...] * scale * gain_ref[...]).astype(bf)
+        out_ref[here, :] = (gate[here, :] * scale * gain_ref[...]).astype(bf)
         return 0
 
     lax.fori_loop(0, n // QB, one, 0)
 
 
-def run_gate(y, cc, cum, states, gate, gain):
+def run_gate(normed, wz, send, y, cc, cum, gain, cid):
     n, width = y.shape
+    D = pltpu.SemaphoreType.DMA
+    many = copies_of(2, True)
     return pl.pallas_call(
         gate_kernel,
         out_shape=jax.ShapeDtypeStruct((n, width), jnp.bfloat16),
-        in_specs=[VM] * 6, out_specs=VM,
-        scratch_shapes=[pltpu.VMEM((N, width), jnp.float32), pltpu.VMEM((QB, width), jnp.float32)],
-        compiler_params=pltpu.CompilerParams(vmem_limit_bytes=32 << 20),
-        cost_estimate=pl.CostEstimate(flops=2_000_000_000, bytes_accessed=8 << 20, transcendentals=0),
-    )(y, cc, cum, states, gate, gain)
+        in_specs=[VM] * 7, out_specs=VM,
+        scratch_shapes=[pltpu.VMEM((16,) + send.shape, jnp.bfloat16), pltpu.VMEM((N, width), jnp.float32),
+                        pltpu.VMEM((n, width), jnp.float32), D, D((many,)), D((many,))],
+        compiler_params=pltpu.CompilerParams(collective_id=cid, has_side_effects=True, vmem_limit_bytes=40 << 20),
+    )(normed, wz, send, y, cc, cum, gain)
 
 
 def out_kernel(y_ref, w_ref, out_ref):
@@ -406,10 +547,6 @@
     )(q, kv)
 
 
-def rms_norm(values, gain):
-    return values * lax.rsqrt(jnp.mean(values * values, axis=-1, keepdims=True) + 1e-05) * gain
-
-
 def padded(vector):
     return jnp.pad(vector, (0, 128 - vector.shape[0]))[None, :]
 
@@ -419,11 +556,9 @@
     f32, bf = jnp.float32, jnp.bfloat16
     n = hidden_in.shape[0]
     w_bcd = jnp.concatenate([w_b, w_c, jnp.pad(w_dt, ((0, 0), (0, 128 - w_dt.shape[1])))], axis=1)
-    w_x_all = lax.all_gather(w_x, "seq", axis=0, tiled=True)
-    w_bcd_all = lax.all_gather(w_bcd, "seq", axis=0, tiled=True)
     w_z_all = lax.all_gather(w_z, "seq", axis=0, tiled=True)
     w_out_all = lax.all_gather(w_out, "seq")
-    normed = mp_gather_norm(hidden_in, norm_gain[None, :], 0)
+    normed, w_x_all, w_bcd_all = run_first(hidden_in, w_x, w_bcd, norm_gain[None, :], 0)
     bcd = jnp.dot(normed, w_bcd_all, preferred_element_type=f32)
     xp = jnp.dot(normed, w_x_all, preferred_element_type=f32)
     route = [(i, i + 1) for i in range(lax.axis_size("seq") - 1)]
@@ -432,12 +567,10 @@
     y, cc, cum, send = run_ssd(
         xp, bcd, rims[:, 0:width], rims[:, width:], conv_x, jnp.concatenate([conv_b, conv_c], axis=1),
         padded(dt_bias), padded(a_rate), jnp.repeat(skip_gain, P_SIZE)[None, :])
-    states = lax.all_gather(send, "seq")
-    gate = jnp.dot(normed, w_z_all, preferred_element_type=f32)
-    y_normed = run_gate(y, cc, cum, states, gate, group_gain[None, :])
+    y_normed = run_gate(normed, w_z_all, send, y, cc, cum, group_gain[None, :], 3)
     parts = run_out(y_normed, w_out_all)
     mixed = hidden_in.astype(f32) + mp_reduce(parts, 1)
-    normed_two = mp_gather_norm(mixed.astype(bf), attn_gain[None, :], 2)
+    normed_two = run_norm(mixed.astype(bf), attn_gain[None, :], 2)
     keys = jnp.dot(normed_two, w_k, preferred_element_type=f32).astype(bf)
     values = jnp.dot(normed_two, w_v, preferred_element_type=f32).astype(bf)
     kv = lax.all_gather(jnp.concatenate([keys, values], axis=1), "seq")

time: 438 us -> 360 us (0.82)
  waiting for transfers between devices: 186 us -> 38.2 us
  Pallas kernels: 168 us -> 254 us
  matrix products: 32.9 us -> 15.6 us
    all_gather x3 -> x0, waiting for transfers between devices: 76.3 us -> none  [the longest x1 45.8 us: on_device(): w_x_all = lax.all_gather(w_x, 'seq', axis=0, tiled=True)]
    pallas_call x2, Pallas kernels: 80.9 us -> 136 us  [the longest x1 96.5 us: run_first(): pl.pallas_call(first_kernel, out_shape=(jax.ShapeDtypeStruct((n, 8 * w),...]
    all_gather x1, waiting for transfers between devices: 46.4 us -> 0.01 us  [on_device(): w_out_all = lax.all_gather(w_out, 'seq')]
    pallas_call x1, Pallas kernels: 2.79 us -> 34.1 us  [run_gate(): pl.pallas_call(gate_kernel, out_shape=jax.ShapeDtypeStruct((n, width), jn...]
    all_gather x1, waiting for transfers between devices: 24.3 us -> 0.01 us  [on_device(): w_z_all = lax.all_gather(w_z, 'seq', axis=0, tiled=True)]
    dot_general x1 -> x0, matrix products: 10.5 us -> none  [on_device(): gate = jnp.dot(normed, w_z_all, preferred_element_type=f32)]
    unnamed x52 -> x63, local copies, waits for them, and re-layouts: 23.6 us -> 24.3 us
  transfers between devices with their start and end apart: 7 -> 4, of which waited for: 6 -> 2; matrix products, arithmetic and copies ran while one was open for 7% -> 4% of each run, Pallas kernels for 12% -> 39%
where the time goes in v2:
time: 360 us; the launch traced here: 358 us
  Pallas kernels  254 us (71%)
  waiting for transfers between devices  38.2 us (11%)
  local copies, waits for them, and re-layouts  30.9 us (9%)
  matrix products  15.6 us (4%)
  between operations  14.1 us (4%)
    pallas_call x1, Pallas kernels, run_first(): pl.pallas_call(first_kernel, out_shape=(jax.ShapeDtypeStruct((n, 8 * w),...  96.5 us
    pallas_call x1, Pallas kernels, mp_reduce(): pl.pallas_call(reduce_kernel, out_shape=jax.ShapeDtypeStruct((n, w), jnp....  47.7 us
    pallas_call x1, Pallas kernels, run_norm(): pl.pallas_call(norm_kernel, out_shape=jax.ShapeDtypeStruct((n, 8 * w), x....  39.2 us
    pallas_call x1, Pallas kernels, run_gate(): pl.pallas_call(gate_kernel, out_shape=jax.ShapeDtypeStruct((n, width), jn...  34.1 us
    all_gather x1, waiting for transfers between devices, on_device(): kv = lax.all_gather(jnp.concatenate([keys, values], axis=1), 'seq')  31.3 us
    unnamed x63, local copies, waits for them, and re-layouts  24.3 us
    pallas_call x1, Pallas kernels, run_attention(): pl.pallas_call(attention_kernel, out_shape=jax.ShapeDtypeStruct((n, width...  21 us
    pallas_call x1, Pallas kernels, run_ssd(): pl.pallas_call(ssd_kernel, out_shape=(jax.ShapeDtypeStruct((n, width), f3...  7.85 us
  transfers between devices with their start and end apart: 4, of which 2 were waited for; matrix products, arithmetic and copies ran while one was open for 4% of the time, Pallas kernels for 39%

profile of v2, /device:TPU:8, one launch (start us, length us, event | category | flops | bytes accessed | tf_op | source)
XLA Modules:
  0.0 358.5 jit_solution(12334678813922398735)
XLA Ops:
  13.2 96.5 %shard_map.194 = (bf16[512,4096]{1,0:T(8,128)(2,1)S(1)}, bf16[4096,1024]{1,0:T(8,128)(2,1)}, bf16[4096,384]{1,0:T(8,128)(2,1)S(1)}) custom-call(bf16[512,512]{1,0:T(8,128)(2,1)S(1)} %copy-done.6, bf16[256,1024]{1,0:T(8,128)(2,1)S(1)} %copy-done.10, bf16[256,384]{1,0:T(8,128)(2,1)S(1)} %fusion.1.wb_ref, f32[1,4096]{1,0:T(1,128)S(1)} %bitcast.20), custom_call_target="tpu_custom_call" | custom-call | tf_op jit(solution)/shard_map/pallas_call | solution.py:183
  109.8 2.3 fusion.4.bcd_ref
  113.0 1.9 copy-done.30
  115.0 4.5 %fusion.3.xp_ref = f32[512,1024]{1,0:T(8,128)S(1)} fusion(bf16[512,4096]{1,0:T(8,128)(2,1)S(1)} %get-tuple-element.9.normed_ref, bf16[4096,1024]{1,0:T(8,128)(2,1)S(1)} %copy-done.30), kind=kOutput, calls=%fused_computation.13 | convolution fusion | flops 4294967296 | bytes 14680064 | tf_op jit(solution)/shard_map/dot_general | solution.py:563
  119.5 1.3 copy-done.18
  120.9 2.7 collective-permute-start
  123.8 5.5 %collective-permute-done = f32[8,1280]{1,0:T(8,128)S(1)} collective-permute-done((f32[8,1280]{1,0:T(8,128)S(1)}, f32[8,1280]{1,0:T(8,128)S(1)}, u32[]{:S(2)}, u32[]{:S(2)}) %collective-permute-start) | collective-permute-done | bytes 40992 | tf_op jit(solution)/shard_map/ppermute | solution.py:565
  129.3 1.6 copy-done.19
  132.0 7.8 %shard_map.195 = (f32[512,1024]{1,0:T(8,128)S(1)}, bf16[512,128]{1,0:T(8,128)(2,1)S(1)}, f32[512,128]{1,0:T(8,128)S(1)}, bf16[144,1024]{1,0:T(8,128)(2,1)S(1)}) custom-call(f32[512,1024]{1,0:T(8,128)S(1)} %copy-done.19, f32[512,384]{1,0:T(8,128)S(1)} %copy-done.21, f32[8,1024]{1,0:T(8,128)S(1)} %slice.18.rimx_ref, f32[8,256]{1,0:T(8,128)S(1)} %slice.19.rimbc_ref, ...), custom_call_target="tpu_custom_call" | custom-call | flops 4000000000 | bytes 8388608 | tf_op jit(solution)/shard_map/pallas_call | solution.py:376
  141.3 2.3 copy-done.4
  145.4 34.1 %shard_map.196.y_ref = bf16[512,1024]{1,0:T(8,128)(2,1)S(1)} custom-call(bf16[512,4096]{1,0:T(8,128)(2,1)S(1)} %copy-done.4, bf16[4096,1024]{1,0:T(8,128)(2,1)} %all-gather.6.cloned.1.call-done.wz_ref, bf16[144,1024]{1,0:T(8,128)(2,1)S(1)} %get-tuple-element.12.send_ref, f32[512,1024]{1,0:T(8,128)S(1)} %get-tuple-element.13.y_ref, ...), custom_call_target="tpu_custom_call" | custom-call | tf_op jit(solution)/shard_map/pallas_call | solution.py:457
  180.5 1.2 copy-done.9
  181.7 3.4 copy-done.22
  185.1 7.7 %shard_map.197.p_ref = bf16[8,512,512]{2,1,0:T(8,128)(2,1)S(1)} custom-call(bf16[512,1024]{1,0:T(8,128)(2,1)S(1)} %copy-done.9, bf16[16,1024,256]{2,1,0:T(8,128)(2,1)S(1)} %bitcast.23), custom_call_target="tpu_custom_call" | custom-call | flops 4294967296 | bytes 16777216 | tf_op jit(solution)/shard_map/pallas_call | solution.py:474
  192.9 47.7 %shard_map.198 = f32[512,512]{1,0:T(8,128)S(1)} custom-call(bf16[8,512,512]{2,1,0:T(8,128)(2,1)S(1)} %shard_map.197.p_ref), custom_call_target="tpu_custom_call" | custom-call | tf_op jit(solution)/shard_map/pallas_call | solution.py:280
  240.6 1.2 fusion.2
  241.8 39.2 %shard_map.199 = bf16[512,4096]{1,0:T(8,128)(2,1)S(1)} custom-call(bf16[512,512]{1,0:T(8,128)(2,1)S(1)} %get-tuple-element.16.x_ref, f32[1,4096]{1,0:T(1,128)S(1)} %bitcast.21), custom_call_target="tpu_custom_call" | custom-call | tf_op jit(solution)/shard_map/pallas_call | solution.py:216
  281.0 1.5 convolution_convert_fusion.1
  283.0 1.5 convolution_convert_fusion.2
  285.3 5.8 %convolution_convert_fusion.q_ref = bf16[512,512]{1,0:T(8,128)(2,1)S(1)} fusion(bf16[512,4096]{1,0:T(8,128)(2,1)} %copy-done.2, bf16[4096,512]{1,0:T(8,128)(2,1)} %param.35), kind=kOutput, calls=%fused_computation | convolution fusion | flops 2147745792 | bytes 8912896 | tf_op jit(solution)/shard_map/dot_general | solution.py:577
  291.1 31.3 %all-gather.10.cloned.1.call-done = bf16[8192,256]{0,1:T(8,128)(2,1)} async-done(((bf16[512,256]{0,1:T(8,128)(2,1)}), bf16[8192,256]{0,1:T(8,128)(2,1)}) %all-gather.10.cloned.1.call-update) | async-done | bytes 4194320 | tf_op jit(solution)/shard_map/all_gather | solution.py:576
  322.4 6.4 %copy.22 = bf16[8192,256]{1,0:T(8,128)(2,1)} copy(bf16[8192,256]{0,1:T(8,128)(2,1)} %all-gather.10.cloned.1.call-done) | data formatting | bytes 8388608 | tf_op jit(solution)/shard_map/all_gather | solution.py:576
  328.8 2.2 copy-done.5
  331.0 21.0 %shard_map.200 = f32[512,512]{1,0:T(8,128)} custom-call(bf16[512,512]{1,0:T(8,128)(2,1)S(1)} %convolution_convert_fusion.q_ref, bf16[16,512,256]{2,1,0:T(8,128)(2,1)S(1)} %bitcast.19), custom_call_target="tpu_custom_call" | custom-call | flops 8589934592 | bytes 8388608 | tf_op jit(solution)/shard_map/pallas_call | solution.py:537
  (75 shorter events, 13.7 us)
Async XLA Ops:
  7.2 273.8 %copy-start = (bf16[4096,128]{1,0:T(8,128)(2,1)S(1)}, bf16[4096,128]{1,0:T(8,128)(2,1)}, u32[]{:S(2)}) copy-start(bf16[4096,128]{1,0:T(8,128)(2,1)} %param.37) | copy-start | bytes 3145732
  7.2 134.1 %all-gather.6.cloned.1.call-start = ((), (), s32[]{:S(2)}) async-start(), calls=%async_computation | async-start | bytes 8912896 | tf_op jit(solution)/shard_map/all_gather | solution.py:559
  7.9 172.6 %all-gather.8.cloned.1.call-start = ((), (), s32[]{:S(2)}) async-start(), calls=%async_computation.1 | async-start | bytes 8912896 | tf_op jit(solution)/shard_map/all_gather | solution.py:560
  8.7 313.7 %all-gather.10.cloned.1.call-start = ((), (), s32[]{:S(2)}) async-start(), calls=%async_computation.2 | async-start | bytes 4456448 | tf_op jit(solution)/shard_map/all_gather | solution.py:576
  109.8 3.2 copy-start.3
  109.8 5.2 %copy-start.30 = (bf16[4096,1024]{1,0:T(8,128)(2,1)S(1)}, bf16[4096,1024]{1,0:T(8,128)(2,1)}, u32[]{:S(2)}) copy-start(bf16[4096,1024]{1,0:T(8,128)(2,1)} %get-tuple-element.10) | copy-start | bytes 25165828
  115.0 8.6 %copy-start.25 = (f32[4,128]{1,0:T(4,128)S(1)}, f32[4,128]{1,0:T(4,128)}, u32[]{:S(2)}) copy-start(f32[4,128]{1,0:T(4,128)} %param.28) | copy-start | bytes 6148
  115.0 8.6 %copy-start.26 = (f32[4,128]{1,0:T(4,128)S(1)}, f32[4,128]{1,0:T(4,128)}, u32[]{:S(2)}) copy-start(f32[4,128]{1,0:T(4,128)} %param.27) | copy-start | bytes 6148
  115.0 8.7 %copy-start.28 = (f32[16]{0:T(128)S(1)}, f32[16]{0:T(128)}, u32[]{:S(2)}) copy-start(f32[16]{0:T(128)} %param.30) | copy-start | bytes 196
  115.0 8.7 %copy-start.29 = (f32[16]{0:T(128)S(1)}, f32[16]{0:T(128)}, u32[]{:S(2)}) copy-start(f32[16]{0:T(128)} %param.29) | copy-start | bytes 196
  115.0 8.7 %copy-start.27 = (f32[16]{0:T(128)S(1)}, f32[16]{0:T(128)}, u32[]{:S(2)}) copy-start(f32[16]{0:T(128)} %param.31) | copy-start | bytes 196
  115.0 14.3 %copy-start.23 = (f32[4,1024]{1,0:T(4,128)S(1)}, f32[4,1024]{1,0:T(4,128)}, u32[]{:S(2)}) copy-start(f32[4,1024]{1,0:T(4,128)} %cx_ref.1) | copy-start | bytes 49156
  119.5 1.4 copy-start.18
  120.9 8.4 %collective-permute-start = (f32[8,1280]{1,0:T(8,128)S(1)}, f32[8,1280]{1,0:T(8,128)S(1)}, u32[]{:S(2)}, u32[]{:S(2)}) collective-permute-start(f32[8,1280]{1,0:T(8,128)S(1)} %pad_maximum_fusion.1), channel_id=1, source_target_pairs={{0,8},{8,16},{16,24},{24,32},{32,40},{40,48},{48,56},{56,64},{64,7... | collective-permute-start | bytes 122888 | tf_op jit(solution)/shard_map/ppermute | solution.py:565
  129.3 1.6 copy-start.19
  132.0 9.2 %copy-start.17 = (f32[1024]{0:T(1024)S(1)}, f32[1024]{0:T(1024)}, u32[]{:S(2)}) copy-start(f32[1024]{0:T(1024)} %param.32) | copy-start | bytes 12292
  141.3 2.3 copy-start.4
  181.7 3.4 copy-start.22
  192.9 47.8 %copy-start.7 = (bf16[512,512]{1,0:T(8,128)(2,1)S(1)}, bf16[512,512]{1,0:T(8,128)(2,1)}, u32[]{:S(2)}) copy-start(bf16[512,512]{1,0:T(8,128)(2,1)} %x_ref.1) | copy-start | bytes 1572868
  192.9 48.9 %copy-start.16 = (f32[4096]{0:T(1024)S(1)}, f32[4096]{0:T(1024)}, u32[]{:S(2)}) copy-start(f32[4096]{0:T(1024)} %param.34) | copy-start | bytes 49156
  281.0 3.5 copy-start.2
  281.0 2.0 copy-start.24
  328.8 2.2 copy-start.5
  331.0 21.0 %copy-start.1 = (bf16[4096,128]{1,0:T(8,128)(2,1)S(1)}, bf16[4096,128]{1,0:T(8,128)(2,1)}, u32[]{:S(2)}) copy-start(bf16[4096,128]{1,0:T(8,128)(2,1)} %param.37) | copy-start | bytes 3145732
  (11 other events, 10.2 us)
Sparse Core Ops, SparseCore 0:
  9.7 93.7 all-gather.5
  105.2 57.2 all-gather.7
  285.4 36.9 all-gather.9

commit v3 on v2

--- a/solution.py
+++ b/solution.py
@@ -482,69 +482,107 @@
     )(y, w)
 
 
-def attention_kernel(q_ref, kv_ref, out_ref, peak, total):
+def attention_kernel(x_ref, wq_ref, wk_ref, wv_ref, out_ref, own, kv, q, peak, total, local, ss, sr):
     place = lax.axis_index("seq")
-    j = pl.program_id(0)
-    reach = pl.num_programs(0) - 1
-    n = q_ref.shape[0]
-    heads = q_ref.shape[1] // HD
+    pair, ring, core = seq_place()
+    greet(neighbours(seq_names, pair, ring, core, True))
+    n = x_ref.shape[0]
+    heads = q.shape[0]
+    bf, f32 = jnp.bfloat16, jnp.float32
     scale = HD ** -0.5 * 1.4426950408889634
-
-    @pl.when(j == 0)
-    def _():
-        peak[...] = jnp.full_like(peak, -1e30)
-        total[...] = jnp.zeros_like(total)
-
-    def work(edge):
-        keys = kv_ref[0, :, 0:HD]
-        both = jnp.concatenate([kv_ref[0, :, HD:2 * HD], jnp.ones((n, HD), jnp.bfloat16)], axis=1)
-        for h in range(heads):
-            scores = lax.dot_general(q_ref[:, h * HD:(h + 1) * HD], keys, (((1,), (1,)), ((), ())),
-                                     preferred_element_type=jnp.float32) * scale
+    own[:, 0:HD] = jnp.dot(x_ref[...], wk_ref[...], preferred_element_type=f32).astype(bf)
+    own[:, HD:2 * HD] = jnp.dot(x_ref[...], wv_ref[...], preferred_element_type=f32).astype(bf)
+    every = Gather(lambda pair, ring, core, piece: kv.at[(pair * 4 + ring) * 2 + core, piece], lambda piece: own.at[piece],
+                   seq_names, pair, ring, core, ss, sr, 0, cut(n, 2), True)
+    every.begin()
+    for h in range(heads):
+        q[h] = jnp.dot(x_ref[...], wq_ref[:, h * HD:(h + 1) * HD], preferred_element_type=f32).astype(bf)
+    peak[...] = jnp.full_like(peak, -1e30)
+    total[...] = jnp.zeros_like(total)
+
+    def work(block, edge):
+        def head(h, _):
+            keys = block[:, 0:HD]
+            both = jnp.concatenate([block[:, HD:2 * HD], jnp.ones((n, HD), bf)], axis=1)
             if edge is not None:
                 t = lax.broadcasted_iota(jnp.int32, (n, n), 0)
                 s = lax.broadcasted_iota(jnp.int32, (n, n), 1)
-                scores = jnp.where(s > t if edge == 0 else s <= t, scores, -1e30)
+                allowed = s > t if edge == 0 else s <= t
+            scores = lax.dot_general(q[h], keys, (((1,), (1,)), ((), ())), preferred_element_type=f32) * scale
+            if edge is not None:
+                scores = jnp.where(allowed, scores, -1e30)
             old = peak[h]
             new = jnp.maximum(old, jnp.max(scores, axis=1, keepdims=True))
             weights = jnp.exp2(scores - new[:, 0:1])
             if edge == 0:
-                weights = jnp.where(s > t, weights, 0.0)
+                weights = jnp.where(allowed, weights, 0.0)
             shrink = jnp.exp2(old - new)
             peak[h] = new
             total[h] = jnp.concatenate([shrink, shrink], axis=1) * total[h] + jnp.dot(
-                weights.astype(jnp.bfloat16), both, preferred_element_type=jnp.float32)
-
-    @pl.when((j == 0) & (place >= reach))
+                weights.astype(bf), both, preferred_element_type=f32)
+            return 0
+
+        lax.fori_loop(0, heads, head, 0)
+
+    def visit(first, count, chip):
+        def one(j, _):
+            other_pair, other_ring = chip(j // 2)
+            which = (other_pair * 4 + other_ring) * 2 + j % 2
+            away = place - which
+
+            @pl.when((away >= 1) & (away < WINDOW // n))
+            def _():
+                work(kv.at[which], None)
+            return 0
+
+        lax.fori_loop(first, count, one, 0)
+
+    work(own, 1)
+    every.second(0)
+    every.second(1)
+
+    @pl.when(pair == 1)
     def _():
-        work(0)
-
-    @pl.when((j > 0) & (j < reach) & (place + j >= reach))
-    def _():
-        work(None)
-
-    @pl.when(j == reach)
-    def _():
-        work(1)
-        for h in range(heads):
-            out_ref[:, h * HD:(h + 1) * HD] = total[h, :, 0:HD] / total[h, :, HD:2 * HD]
-
-
-def run_attention(q, kv):
-    n, width = q.shape
-    reach = WINDOW // n
+        work(kv.at[ring * 2 + core], 0)
+
+    every.forward(0, 0)
+    every.forward(0, 1)
+    for copy in every.across[0:4]:
+        copy.wait_recv()
+    mine = pltpu.make_async_copy(own, kv.at[place], local)
+    mine.start()
+    mine.wait()
+    visit(0, 4, lambda g: (jnp.where(g == 0, pair, 1 - pair), ring))
+    every.forward(1, 0)
+    every.forward(1, 1)
+    for copy in every.across[4:12]:
+        copy.wait_recv()
+    visit(0, 8, lambda g: (jnp.where(g < 2, pair, 1 - pair), (ring + 1 + 2 * (g % 2)) % 4))
+    every.last()
+    for copy in every.across[12:]:
+        copy.wait_recv()
+    visit(0, 4, lambda g: (jnp.where(g == 0, pair, 1 - pair), (ring + 2) % 4))
+    for copy in every.started:
+        copy.wait_send()
+    for h in range(heads):
+        out_ref[:, h * HD:(h + 1) * HD] = total[h, :, 0:HD] / total[h, :, HD:2 * HD]
+
+
+def run_attention(x, wq, wk, wv, cid):
+    n = x.shape[0]
+    width = wq.shape[1]
     heads = width // HD
+    D = pltpu.SemaphoreType.DMA
+    many = copies_of(2, True)
+    bf, f32 = jnp.bfloat16, jnp.float32
     return pl.pallas_call(
         attention_kernel,
-        out_shape=jax.ShapeDtypeStruct((n, width), jnp.float32),
-        grid=(reach + 1,),
-        in_specs=[pl.BlockSpec((n, width), lambda j: (0, 0)),
-                  pl.BlockSpec((1, n, 2 * HD), lambda j: (jnp.maximum(lax.axis_index("seq") + j - reach, 0), 0, 0))],
-        out_specs=pl.BlockSpec((n, width), lambda j: (0, 0)),
-        scratch_shapes=[pltpu.VMEM((heads, n, HD), jnp.float32), pltpu.VMEM((heads, n, 2 * HD), jnp.float32)],
-        compiler_params=pltpu.CompilerParams(vmem_limit_bytes=32 << 20),
-        cost_estimate=pl.CostEstimate(flops=8 * n * width * WINDOW, bytes_accessed=8 << 20, transcendentals=0),
-    )(q, kv)
+        out_shape=jax.ShapeDtypeStruct((n, width), f32),
+        in_specs=[VM] * 4, out_specs=VM,
+        scratch_shapes=[pltpu.VMEM((n, 2 * HD), bf), pltpu.VMEM((16, n, 2 * HD), bf), pltpu.VMEM((heads, n, HD), bf),
+                        pltpu.VMEM((heads, n, HD), f32), pltpu.VMEM((heads, n, 2 * HD), f32), D, D((many,)), D((many,))],
+        compiler_params=pltpu.CompilerParams(collective_id=cid, has_side_effects=True, vmem_limit_bytes=40 << 20),
+    )(x, wq, wk, wv)
 
 
 def padded(vector):
@@ -571,11 +609,7 @@
     parts = run_out(y_normed, w_out_all)
     mixed = hidden_in.astype(f32) + mp_reduce(parts, 1)
     normed_two = run_norm(mixed.astype(bf), attn_gain[None, :], 2)
-    keys = jnp.dot(normed_two, w_k, preferred_element_type=f32).astype(bf)
-    values = jnp.dot(normed_two, w_v, preferred_element_type=f32).astype(bf)
-    kv = lax.all_gather(jnp.concatenate([keys, values], axis=1), "seq")
-    queries = jnp.dot(normed_two, w_q, preferred_element_type=f32).astype(bf)
-    return (mixed, run_attention(queries, kv))
+    return (mixed, run_attention(normed_two, w_q, w_k, w_v, 4))
 
 
 def solution(mesh):

time: 360 us -> 343 us (0.953)
  Pallas kernels: 254 us -> 289 us
  waiting for transfers between devices: 38.2 us -> 6.9 us
  local copies, waits for them, and re-layouts: 30.9 us -> 20.6 us
  matrix products: 15.6 us -> 6.81 us
    pallas_call x1, Pallas kernels: 21 us -> 56 us  [run_attention(): pl.pallas_call(attention_kernel, out_shape=jax.ShapeDtypeStruct((n, width...]
    all_gather x1 -> x0, waiting for transfers between devices: 31.3 us -> none  [on_device(): kv = lax.all_gather(jnp.concatenate([keys, values], axis=1), 'seq')]
    dot_general x3 -> x0, matrix products: 8.8 us -> none  [the longest x1 5.79 us: on_device(): queries = jnp.dot(normed_two, w_q, preferred_element_type=f32).astype(bf)]
    all_gather x1 -> x0, local copies, waits for them, and re-layouts: 6.4 us -> none  [on_device(): kv = lax.all_gather(jnp.concatenate([keys, values], axis=1), 'seq')]
    unnamed x63 -> x56, local copies, waits for them, and re-layouts: 24.3 us -> 20.4 us
  transfers between devices with their start and end apart: 4 -> 3, of which waited for: 2 -> 1; matrix products, arithmetic and copies ran while one was open for 4% -> 3% of each run, Pallas kernels for 39% -> 40%
where the time goes in v3:
time: 343 us
  Pallas kernels  289 us (84%)
  local copies, waits for them, and re-layouts  20.6 us (6%)
  between operations  14.4 us (4%)
  waiting for transfers between devices  6.9 us (2%)
  matrix products  6.81 us (2%)
    pallas_call x1, Pallas kernels, run_first(): pl.pallas_call(first_kernel, out_shape=(jax.ShapeDtypeStruct((n, 8 * w),...  96.5 us
    pallas_call x1, Pallas kernels, run_attention(): pl.pallas_call(attention_kernel, out_shape=jax.ShapeDtypeStruct((n, width...  56 us
    pallas_call x1, Pallas kernels, mp_reduce(): pl.pallas_call(reduce_kernel, out_shape=jax.ShapeDtypeStruct((n, w), jnp....  47.7 us
    pallas_call x1, Pallas kernels, run_norm(): pl.pallas_call(norm_kernel, out_shape=jax.ShapeDtypeStruct((n, 8 * w), x....  39.2 us
    pallas_call x1, Pallas kernels, run_gate(): pl.pallas_call(gate_kernel, out_shape=jax.ShapeDtypeStruct((n, width), jn...  34.1 us
    unnamed x56, local copies, waits for them, and re-layouts  20.4 us
    pallas_call x1, Pallas kernels, run_ssd(): pl.pallas_call(ssd_kernel, out_shape=(jax.ShapeDtypeStruct((n, width), f3...  7.84 us
    pallas_call x1, Pallas kernels, run_out(): pl.pallas_call(out_kernel, out_shape=jax.ShapeDtypeStruct((8, n, 2 * cols...  7.72 us
  transfers between devices with their start and end apart: 3, of which 1 were waited for; matrix products, arithmetic and copies ran while one was open for 3% of the time, Pallas kernels for 40%

profile of v3, /device:TPU:8, one launch (start us, length us, event | category | flops | bytes accessed | tf_op | source)
XLA Modules:
  0.0 342.7 jit_solution(13913262754816552346)
XLA Ops:
  9.5 0.9 fusion.1.wb_ref
  10.4 1.0 copy-done.3
  11.4 1.0 copy-done.7
  13.2 96.5 %shard_map.194 = (bf16[512,4096]{1,0:T(8,128)(2,1)S(1)}, bf16[4096,1024]{1,0:T(8,128)(2,1)}, bf16[4096,384]{1,0:T(8,128)(2,1)S(1)}) custom-call(bf16[512,512]{1,0:T(8,128)(2,1)S(1)} %copy-done.3, bf16[256,1024]{1,0:T(8,128)(2,1)S(1)} %copy-done.7, bf16[256,384]{1,0:T(8,128)(2,1)S(1)} %fusion.1.wb_ref, f32[1,4096]{1,0:T(1,128)S(1)} %bitcast.12), custom_call_target="tpu_custom_call" | custom-call | tf_op jit(solution)/shard_map/pallas_call | solution.py:183
  109.7 2.3 fusion.4.bcd_ref
  113.0 1.9 copy-done.26
  114.9 4.5 %fusion.3.xp_ref = f32[512,1024]{1,0:T(8,128)S(1)} fusion(bf16[512,4096]{1,0:T(8,128)(2,1)S(1)} %get-tuple-element.9.normed_ref, bf16[4096,1024]{1,0:T(8,128)(2,1)S(1)} %copy-done.26), kind=kOutput, calls=%fused_computation.9 | convolution fusion | flops 4294967296 | bytes 14680064 | tf_op jit(solution)/shard_map/dot_general | solution.py:601
  119.5 1.3 copy-done.15
  120.8 2.7 collective-permute-start
  123.7 5.5 %collective-permute-done = f32[8,1280]{1,0:T(8,128)S(1)} collective-permute-done((f32[8,1280]{1,0:T(8,128)S(1)}, f32[8,1280]{1,0:T(8,128)S(1)}, u32[]{:S(2)}, u32[]{:S(2)}) %collective-permute-start) | collective-permute-done | bytes 40992 | tf_op jit(solution)/shard_map/ppermute | solution.py:603
  129.2 1.6 copy-done.16
  130.8 1.1 copy-done.18
  132.0 7.8 %shard_map.195 = (f32[512,1024]{1,0:T(8,128)S(1)}, bf16[512,128]{1,0:T(8,128)(2,1)S(1)}, f32[512,128]{1,0:T(8,128)S(1)}, bf16[144,1024]{1,0:T(8,128)(2,1)S(1)}) custom-call(f32[512,1024]{1,0:T(8,128)S(1)} %copy-done.16, f32[512,384]{1,0:T(8,128)S(1)} %copy-done.18, f32[8,1024]{1,0:T(8,128)S(1)} %slice.18.rimx_ref, f32[8,256]{1,0:T(8,128)S(1)} %slice.19.rimbc_ref, ...), custom_call_target="tpu_custom_call" | custom-call | flops 4000000000 | bytes 8388608 | tf_op jit(solution)/shard_map/pallas_call | solution.py:376
  141.2 2.3 copy-done.1
  143.5 1.0 copy-done.9
  144.4 0.9 copy-done.11
  145.3 34.1 %shard_map.196.y_ref = bf16[512,1024]{1,0:T(8,128)(2,1)S(1)} custom-call(bf16[512,4096]{1,0:T(8,128)(2,1)S(1)} %copy-done.1, bf16[4096,1024]{1,0:T(8,128)(2,1)} %all-gather.4.cloned.1.call-done.wz_ref, bf16[144,1024]{1,0:T(8,128)(2,1)S(1)} %get-tuple-element.12.send_ref, f32[512,1024]{1,0:T(8,128)S(1)} %get-tuple-element.13.y_ref, ...), custom_call_target="tpu_custom_call" | custom-call | tf_op jit(solution)/shard_map/pallas_call | solution.py:457
  179.5 3.4 copy-done.19
  182.9 7.7 %shard_map.197.p_ref = bf16[8,512,512]{2,1,0:T(8,128)(2,1)S(1)} custom-call(bf16[512,1024]{1,0:T(8,128)(2,1)S(1)} %shard_map.196.y_ref, bf16[16,1024,256]{2,1,0:T(8,128)(2,1)S(1)} %bitcast.15), custom_call_target="tpu_custom_call" | custom-call | flops 4294967296 | bytes 16777216 | tf_op jit(solution)/shard_map/pallas_call | solution.py:474
  190.6 47.7 %shard_map.198 = f32[512,512]{1,0:T(8,128)S(1)} custom-call(bf16[8,512,512]{2,1,0:T(8,128)(2,1)S(1)} %shard_map.197.p_ref), custom_call_target="tpu_custom_call" | custom-call | tf_op jit(solution)/shard_map/pallas_call | solution.py:280
  238.4 1.2 fusion.2
  239.6 39.2 %shard_map.199.x_ref = bf16[512,4096]{1,0:T(8,128)(2,1)S(1)} custom-call(bf16[512,512]{1,0:T(8,128)(2,1)S(1)} %get-tuple-element.16.x_ref, f32[1,4096]{1,0:T(1,128)S(1)} %bitcast.13), custom_call_target="tpu_custom_call" | custom-call | tf_op jit(solution)/shard_map/pallas_call | solution.py:216
  278.8 56.0 %shard_map.200 = f32[512,512]{1,0:T(8,128)S(1)} custom-call(bf16[512,4096]{1,0:T(8,128)(2,1)S(1)} %shard_map.199.x_ref, bf16[4096,512]{1,0:T(8,128)(2,1)S(1)} %copy-done.2, bf16[4096,128]{1,0:T(8,128)(2,1)S(1)} %copy-done.5, bf16[4096,128]{1,0:T(8,128)(2,1)S(1)} %copy-done.6), custom_call_target="tpu_custom_call" | custom-call | tf_op jit(solution)/shard_map/pallas_call | solution.py:578
  334.9 1.0 copy.23
  (60 shorter events, 5.5 us)
Async XLA Ops:
  7.2 134.0 %all-gather.4.cloned.1.call-start = ((), (), s32[]{:S(2)}) async-start(), calls=%async_computation | async-start | bytes 8912896 | tf_op jit(solution)/shard_map/all_gather | solution.py:597
  7.9 171.6 %all-gather.6.cloned.1.call-start = ((), (), s32[]{:S(2)}) async-start(), calls=%async_computation.1 | async-start | bytes 8912896 | tf_op jit(solution)/shard_map/all_gather | solution.py:598
  10.4 1.0 copy-start.3
  11.4 1.0 copy-start.7
  109.7 3.2 copy-start
  109.7 5.2 %copy-start.26 = (bf16[4096,1024]{1,0:T(8,128)(2,1)S(1)}, bf16[4096,1024]{1,0:T(8,128)(2,1)}, u32[]{:S(2)}) copy-start(bf16[4096,1024]{1,0:T(8,128)(2,1)} %get-tuple-element.10) | copy-start | bytes 25165828
  114.9 8.6 %copy-start.21 = (f32[4,128]{1,0:T(4,128)S(1)}, f32[4,128]{1,0:T(4,128)}, u32[]{:S(2)}) copy-start(f32[4,128]{1,0:T(4,128)} %param.28) | copy-start | bytes 6148
  114.9 8.6 %copy-start.22 = (f32[4,128]{1,0:T(4,128)S(1)}, f32[4,128]{1,0:T(4,128)}, u32[]{:S(2)}) copy-start(f32[4,128]{1,0:T(4,128)} %param.27) | copy-start | bytes 6148
  114.9 8.6 %copy-start.24 = (f32[16]{0:T(128)S(1)}, f32[16]{0:T(128)}, u32[]{:S(2)}) copy-start(f32[16]{0:T(128)} %param.30) | copy-start | bytes 196
  114.9 8.6 %copy-start.25 = (f32[16]{0:T(128)S(1)}, f32[16]{0:T(128)}, u32[]{:S(2)}) copy-start(f32[16]{0:T(128)} %param.29) | copy-start | bytes 196
  114.9 8.6 %copy-start.23 = (f32[16]{0:T(128)S(1)}, f32[16]{0:T(128)}, u32[]{:S(2)}) copy-start(f32[16]{0:T(128)} %param.31) | copy-start | bytes 196
  114.9 14.3 %copy-start.20 = (f32[4,1024]{1,0:T(4,128)S(1)}, f32[4,1024]{1,0:T(4,128)}, u32[]{:S(2)}) copy-start(f32[4,1024]{1,0:T(4,128)} %cx_ref.1) | copy-start | bytes 49156
  119.4 1.4 copy-start.15
  120.8 8.4 %collective-permute-start = (f32[8,1280]{1,0:T(8,128)S(1)}, f32[8,1280]{1,0:T(8,128)S(1)}, u32[]{:S(2)}, u32[]{:S(2)}) collective-permute-start(f32[8,1280]{1,0:T(8,128)S(1)} %pad_maximum_fusion), channel_id=1, source_target_pairs={{0,8},{8,16},{16,24},{24,32},{32,40},{40,48},{48,56},{56,64},{64,7... | collective-permute-start | bytes 122888 | tf_op jit(solution)/shard_map/ppermute | solution.py:603
  129.2 1.6 copy-start.16
  130.8 1.1 copy-start.18
  132.0 9.2 %copy-start.14 = (f32[1024]{0:T(1024)S(1)}, f32[1024]{0:T(1024)}, u32[]{:S(2)}) copy-start(f32[1024]{0:T(1024)} %param.32) | copy-start | bytes 12292
  141.2 2.3 copy-start.1
  179.5 3.4 copy-start.19
  190.6 47.8 %copy-start.4 = (bf16[512,512]{1,0:T(8,128)(2,1)S(1)}, bf16[512,512]{1,0:T(8,128)(2,1)}, u32[]{:S(2)}) copy-start(bf16[512,512]{1,0:T(8,128)(2,1)} %x_ref.1) | copy-start | bytes 1572868
  190.6 49.0 %copy-start.13 = (f32[4096]{0:T(1024)S(1)}, f32[4096]{0:T(1024)}, u32[]{:S(2)}) copy-start(f32[4096]{0:T(1024)} %param.34) | copy-start | bytes 49156
  238.4 40.4 %copy-start.2 = (bf16[4096,512]{1,0:T(8,128)(2,1)S(1)}, bf16[4096,512]{1,0:T(8,128)(2,1)}, u32[]{:S(2)}) copy-start(bf16[4096,512]{1,0:T(8,128)(2,1)} %wq_ref.1) | copy-start | bytes 12582916
  238.4 40.4 %copy-start.5 = (bf16[4096,128]{1,0:T(8,128)(2,1)S(1)}, bf16[4096,128]{1,0:T(8,128)(2,1)}, u32[]{:S(2)}) copy-start(bf16[4096,128]{1,0:T(8,128)(2,1)} %wk_ref.1) | copy-start | bytes 3145732
  238.4 40.4 %copy-start.6 = (bf16[4096,128]{1,0:T(8,128)(2,1)S(1)}, bf16[4096,128]{1,0:T(8,128)(2,1)}, u32[]{:S(2)}) copy-start(bf16[4096,128]{1,0:T(8,128)(2,1)} %wv_ref.1) | copy-start | bytes 3145732
  (6 other events, 4.8 us)
Sparse Core Ops, SparseCore 0:
  9.7 93.7 all-gather.3
  105.1 57.3 all-gather.5

commit v4 on v3

--- a/solution.py
+++ b/solution.py
@@ -116,11 +116,11 @@
     return [pl.ds(k * (total // count), total // count) for k in range(count)]
 
 
-def write_normed(whole, gain_ref, normed_ref):
-    blocks, n, wide = whole.shape
+def write_normed(whole, gain_ref, normed_ref, start, count):
+    blocks, _, wide = whole.shape
 
     def norm(c, _):
-        piece = rows(pl.multiple_of(c * 32, 32), 32)
+        piece = rows(pl.multiple_of(start + c * 32, 32), 32)
         square = jnp.zeros((32, wide), jnp.float32)
         for b in range(blocks):
             value = whole[b, piece, :].astype(jnp.float32)
@@ -131,7 +131,7 @@
             normed_ref[piece, lanes] = (whole[b, piece, :].astype(jnp.float32) * scale * gain_ref[:, lanes]).astype(normed_ref.dtype)
         return 0
 
-    lax.fori_loop(0, n // 32, norm, 0)
+    lax.fori_loop(0, count // 32, norm, 0)
 
 
 def first_kernel(x_ref, wx_ref, wb_ref, gain_ref, normed_ref, wxa_ref, wba_ref, whole, local, ms, mr, bs, br, xs, xr):
@@ -165,7 +165,7 @@
                 g.forward(which, k)
     hidden.last()
     mine[0].wait()
-    write_normed(whole, gain_ref, normed_ref)
+    write_normed(whole, gain_ref, normed_ref, 0, whole.shape[1])
     small.last()
     big.last()
     for g in everything:
@@ -190,102 +190,144 @@
     )(x, wx, wb, gain)
 
 
-def norm_kernel(x_ref, gain_ref, normed_ref, whole, local, ms, mr):
-    pair, ring = mp_place()
-    greet(neighbours(mp_names, pair, ring, 0, False))
-    hidden = Gather(lambda pair, ring, core, piece: whole.at[pair * 4 + ring, piece], lambda piece: x_ref.at[piece], mp_names,
-                    pair, ring, 0, ms, mr, 0, cut(x_ref.shape[0], 4), False)
-    mine = pltpu.make_async_copy(x_ref, whole.at[pair * 4 + ring], local)
-    hidden.begin()
-    mine.start()
-    for k in range(4):
-        hidden.second(k)
-    for which in range(2):
-        for k in range(4):
-            hidden.forward(which, k)
-    hidden.last()
-    hidden.finish()
-    mine.wait()
-    write_normed(whole, gain_ref, normed_ref)
-
-
-def run_norm(x, gain, cid):
-    n, w = x.shape
-    D = pltpu.SemaphoreType.DMA
-    few = copies_of(4, False)
-    return pl.pallas_call(
-        norm_kernel,
-        out_shape=jax.ShapeDtypeStruct((n, 8 * w), x.dtype),
-        in_specs=[VM, VM], out_specs=VM,
-        scratch_shapes=[pltpu.VMEM((8, n, w), x.dtype), D, D((few,)), D((few,))],
-        compiler_params=pltpu.CompilerParams(collective_id=cid, has_side_effects=True, vmem_limit_bytes=24 << 20),
-    )(x, gain)
-
-
-def reduce_kernel(p_ref, out_ref, tmp, d1, d2, ysrc, ydst, s1, r1, s2, r2, sy, ry, sraw, rraw):
+def mix_kernel(y_ref, w_hbm, hidden_ref, gain_ref, mixed_ref, normed_ref, w, p, tmp, d1, d2, ysrc, ydst, whole, wsem,
+               s1, r1, s2, r2, sraw, rraw, sy, ry, gs, gr):
     high, low = mp_place()
-    right, left = (low + 1) % 4, (low + 3) % 4
-    far = (low + 2) % 4
-    partner = (1 - high) * 4 + low
-    greet(neighbours(mp_names, high, low, 0, False))
-    n = p_ref.shape[1]
-    half = n // 2
+    right, left, far = (low + 1) % 4, (low + 3) % 4, (low + 2) % 4
+    me = high * 4 + low
     order = (1 - high, high)
     sides = ((right, left), (left, right))
-
-    def send(src, dst, target, ssem, rsem):
+    n = y_ref.shape[0]
+    half, quarter = n // 2, n // 4
+    f32 = jnp.float32
+    blocks = [pair * 4 + ring for ring in (far, right, left, low) for pair in order]
+    loads = [pltpu.make_async_copy(w_hbm.at[pl.ds(2 * b, 2)], w.at[pl.ds(2 * b, 2)], wsem.at[i]) for i, b in enumerate(blocks)]
+    for load in loads:
+        load.start()
+    greet(neighbours(mp_names, high, low, 0, False))
+
+    def send(src, dst, pair, ring, ssem, rsem):
         copy = pltpu.make_async_remote_copy(src_ref=src, dst_ref=dst, send_sem=ssem, recv_sem=rsem,
-                                            device_id={"mp": target}, device_id_type=MESH)
+                                            device_id=mp_names(pair, ring, 0), device_id_type=MESH)
         copy.start()
+        sent.append(copy)
         return copy
 
-    first = [[send(p_ref.at[order[k] * 4 + far, rows(d * half, half)], d1.at[k, d], high * 4 + sides[d][0],
-                   s1.at[k, d], r1.at[k, d]) for d in range(2)] for k in range(2)]
-    raw = [[send(p_ref.at[order[k] * 4 + sides[d][0], rows((1 - d) * half, half)],
-                 d2.at[k, d, rows((1 - d) * half, half)], high * 4 + sides[d][0],
-                 sraw.at[k, d], rraw.at[k, d]) for d in range(2)] for k in range(2)]
-    second = []
+    def product(h, b):
+        here = slice(h * half, (h + 1) * half)
+        cols = w.shape[2]
+        for c in range(2):
+            p[b, here, c * cols:(c + 1) * cols] = jnp.dot(
+                y_ref[here, :], w[2 * b + c], preferred_element_type=f32).astype(p.dtype)
+
+    def start_first(h, k):
+        return [send(p.at[order[k] * 4 + far, rows(h * half + d * quarter, quarter)], d1.at[h, k, d], high, sides[d][0],
+                     s1.at[h, k, d], r1.at[h, k, d]) for d in range(2)]
+
+    def start_raw(h, k, d):
+        return send(p.at[order[k] * 4 + sides[d][0], rows(h * half + (1 - d) * quarter, quarter)],
+                    d2.at[h, k, d, rows((1 - d) * quarter, quarter)], high, sides[d][0], sraw.at[h, k, d], rraw.at[h, k, d])
+
+    def pass_on(h, k):
+        result = []
+        for d in range(2):
+            first[h][k][d].wait_recv()
+            here = slice(h * half + d * quarter, h * half + (d + 1) * quarter)
+            tmp[h, k, d] = (d1[h, k, d].astype(f32) + p[order[k] * 4 + sides[d][0], here, :].astype(f32)).astype(tmp.dtype)
+            result.append(send(tmp.at[h, k, d], d2.at[h, k, d, rows(d * quarter, quarter)], high, sides[d][0],
+                               s2.at[h, k, d], r2.at[h, k, d]))
+        second[h][k] = result
+
+    def total(h, k):
+        for d in range(2):
+            raw[h][k][d].wait_recv()
+            second[h][k][d].wait_recv()
+        here = slice(h * half, (h + 1) * half)
+        return p[order[k] * 4 + low, here, :].astype(f32) + d2[h, k, 0].astype(f32) + d2[h, k, 1].astype(f32)
+
+    def give(h):
+        ysrc[h] = total(h, 0).astype(ysrc.dtype)
+        across[h] = send(ysrc.at[h], ydst.at[h], 1 - high, low, sy.at[h], ry.at[h])
+
+    def close(h):
+        here = slice(h * half, (h + 1) * half)
+        own = total(h, 1)
+        across[h].wait_recv()
+        result = hidden_ref[here, :].astype(f32) + (own + ydst[h].astype(f32))
+        mixed_ref[here, :] = result
+        whole[me, here, :] = result.astype(whole.dtype)
+        gathers[h].begin()
+
+    sent = []
+    first, raw, second = [[None, None] for _ in range(2)], [[None, None] for _ in range(2)], [[None, None] for _ in range(2)]
+    across = [None, None]
+
+    def view(pair, ring, core, piece):
+        return whole.at[pair * 4 + ring, piece]
+
+    gathers = [Gather(view, lambda piece: whole.at[me, piece], mp_names, high, low, 0, gs, gr, h * copies_of(2, False),
+                      [pl.ds(h * half, quarter), pl.ds(h * half + quarter, quarter)], False) for h in range(2)]
+    for h in range(2):
+        raw[h] = [[None, None], [None, None]]
+        for i, b in enumerate(blocks):
+            if h == 0:
+                loads[i].wait()
+            product(h, b)
+            if h == 0 and i < 2:
+                first[0][i] = start_first(0, i)
+            if h == 0 and 2 <= i < 6:
+                raw[0][i % 2][i // 2 - 1] = start_raw(0, i % 2, i // 2 - 1)
+    pass_on(0, 0)
+    pass_on(0, 1)
+    for k in range(2):
+        first[1][k] = start_first(1, k)
     for k in range(2):
         for d in range(2):
-            first[k][d].wait_recv()
-            tmp[k, d] = (d1[k, d].astype(jnp.float32)
-                         + p_ref[order[k] * 4 + sides[d][0], d * half:(d + 1) * half].astype(jnp.float32)).astype(tmp.dtype)
-            second.append(send(tmp.at[k, d], d2.at[k, d, rows(d * half, half)], high * 4 + sides[d][0],
-                               s2.at[k, d], r2.at[k, d]))
-    totals = None
-    for k in range(2):
-        for d in range(2):
-            raw[k][d].wait_recv()
-            second[k * 2 + d].wait_recv()
-        total = (p_ref[order[k] * 4 + low].astype(jnp.float32) + d2[k, 0].astype(jnp.float32)
-                 + d2[k, 1].astype(jnp.float32))
-        if k == 0:
-            ysrc[...] = total.astype(ysrc.dtype)
-            ycopy = send(ysrc, ydst, partner, sy, ry)
-        else:
-            ycopy.wait_recv()
-            out_ref[...] = total + ydst[...].astype(jnp.float32)
-    ycopy.wait_send()
-    for k in range(2):
-        for d in range(2):
-            first[k][d].wait_send()
-            raw[k][d].wait_send()
-            second[k * 2 + d].wait_send()
-
-
-def mp_reduce(p, cid):
-    _, n, w = p.shape
+            raw[1][k][d] = start_raw(1, k, d)
+    give(0)
+    pass_on(1, 0)
+    pass_on(1, 1)
+    close(0)
+    give(1)
+    early, late = gathers
+    early.second(0)
+    early.second(1)
+    early.forward(0, 0)
+    early.forward(0, 1)
+    close(1)
+    early.forward(1, 0)
+    early.forward(1, 1)
+    late.second(0)
+    late.second(1)
+    late.forward(0, 0)
+    late.forward(0, 1)
+    early.last()
+    late.forward(1, 0)
+    late.forward(1, 1)
+    write_normed(whole, gain_ref, normed_ref, 0, half)
+    late.last()
+    write_normed(whole, gain_ref, normed_ref, half, half)
+    early.finish()
+    late.finish()
+    for copy in sent:
+        copy.wait_send()
+
+
+def run_mix(y, w, hidden, gain, cid):
+    n, width = hidden.shape
     D = pltpu.SemaphoreType.DMA
-    half = n // 2
+    bf = jnp.bfloat16
+    V = pltpu.VMEM
+    few = 2 * copies_of(2, False)
     return pl.pallas_call(
-        reduce_kernel,
-        out_shape=jax.ShapeDtypeStruct((n, w), jnp.float32),
-        in_specs=[VM], out_specs=VM,
-        scratch_shapes=[pltpu.VMEM((2, 2, half, w), p.dtype), pltpu.VMEM((2, 2, half, w), p.dtype),
-                        pltpu.VMEM((2, 2, n, w), p.dtype), pltpu.VMEM((n, w), p.dtype), pltpu.VMEM((n, w), p.dtype),
-                        D((2, 2)), D((2, 2)), D((2, 2)), D((2, 2)), D, D, D((2, 2)), D((2, 2))],
-        compiler_params=pltpu.CompilerParams(collective_id=cid, has_side_effects=True, vmem_limit_bytes=32 << 20),
-    )(p)
+        mix_kernel,
+        out_shape=(jax.ShapeDtypeStruct((n, width), jnp.float32), jax.ShapeDtypeStruct((n, 8 * width), bf)),
+        in_specs=[VM, pl.BlockSpec(memory_space=pl.ANY), VM, VM], out_specs=(VM, VM),
+        scratch_shapes=[V(w.shape, bf), V((8, n, width), bf), V((2, 2, 2, n // 4, width), bf), V((2, 2, 2, n // 4, width), bf),
+                        V((2, 2, 2, n // 2, width), bf), V((2, n // 2, width), bf), V((2, n // 2, width), bf), V((8, n, width), bf),
+                        D((8,))] + [D((2, 2, 2))] * 6 + [D((2,))] * 2 + [D((few,))] * 2,
+        compiler_params=pltpu.CompilerParams(collective_id=cid, has_side_effects=True, vmem_limit_bytes=48 << 20),
+    )(y, w, hidden, gain)
 
 
 def ssd_kernel(xp_ref, bcd_ref, rimx_ref, rimbc_ref, cx_ref, cbc_ref, bias_ref, rate_ref, skip_ref,
@@ -464,24 +506,6 @@
     )(normed, wz, send, y, cc, cum, gain)
 
 
-def out_kernel(y_ref, w_ref, out_ref):
-    out_ref[0] = jnp.dot(y_ref[...], w_ref[0], preferred_element_type=jnp.float32).astype(out_ref.dtype)
-
-
-def run_out(y, w):
-    n, width = y.shape
-    cols = w.shape[2]
-    return pl.pallas_call(
-        out_kernel,
-        out_shape=jax.ShapeDtypeStruct((8, n, 2 * cols), jnp.bfloat16),
-        grid=(w.shape[0],),
-        in_specs=[pl.BlockSpec((n, width), lambda j: (0, 0)), pl.BlockSpec((1, width, cols), lambda j: (j, 0, 0))],
-        out_specs=pl.BlockSpec((1, n, cols), lambda j: (j // 2, 0, j % 2)),
-        compiler_params=pltpu.CompilerParams(vmem_limit_bytes=16 << 20),
-        cost_estimate=pl.CostEstimate(flops=2 * n * width * 4096, bytes_accessed=16 << 20, transcendentals=0),
-    )(y, w)
-
-
 def attention_kernel(x_ref, wq_ref, wk_ref, wv_ref, out_ref, own, kv, q, peak, total, local, ss, sr):
     place = lax.axis_index("seq")
     pair, ring, core = seq_place()
@@ -606,9 +630,7 @@
         xp, bcd, rims[:, 0:width], rims[:, width:], conv_x, jnp.concatenate([conv_b, conv_c], axis=1),
         padded(dt_bias), padded(a_rate), jnp.repeat(skip_gain, P_SIZE)[None, :])
     y_normed = run_gate(normed, w_z_all, send, y, cc, cum, group_gain[None, :], 3)
-    parts = run_out(y_normed, w_out_all)
-    mixed = hidden_in.astype(f32) + mp_reduce(parts, 1)
-    normed_two = run_norm(mixed.astype(bf), attn_gain[None, :], 2)
+    mixed, normed_two = run_mix(y_normed, w_out_all, hidden_in, attn_gain[None, :], 1)
     return (mixed, run_attention(normed_two, w_q, w_k, w_v, 4))
 
 

time: 343 us -> 327 us (0.953)
  Pallas kernels: 289 us -> 274 us
    pallas_call x3 -> x1, Pallas kernels: 94.6 us -> 77.6 us  [run_mix(): pl.pallas_call(mix_kernel, out_shape=(jax.ShapeDtypeStruct((n, width), jn...]
    unnamed x56 -> x53, local copies, waits for them, and re-layouts: 20.4 us -> 19.8 us
  transfers between devices with their start and end apart: 3 -> 3, of which waited for: 1 -> 1; matrix products, arithmetic and copies ran while one was open for 3% -> 3% of each run, Pallas kernels for 40% -> 43%
where the time goes in v4:
time: 327 us; the launch traced here: 326 us
  Pallas kernels  274 us (84%)
  local copies, waits for them, and re-layouts  19.9 us (6%)
  between operations  14.3 us (4%)
  waiting for transfers between devices  7.09 us (2%)
  matrix products  6.89 us (2%)
    pallas_call x1, Pallas kernels, run_first(): pl.pallas_call(first_kernel, out_shape=(jax.ShapeDtypeStruct((n, 8 * w),...  96.5 us
    pallas_call x1, Pallas kernels, run_mix(): pl.pallas_call(mix_kernel, out_shape=(jax.ShapeDtypeStruct((n, width), jn...  77.6 us
    pallas_call x1, Pallas kernels, run_attention(): pl.pallas_call(attention_kernel, out_shape=jax.ShapeDtypeStruct((n, width...  57.3 us
    pallas_call x1, Pallas kernels, run_gate(): pl.pallas_call(gate_kernel, out_shape=jax.ShapeDtypeStruct((n, width), jn...  34.9 us
    unnamed x53, local copies, waits for them, and re-layouts  19.8 us
    pallas_call x1, Pallas kernels, run_ssd(): pl.pallas_call(ssd_kernel, out_shape=(jax.ShapeDtypeStruct((n, width), f3...  7.85 us
  transfers between devices with their start and end apart: 3, of which 1 were waited for; matrix products, arithmetic and copies ran while one was open for 3% of the time, Pallas kernels for 43%

profile of v4, /device:TPU:8, one launch (start us, length us, event | category | flops | bytes accessed | tf_op | source)
XLA Modules:
  0.0 325.9 jit_solution(7540809841991300677)
XLA Ops:
  8.6 0.8 copy.21
  9.5 0.9 fusion.1.wb_ref
  10.4 1.0 copy-done.4
  11.4 1.0 copy-done.8
  12.5 0.7 copy-done.13
  13.2 96.5 %shard_map.194 = (bf16[512,4096]{1,0:T(8,128)(2,1)S(1)}, bf16[4096,1024]{1,0:T(8,128)(2,1)}, bf16[4096,384]{1,0:T(8,128)(2,1)S(1)}) custom-call(bf16[512,512]{1,0:T(8,128)(2,1)S(1)} %copy-done.4, bf16[256,1024]{1,0:T(8,128)(2,1)S(1)} %copy-done.8, bf16[256,384]{1,0:T(8,128)(2,1)S(1)} %fusion.1.wb_ref, f32[1,4096]{1,0:T(1,128)S(1)} %bitcast.12), custom_call_target="tpu_custom_call" | custom-call | tf_op jit(solution)/shard_map/pallas_call | solution.py:183
  109.7 2.3 fusion.3.bcd_ref
  112.1 2.5 copy-done.24
  114.7 4.6 %fusion.2.xp_ref = f32[512,1024]{1,0:T(8,128)S(1)} fusion(bf16[512,4096]{1,0:T(8,128)(2,1)S(1)} %get-tuple-element.11.normed_ref, bf16[4096,1024]{1,0:T(8,128)(2,1)S(1)} %copy-done.24), kind=kOutput, calls=%fused_computation.7 | convolution fusion | flops 4294967296 | bytes 14680064 | tf_op jit(solution)/shard_map/dot_general | solution.py:625
  119.3 1.3 copy-done.16
  120.6 2.5 collective-permute-start
  123.3 5.7 %collective-permute-done = f32[8,1280]{1,0:T(8,128)S(1)} collective-permute-done((f32[8,1280]{1,0:T(8,128)S(1)}, f32[8,1280]{1,0:T(8,128)S(1)}, u32[]{:S(2)}, u32[]{:S(2)}) %collective-permute-start) | collective-permute-done | bytes 40992 | tf_op jit(solution)/shard_map/ppermute | solution.py:627
  129.0 1.6 copy-done.17
  130.6 7.9 %shard_map.195 = (f32[512,1024]{1,0:T(8,128)S(1)}, bf16[512,128]{1,0:T(8,128)(2,1)S(1)}, f32[512,128]{1,0:T(8,128)S(1)}, bf16[144,1024]{1,0:T(8,128)(2,1)S(1)}) custom-call(f32[512,1024]{1,0:T(8,128)S(1)} %copy-done.17, f32[512,384]{1,0:T(8,128)S(1)} %fusion.3.bcd_ref, f32[8,1024]{1,0:T(8,128)S(1)} %slice.18.rimx_ref, f32[8,256]{1,0:T(8,128)S(1)} %slice.19.rimbc_ref, ...), custom_call_target="tpu_custom_call" | custom-call | flops 4000000000 | bytes 8388608 | tf_op jit(solution)/shard_map/pallas_call | solution.py:418
  139.9 2.3 copy-done.1
  142.1 0.9 copy-done.10
  143.1 0.9 copy-done.12
  144.0 34.9 %shard_map.196.y_ref = bf16[512,1024]{1,0:T(8,128)(2,1)S(1)} custom-call(bf16[512,4096]{1,0:T(8,128)(2,1)S(1)} %copy-done.1, bf16[4096,1024]{1,0:T(8,128)(2,1)} %all-gather.4.cloned.1.call-done.wz_ref, bf16[144,1024]{1,0:T(8,128)(2,1)S(1)} %get-tuple-element.14.send_ref, f32[512,1024]{1,0:T(8,128)S(1)} %get-tuple-element.15.y_ref, ...), custom_call_target="tpu_custom_call" | custom-call | tf_op jit(solution)/shard_map/pallas_call | solution.py:499
  179.0 1.0 copy-done.5
  180.0 77.6 %shard_map.197 = (f32[512,512]{1,0:T(8,128)S(1)}, bf16[512,4096]{1,0:T(8,128)(2,1)}) custom-call(bf16[512,1024]{1,0:T(8,128)(2,1)S(1)} %shard_map.196.y_ref, bf16[16,1024,256]{2,1,0:T(8,128)(2,1)} %bitcast.15, bf16[512,512]{1,0:T(8,128)(2,1)S(1)} %copy-done.5, f32[1,4096]{1,0:T(1,128)S(1)} %bitcast.13), custom_call_target="tpu_custom_call" | custom-call | tf_op jit(solution)/shard_map/pallas_call | solution.py:322
  257.7 2.2 copy-done.3
  259.9 57.3 %shard_map.198 = f32[512,512]{1,0:T(8,128)S(1)} custom-call(bf16[512,4096]{1,0:T(8,128)(2,1)S(1)} %copy-done.3, bf16[4096,512]{1,0:T(8,128)(2,1)S(1)} %copy-done.2, bf16[4096,128]{1,0:T(8,128)(2,1)S(1)} %copy-done.6, bf16[4096,128]{1,0:T(8,128)(2,1)S(1)} %copy-done.7), custom_call_target="tpu_custom_call" | custom-call | tf_op jit(solution)/shard_map/pallas_call | solution.py:602
  317.2 1.0 copy.24
  318.1 1.0 copy.25
  (54 shorter events, 3.1 us)
Async XLA Ops:
  7.2 132.7 %all-gather.4.cloned.1.call-start = ((), (), s32[]{:S(2)}) async-start(), calls=%async_computation | async-start | bytes 8912896 | tf_op jit(solution)/shard_map/all_gather | solution.py:621
  7.9 171.0 %all-gather.6.cloned.1.call-start = ((), (), s32[]{:S(2)}) async-start(), calls=%async_computation.1 | async-start | bytes 8912896 | tf_op jit(solution)/shard_map/all_gather | solution.py:622
  10.4 1.0 copy-start.4
  11.4 1.0 copy-start.8
  109.7 2.4 copy-start
  109.7 4.9 %copy-start.24 = (bf16[4096,1024]{1,0:T(8,128)(2,1)S(1)}, bf16[4096,1024]{1,0:T(8,128)(2,1)}, u32[]{:S(2)}) copy-start(bf16[4096,1024]{1,0:T(8,128)(2,1)} %get-tuple-element.12) | copy-start | bytes 25165828
  114.6 8.5 %copy-start.19 = (f32[4,128]{1,0:T(4,128)S(1)}, f32[4,128]{1,0:T(4,128)}, u32[]{:S(2)}) copy-start(f32[4,128]{1,0:T(4,128)} %param.28) | copy-start | bytes 6148
  114.6 8.5 %copy-start.20 = (f32[4,128]{1,0:T(4,128)S(1)}, f32[4,128]{1,0:T(4,128)}, u32[]{:S(2)}) copy-start(f32[4,128]{1,0:T(4,128)} %param.27) | copy-start | bytes 6148
  114.6 8.5 %copy-start.22 = (f32[16]{0:T(128)S(1)}, f32[16]{0:T(128)}, u32[]{:S(2)}) copy-start(f32[16]{0:T(128)} %param.30) | copy-start | bytes 196
  114.6 8.5 %copy-start.23 = (f32[16]{0:T(128)S(1)}, f32[16]{0:T(128)}, u32[]{:S(2)}) copy-start(f32[16]{0:T(128)} %param.29) | copy-start | bytes 196
  114.6 8.5 %copy-start.21 = (f32[16]{0:T(128)S(1)}, f32[16]{0:T(128)}, u32[]{:S(2)}) copy-start(f32[16]{0:T(128)} %param.31) | copy-start | bytes 196
  114.6 14.4 %copy-start.18 = (f32[4,1024]{1,0:T(4,128)S(1)}, f32[4,1024]{1,0:T(4,128)}, u32[]{:S(2)}) copy-start(f32[4,1024]{1,0:T(4,128)} %cx_ref.1) | copy-start | bytes 49156
  119.2 1.3 copy-start.16
  120.6 8.4 %collective-permute-start = (f32[8,1280]{1,0:T(8,128)S(1)}, f32[8,1280]{1,0:T(8,128)S(1)}, u32[]{:S(2)}, u32[]{:S(2)}) collective-permute-start(f32[8,1280]{1,0:T(8,128)S(1)} %pad_maximum_fusion), channel_id=1, source_target_pairs={{0,8},{8,16},{16,24},{24,32},{32,40},{40,48},{48,56},{56,64},{64,7... | collective-permute-start | bytes 122888 | tf_op jit(solution)/shard_map/ppermute | solution.py:627
  129.0 1.6 copy-start.17
  130.6 9.2 %copy-start.15 = (f32[1024]{0:T(1024)S(1)}, f32[1024]{0:T(1024)}, u32[]{:S(2)}) copy-start(f32[1024]{0:T(1024)} %param.32) | copy-start | bytes 12292
  139.9 2.3 copy-start.1
  142.1 1.0 copy-start.10
  144.0 35.0 %copy-start.14 = (f32[4096]{0:T(1024)S(1)}, f32[4096]{0:T(1024)}, u32[]{:S(2)}) copy-start(f32[4096]{0:T(1024)} %param.34) | copy-start | bytes 49156
  179.0 1.0 copy-start.5
  180.0 77.6 %copy-start.2 = (bf16[4096,512]{1,0:T(8,128)(2,1)S(1)}, bf16[4096,512]{1,0:T(8,128)(2,1)}, u32[]{:S(2)}) copy-start(bf16[4096,512]{1,0:T(8,128)(2,1)} %wq_ref.1) | copy-start | bytes 12582916
  180.0 77.6 %copy-start.6 = (bf16[4096,128]{1,0:T(8,128)(2,1)S(1)}, bf16[4096,128]{1,0:T(8,128)(2,1)}, u32[]{:S(2)}) copy-start(bf16[4096,128]{1,0:T(8,128)(2,1)} %wk_ref.1) | copy-start | bytes 3145732
  180.0 77.6 %copy-start.7 = (bf16[4096,128]{1,0:T(8,128)(2,1)S(1)}, bf16[4096,128]{1,0:T(8,128)(2,1)}, u32[]{:S(2)}) copy-start(bf16[4096,128]{1,0:T(8,128)(2,1)} %wv_ref.1) | copy-start | bytes 3145732
  257.7 2.2 copy-start.3
  (4 other events, 3.0 us)
Sparse Core Ops, SparseCore 0:
  9.7 93.7 all-gather.3
  105.1 58.8 all-gather.5

commit v5 on v4

--- a/solution.py
+++ b/solution.py
@@ -116,12 +116,12 @@
     return [pl.ds(k * (total // count), total // count) for k in range(count)]
 
 
-def write_normed(whole, gain_ref, normed_ref, start, count):
+def write_normed(whole, gain_ref, normed_ref, start, count, size):
     blocks, _, wide = whole.shape
 
     def norm(c, _):
-        piece = rows(pl.multiple_of(start + c * 32, 32), 32)
-        square = jnp.zeros((32, wide), jnp.float32)
+        piece = rows(pl.multiple_of(start + c * size, 16), size)
+        square = jnp.zeros((size, wide), jnp.float32)
         for b in range(blocks):
             value = whole[b, piece, :].astype(jnp.float32)
             square = square + value * value
@@ -131,63 +131,337 @@
             normed_ref[piece, lanes] = (whole[b, piece, :].astype(jnp.float32) * scale * gain_ref[:, lanes]).astype(normed_ref.dtype)
         return 0
 
-    lax.fori_loop(0, count // 32, norm, 0)
-
-
-def first_kernel(x_ref, wx_ref, wb_ref, gain_ref, normed_ref, wxa_ref, wba_ref, whole, local, ms, mr, bs, br, xs, xr):
+    lax.fori_loop(0, count // size, norm, 0)
+
+
+class RingFirst(Gather):
+    def begin(self):
+        me = (self.pair, self.ring, self.core)
+        self.pairs_open = []
+        for k, piece in enumerate(self.pieces):
+            src = self.own(piece)
+            self.a[k] = [self.send(src, me, piece, self.pair, to, self.core) for to in (self.right, self.left)]
+            self.pairs_open.append((self.send(src, me, piece, 1 - self.pair, self.ring, self.core), self.ring, piece))
+            self.over(src, me, piece)
+
+    def beside(self, src, block, piece):
+        self.pairs_open.append((self.send(src, block, piece, 1 - self.pair, self.ring, self.core), block[1], piece))
+        self.over(src, block, piece)
+
+    def forward(self, k):
+        piece, first = self.pieces[k], k < len(self.pieces) // 2
+        for d, (to, origin) in enumerate(((self.right, self.left), (self.left, self.right))):
+            self.a[k][d].wait_recv()
+            block = (self.pair, origin, self.core)
+            src = self.view(*block, piece)
+            if first == (d == 0):
+                self.f.append((self.send(src, block, piece, self.pair, to, self.core), (self.pair, self.far, self.core), piece))
+            self.beside(src, block, piece)
+
+    def last(self):
+        for copy, block, piece in self.f:
+            copy.wait_recv()
+            self.beside(self.view(*block, piece), block, piece)
+
+    def pairs(self):
+        for copy, ring, piece in self.pairs_open:
+            copy.wait_recv()
+            block = (1 - self.pair, ring, self.core)
+            self.over(self.view(*block, piece), block, piece)
+
+
+def three_terms(decay):
+    bf, f32 = jnp.bfloat16, jnp.float32
+    big = decay.astype(bf).astype(f32)
+    middle = (decay - big).astype(bf).astype(f32)
+    small = (decay - big - middle).astype(bf).astype(f32)
+    which = lax.broadcasted_iota(jnp.int32, decay.shape, 0)
+    return jnp.where(which == 0, big, jnp.where(which == 1, middle, small)).astype(bf)
+
+
+def decay_of(block):
+    tail = block.astype(jnp.float32)
+    return tail[0:1] + (tail[1:2] + tail[2:3])
+
+
+def mixer_kernel(x_ref, wx_ref, wb_ref, wz_ref, wo_ref, norm_ref, cx_ref, cbc_ref, bias_ref, rate_ref, skip_ref, gain_ref,
+                 out_ref, woa, whole, normed, wxa, wba, wza, padx, padbc, bcd, y, gate, state, cc, cumul, tail, mine, theirs,
+                 agg, aggs, turn, half_in, half_out, incoming, local, ts, tr, hs, hr, es, er, bs, br, xs, xr, zs, zr, os, orr, gs, gr):
+    bf, f32 = jnp.bfloat16, jnp.float32
     mpair, mring = mp_place()
-    spair, sring, score = seq_place()
-    greet(neighbours(mp_names, mpair, mring, 0, False) + neighbours(seq_names, spair, sring, score, True))
-    depth = wx_ref.shape[0]
+    pair, ring, core = seq_place()
+    place = lax.axis_index("seq")
+    following, previous = (place + 1) % 16, (place + 15) % 16
+    greet(neighbours(mp_names, mpair, mring, 0, False) + neighbours(seq_names, pair, ring, core, True)
+          + [{"seq": following}, {"seq": previous}])
+    n = x_ref.shape[0]
+    depth, tall = wx_ref.shape[0], wo_ref.shape[0]
+    count = n // QB
+    width = wx_ref.shape[1]
 
     def wide_view(ref):
         return lambda pair, ring, core, piece: ref.at[pl.ds(((pair * 4 + ring) * 2 + core) * depth + piece.start, piece.size), :]
 
-    hidden = Gather(lambda pair, ring, core, piece: whole.at[pair * 4 + ring, piece], lambda piece: x_ref.at[piece], mp_names,
-                    mpair, mring, 0, ms, mr, 0, cut(x_ref.shape[0], 2), False)
-    small = Gather(wide_view(wba_ref), lambda piece: wb_ref.at[piece], seq_names, spair, sring, score, bs, br, 0, cut(depth, 2), True)
-    big = Gather(wide_view(wxa_ref), lambda piece: wx_ref.at[piece], seq_names, spair, sring, score, xs, xr, 0, cut(depth, 2), True)
-    here = (spair * 4 + sring) * 2 + score
-    mine = [pltpu.make_async_copy(x_ref, whole.at[mpair * 4 + mring], local.at[0]),
-            pltpu.make_async_copy(wx_ref, wxa_ref.at[pl.ds(here * depth, depth), :], local.at[1]),
-            pltpu.make_async_copy(wb_ref, wba_ref.at[pl.ds(here * depth, depth), :], local.at[2])]
-    everything = (hidden, small, big)
-    for g in everything:
-        g.begin()
-    for copy in mine:
+    def seq_gather(kind, view, own, sends, recvs, base, pieces, fan=True):
+        return kind(view, lambda piece: own.at[piece], seq_names, pair, ring, core, sends, recvs, base, pieces, fan)
+
+    def mp_view(pair, ring, core, piece):
+        return whole.at[pair * 4 + ring, piece]
+
+    hidden = Gather(mp_view, lambda piece: x_ref.at[piece], mp_names, mpair, mring, 0, hs, hr, 0, cut(n, 2), False)
+    edge = Gather(mp_view, lambda piece: tail, mp_names, mpair, mring, 0, es, er, 0, [pl.ds(n, 16)], False)
+    small = seq_gather(Gather, wide_view(wba), wb_ref, bs, br, 0, cut(depth, 2))
+    big = seq_gather(Gather, wide_view(wxa), wx_ref, xs, xr, 0, cut(depth, 2))
+    fan2 = copies_of(2, True)
+    quarters, parts = cut(depth, 4), cut(tall, 4)
+    z_pair = seq_gather(Gather, wide_view(wza), wz_ref, zs, zr, 0, quarters[0:2])
+    z_ring = seq_gather(RingFirst, wide_view(wza), wz_ref, zs, zr, fan2, quarters[2:4])
+
+    def out_view(pair, ring, core, piece):
+        return woa.at[(pair * 4 + ring) * 2 + core, piece]
+
+    o_pair = seq_gather(Gather, out_view, wo_ref, os, orr, 0, parts[0:2])
+    o_ring = seq_gather(RingFirst, out_view, wo_ref, os, orr, fan2, parts[2:4])
+    own_rows = pl.ds(place * depth, depth)
+    at_home = [pltpu.make_async_copy(x_ref, whole.at[mpair * 4 + mring, pl.ds(0, n)], local.at[0]),
+               pltpu.make_async_copy(wx_ref, wxa.at[own_rows, :], local.at[1]),
+               pltpu.make_async_copy(wb_ref, wba.at[own_rows, :], local.at[2]),
+               pltpu.make_async_copy(wz_ref, wza.at[own_rows, :], local.at[3]),
+               pltpu.make_async_copy(wo_ref, woa.at[place], local.at[4])]
+
+    def to_device(src, dst, index, device):
+        copy = pltpu.make_async_remote_copy(src_ref=src, dst_ref=dst, send_sem=ts.at[index], recv_sem=tr.at[index],
+                                            device_id=device, device_id_type=MESH)
         copy.start()
+        return copy
+
+    shifted = to_device(x_ref.at[pl.ds(n - 16, 16)], tail, 0, {"seq": following})
+    small.begin()
+    hidden.begin()
+    big.begin()
+    for copy in at_home:
+        copy.start()
+    shifted.wait_recv()
+    edge.begin()
+    home_tail = pltpu.make_async_copy(tail, whole.at[mpair * 4 + mring, pl.ds(n, 16)], local.at[5])
+    home_tail.start()
     for k in range(2):
-        for g in (small, hidden, big):
-            g.second(k)
+        small.second(k)
+        hidden.second(k)
+        big.second(k)
+    edge.second(0)
     for which in range(2):
         for k in range(2):
             for g in (small, hidden, big):
                 g.forward(which, k)
+        edge.forward(which, 0)
+    z_ring.begin()
+    z_pair.begin()
     hidden.last()
-    mine[0].wait()
-    write_normed(whole, gain_ref, normed_ref, 0, whole.shape[1])
+    edge.last()
+    at_home[0].wait()
+    home_tail.wait()
+    write_normed(whole, norm_ref, normed, 0, n, 32)
+    write_normed(whole, norm_ref, normed, n, 16, 16)
     small.last()
+    small.finish()
+    at_home[2].wait()
+    inside = jnp.where(place > 0, 1.0, 0.0)
+    product = jnp.dot(normed[...], wba[...], preferred_element_type=f32)
+    bcd[...] = product[0:n, 2 * N:3 * N]
+    padbc[pl.ds(8, n), :] = product[0:n, 0:2 * N]
+    padbc[pl.ds(0, 8), :] = product[n + 8:n + 16, 0:2 * N] * inside
+    z_pair.second(0)
+    z_pair.second(1)
     big.last()
-    for g in everything:
+    big.finish()
+    at_home[1].wait()
+    for part in range(4):
+        lanes = slice(part * 256, (part + 1) * 256)
+        product = jnp.dot(normed[...], wxa[:, lanes], preferred_element_type=f32)
+        padx[pl.ds(8, n), lanes] = product[0:n]
+        padx[pl.ds(0, 8), lanes] = product[n + 8:n + 16] * inside
+    z_ring.forward(0)
+    z_ring.forward(1)
+
+    state[...] = jnp.zeros_like(state)
+    row = lax.broadcasted_iota(jnp.int32, (QB, QB), 0)
+    col = lax.broadcasted_iota(jnp.int32, (QB, QB), 1)
+    causal = row >= col
+    tri = jnp.where(causal, 1.0, 0.0).astype(f32)
+    low = col < P_SIZE
+
+    def conv(pad, taps, start, lanes):
+        whole_rows = pad[pl.ds(start, QB + 8), lanes]
+        total = taps[0:1, lanes] * whole_rows[5:5 + QB]
+        for j in range(1, 4):
+            total = total + taps[j:j + 1, lanes] * whole_rows[5 + j:5 + j + QB]
+        return total / (1.0 + jnp.exp(-total))
+
+    def one(c, before):
+        start = pl.multiple_of(c * QB, QB)
+        here = pl.ds(start, QB)
+        bv = conv(padbc, cbc_ref, start, slice(0, N))
+        cv = conv(padbc, cbc_ref, start, slice(N, 2 * N)).astype(bf)
+        cc[here, :] = cv
+        raw = bcd[here, :] + bias_ref[...]
+        step = jnp.maximum(raw, 0.0) + jnp.log1p(jnp.exp(-jnp.abs(raw)))
+        decay = -rate_ref[...] * step
+        cum = jnp.dot(tri, decay, precision=lax.Precision.HIGHEST, preferred_element_type=f32)
+        cumul[here, :] = cum + before
+        cum_t, step_t = cum.T, step.T
+        last = cum[QB - 1:QB, :]
+        bt = bv.T.astype(bf)
+        affinity = jnp.dot(cv, bt, preferred_element_type=f32)
+        for p in range(width // 128):
+            lanes = slice(p * 128, (p + 1) * 128)
+            xv = conv(padx, cx_ref, start, lanes)
+            mixes, grown, tails, ends = [], [], [], []
+            for h in (2 * p, 2 * p + 1):
+                ct = jnp.broadcast_to(cum[:, h:h + 1], (QB, QB))
+                st = jnp.broadcast_to(step[:, h:h + 1], (QB, QB))
+                end = jnp.broadcast_to(last[:, h:h + 1], (1, QB))
+                spread = jnp.where(causal, ct - cum_t[h:h + 1, :], -jnp.inf)
+                mixes.append((affinity * jnp.exp(spread) * step_t[h:h + 1, :]).astype(bf))
+                grown.append(ct)
+                tails.append(jnp.exp(end - ct) * st)
+                ends.append(end)
+            mixed = jnp.concatenate(mixes, axis=1)
+            xs2 = jnp.concatenate([jnp.where(low, xv, 0.0).astype(bf), jnp.where(low, 0.0, xv).astype(bf)], axis=0)
+            out = jnp.dot(mixed, xs2, preferred_element_type=f32)
+            old = state[:, lanes]
+            carried = jnp.dot(cv, old.astype(bf), preferred_element_type=f32)
+            out = out + jnp.exp(jnp.where(low, grown[0], grown[1])) * carried
+            y[here, lanes] = out + skip_ref[0:1, lanes] * xv
+            weighted = (xv * jnp.where(low, tails[0], tails[1])).astype(bf)
+            fresh = jnp.dot(bt, weighted, preferred_element_type=f32)
+            state[:, lanes] = jnp.exp(jnp.where(low[0:1], ends[0], ends[1])) * old + fresh
+        return before + last
+
+    total = lax.fori_loop(0, count, one, jnp.zeros((1, 128), f32))
+    mine[0:N, :] = state[...].astype(bf)
+    for p in range(width // 128):
+        lanes = slice(p * 128, (p + 1) * 128)
+        ends = [jnp.broadcast_to(total[:, h:h + 1], (16, 128)) for h in (2 * p, 2 * p + 1)]
+        mine[N:N + 16, lanes] = three_terms(jnp.exp(jnp.where(low[0:16], ends[0], ends[1])))
+    swapped = to_device(mine, theirs, 1, {"seq": place + 1 - 2 * core})
+    for which in range(2):
+        for k in range(2):
+            z_pair.forward(which, k)
+    swapped.wait_recv()
+    half = width // 2
+    ours = pl.ds(pl.multiple_of(core * half, half), half)
+    rest = pl.ds(pl.multiple_of((1 - core) * half, half), half)
+    a, b = mine[:, ours].astype(f32), theirs[:, ours].astype(f32)
+    head = core == 0
+    early, late = jnp.where(head, a, b), jnp.where(head, b, a)
+    early_decay, late_decay = decay_of(early[N:N + 16]), decay_of(late[N:N + 16])
+    agg[0:N, :] = (late_decay * early[0:N] + late[0:N]).astype(bf)
+    agg[N:N + 16, :] = three_terms(jnp.broadcast_to(early_decay * late_decay, (16, half)))
+    chip = pair * 4 + ring
+    chips = Gather(lambda pair, ring, core, piece: aggs.at[pair * 4 + ring, piece], lambda piece: agg.at[piece], seq_names,
+                   pair, ring, core, gs, gr, 0, [pl.ds(0, 80), pl.ds(80, N + 16 - 80)], False)
+    chips.begin()
+    o_ring.begin()
+    o_pair.begin()
+    z_ring.last()
+    chips.second(0)
+    chips.second(1)
+    z_pair.last()
+    o_pair.second(0)
+    o_pair.second(1)
+    for which in range(2):
+        for k in range(2):
+            chips.forward(which, k)
+    z_ring.pairs()
+    o_ring.forward(0)
+    o_ring.forward(1)
+    z_pair.finish()
+    z_ring.finish()
+    at_home[3].wait()
+
+    def open_gate(part):
+        lanes = slice(part * 256, (part + 1) * 256)
+        gate[:, lanes] = jnp.dot(normed[0:n, :], wza[:, lanes], preferred_element_type=f32)
+
+    open_gate(0)
+    o_pair.forward(0, 0)
+    o_pair.forward(0, 1)
+    open_gate(1)
+    chips.last()
+    half_out[...] = jnp.zeros_like(half_out)
+
+    def add(k, _):
+        half_out[...] = decay_of(aggs[k, N:N + 16, :]) * half_out[...] + aggs[k, 0:N, :].astype(f32)
+        return 0
+
+    lax.fori_loop(0, chip, add, 0)
+    turn[...] = half_out[...].astype(bf)
+    given = to_device(turn, half_in, 2, {"seq": place + 1 - 2 * core})
+    o_pair.forward(1, 0)
+    o_pair.forward(1, 1)
+    open_gate(2)
+    o_ring.last()
+    open_gate(3)
+    given.wait_recv()
+    incoming[:, ours] = half_out[...]
+    incoming[:, rest] = half_in[...].astype(f32)
+    keep = jnp.where(head, 0.0, 1.0)
+    before = theirs[N:N + 16, :].astype(f32)
+    before_decay = jnp.where(head, 1.0, before[0:1] + (before[1:2] + before[2:3]))
+    incoming[...] = before_decay * incoming[...] + keep * theirs[0:N, :].astype(f32)
+    low_rows = low
+
+    def close(c, _):
+        here = pl.ds(pl.multiple_of(c * QB, QB), QB)
+        cv = cc[here, :]
+        cum = cumul[here, :]
+        square = jnp.zeros((QB, 128), f32)
+        for p in range(width // 128):
+            lanes = slice(p * 128, (p + 1) * 128)
+            ct = jnp.where(low_rows, jnp.broadcast_to(cum[:, 2 * p:2 * p + 1], (QB, 128)),
+                           jnp.broadcast_to(cum[:, 2 * p + 1:2 * p + 2], (QB, 128)))
+            carried = jnp.dot(cv, incoming[:, lanes].astype(bf), preferred_element_type=f32)
+            g = gate[here, lanes]
+            value = (y[here, lanes] + jnp.exp(ct) * carried) * (g / (1.0 + jnp.exp(-g)))
+            gate[here, lanes] = value
+            square = square + value * value
+        scale = lax.rsqrt(jnp.sum(square, axis=1, keepdims=True) / width + 1e-05)
+        out_ref[here, :] = (gate[here, :] * scale * gain_ref[...]).astype(bf)
+        return 0
+
+    lax.fori_loop(0, count, close, 0)
+    o_pair.last()
+    o_ring.pairs()
+    for g in (o_pair, o_ring, hidden, edge, chips):
         g.finish()
-    for copy in mine[1:]:
-        copy.wait()
-
-
-def run_first(x, wx, wb, gain, cid):
+    at_home[4].wait()
+    for copy in (shifted, swapped, given):
+        copy.wait_send()
+
+
+def run_mixer(x, wx, wb, wz, wo, norm_gain, conv_x, conv_bc, bias, rate, skip, gain, cid):
     n, w = x.shape
-    depth = wx.shape[0]
-    D = pltpu.SemaphoreType.DMA
-    few, many = copies_of(2, False), copies_of(2, True)
-    bf = jnp.bfloat16
+    depth, width = wx.shape
+    tall, cols = wo.shape
+    D, V = pltpu.SemaphoreType.DMA, pltpu.VMEM
+    bf, f32 = jnp.bfloat16, jnp.float32
+    fan2, plain2 = copies_of(2, True), copies_of(2, False)
+    pairs = []
+    for size in (3, plain2, copies_of(1, False), fan2, fan2, 2 * fan2, 2 * fan2, plain2):
+        pairs += [D((size,)), D((size,))]
     return pl.pallas_call(
-        first_kernel,
-        out_shape=(jax.ShapeDtypeStruct((n, 8 * w), bf), jax.ShapeDtypeStruct((16 * depth, wx.shape[1]), bf),
-                   jax.ShapeDtypeStruct((16 * depth, wb.shape[1]), bf)),
-        in_specs=[VM] * 4, out_specs=(VM,) * 3,
-        scratch_shapes=[pltpu.VMEM((8, n, w), bf), D((3,)), D((few,)), D((few,)), D((many,)), D((many,)), D((many,)), D((many,))],
-        compiler_params=pltpu.CompilerParams(collective_id=cid, has_side_effects=True, vmem_limit_bytes=40 << 20),
-    )(x, wx, wb, gain)
+        mixer_kernel,
+        out_shape=(jax.ShapeDtypeStruct((n, width), bf), jax.ShapeDtypeStruct((16, tall, cols), bf)),
+        in_specs=[VM] * 12, out_specs=(VM, VM),
+        scratch_shapes=[V((8, n + 16, w), bf), V((n + 16, 8 * w), bf), V((16 * depth, width), bf), V((16 * depth, wb.shape[1]), bf),
+                        V((16 * depth, width), bf), V((n + 8, width), f32), V((n + 8, 2 * N), f32), V((n, N), f32),
+                        V((n, width), f32), V((n, width), f32), V((N, width), f32), V((n, N), bf), V((n, 128), f32),
+                        V((16, w), bf), V((N + 16, width), bf), V((N + 16, width), bf), V((N + 16, width // 2), bf),
+                        V((8, N + 16, width // 2), bf), V((N, width // 2), bf), V((N, width // 2), bf), V((N, width // 2), f32), V((N, width), f32),
+                        D((6,))] + pairs,
+        compiler_params=pltpu.CompilerParams(collective_id=cid, has_side_effects=True, vmem_limit_bytes=63 << 20),
+    )(x, wx, wb, wz, wo, norm_gain, conv_x, conv_bc, bias, rate, skip, gain)
 
 
 def mix_kernel(y_ref, w_hbm, hidden_ref, gain_ref, mixed_ref, normed_ref, w, p, tmp, d1, d2, ysrc, ydst, whole, wsem,
@@ -304,9 +578,9 @@
     early.last()
     late.forward(1, 0)
     late.forward(1, 1)
-    write_normed(whole, gain_ref, normed_ref, 0, half)
+    write_normed(whole, gain_ref, normed_ref, 0, half, 32)
     late.last()
-    write_normed(whole, gain_ref, normed_ref, half, half)
+    write_normed(whole, gain_ref, normed_ref, half, half, 32)
     early.finish()
     late.finish()
     for copy in sent:
@@ -328,182 +602,6 @@
                         D((8,))] + [D((2, 2, 2))] * 6 + [D((2,))] * 2 + [D((few,))] * 2,
         compiler_params=pltpu.CompilerParams(collective_id=cid, has_side_effects=True, vmem_limit_bytes=48 << 20),
     )(y, w, hidden, gain)
-
-
-def ssd_kernel(xp_ref, bcd_ref, rimx_ref, rimbc_ref, cx_ref, cbc_ref, bias_ref, rate_ref, skip_ref,
-               y_ref, cc_ref, cum_ref, send_ref, padx, padbc, state):
-    n = xp_ref.shape[0]
-    count = n // QB
-    padx[pl.ds(0, 8), :] = rimx_ref[...]
-    padbc[pl.ds(0, 8), :] = rimbc_ref[...]
-    padx[pl.ds(8, n), :] = xp_ref[...]
-    padbc[pl.ds(8, n), :] = bcd_ref[:, 0:2 * N]
-    state[...] = jnp.zeros_like(state)
-    row = lax.broadcasted_iota(jnp.int32, (QB, QB), 0)
-    col = lax.broadcasted_iota(jnp.int32, (QB, QB), 1)
-    causal = row >= col
-    tri = jnp.where(causal, 1.0, 0.0).astype(jnp.float32)
-    low = col < P_SIZE
-    bf = jnp.bfloat16
-
-    def silu(v):
-        return v / (1.0 + jnp.exp(-v))
-
-    def conv(pad, taps, start, lanes):
-        whole = pad[pl.ds(start, QB + 8), lanes]
-        total = taps[0:1, lanes] * whole[5:5 + QB]
-        for j in range(1, 4):
-            total = total + taps[j:j + 1, lanes] * whole[5 + j:5 + j + QB]
-        return silu(total)
-
-    def one(c, before):
-        start = pl.multiple_of(c * QB, QB)
-        here = pl.ds(start, QB)
-        bv = conv(padbc, cbc_ref, start, slice(0, N))
-        cv = conv(padbc, cbc_ref, start, slice(N, 2 * N)).astype(bf)
-        cc_ref[here, :] = cv
-        raw = bcd_ref[here, 2 * N:3 * N] + bias_ref[...]
-        step = jnp.maximum(raw, 0.0) + jnp.log1p(jnp.exp(-jnp.abs(raw)))
-        decay = -rate_ref[...] * step
-        cum = jnp.dot(tri, decay, precision=lax.Precision.HIGHEST, preferred_element_type=jnp.float32)
-        cum_ref[here, :] = cum + before
-        cum_t, step_t = cum.T, step.T
-        last = cum[QB - 1:QB, :]
-        bt = bv.T.astype(bf)
-        affinity = jnp.dot(cv, bt, preferred_element_type=jnp.float32)
-        for p in range(xp_ref.shape[1] // 128):
-            lanes = slice(p * 128, (p + 1) * 128)
-            xv = conv(padx, cx_ref, start, lanes)
-            mixes, grown, tails, ends = [], [], [], []
-            for h in (2 * p, 2 * p + 1):
-                ct = jnp.broadcast_to(cum[:, h:h + 1], (QB, QB))
-                st = jnp.broadcast_to(step[:, h:h + 1], (QB, QB))
-                end = jnp.broadcast_to(last[:, h:h + 1], (1, QB))
-                spread = jnp.where(causal, ct - cum_t[h:h + 1, :], -jnp.inf)
-                mixes.append((affinity * jnp.exp(spread) * step_t[h:h + 1, :]).astype(bf))
-                grown.append(ct)
-                tails.append(jnp.exp(end - ct) * st)
-                ends.append(end)
-            lowhalf = low[0:1]
-            mixed = jnp.concatenate(mixes, axis=1)
-            xs = jnp.concatenate([jnp.where(low, xv, 0.0).astype(bf), jnp.where(low, 0.0, xv).astype(bf)], axis=0)
-            out = jnp.dot(mixed, xs, preferred_element_type=jnp.float32)
-            old = state[:, lanes]
-            carried = jnp.dot(cv, old.astype(bf), preferred_element_type=jnp.float32)
-            out = out + jnp.exp(jnp.where(low, grown[0], grown[1])) * carried
-            y_ref[here, lanes] = out + skip_ref[0:1, lanes] * xv
-            weighted = (xv * jnp.where(low, tails[0], tails[1])).astype(bf)
-            fresh = jnp.dot(bt, weighted, preferred_element_type=jnp.float32)
-            state[:, lanes] = jnp.exp(jnp.where(lowhalf, ends[0], ends[1])) * old + fresh
-        return before + last
-
-    total = lax.fori_loop(0, count, one, jnp.zeros((1, 128), jnp.float32))
-    send_ref[0:N, :] = state[...].astype(bf)
-    for p in range(xp_ref.shape[1] // 128):
-        lanes = slice(p * 128, (p + 1) * 128)
-        ends = [jnp.broadcast_to(total[:, h:h + 1], (16, 128)) for h in (2 * p, 2 * p + 1)]
-        decay = jnp.exp(jnp.where(low[0:16], ends[0], ends[1]))
-        big = decay.astype(bf)
-        rest = decay - big.astype(jnp.float32)
-        middle = rest.astype(bf)
-        small = (rest - middle.astype(jnp.float32)).astype(bf)
-        which = row[0:16]
-        send_ref[N:N + 16, lanes] = jnp.where(which == 0, big.astype(jnp.float32), jnp.where(
-            which == 1, middle.astype(jnp.float32), small.astype(jnp.float32))).astype(bf)
-
-
-def run_ssd(xp, bcd, rimx, rimbc, conv_x, conv_bc, bias, rate, skip):
-    n, width = xp.shape
-    f32, bf = jnp.float32, jnp.bfloat16
-    return pl.pallas_call(
-        ssd_kernel,
-        out_shape=(jax.ShapeDtypeStruct((n, width), f32), jax.ShapeDtypeStruct((n, N), bf),
-                   jax.ShapeDtypeStruct((n, 128), f32), jax.ShapeDtypeStruct((N + 16, width), bf)),
-        in_specs=[VM] * 9, out_specs=(VM,) * 4,
-        scratch_shapes=[pltpu.VMEM((n + 8, width), f32), pltpu.VMEM((n + 8, 2 * N), f32), pltpu.VMEM((N, width), f32)],
-        compiler_params=pltpu.CompilerParams(vmem_limit_bytes=32 << 20),
-        cost_estimate=pl.CostEstimate(flops=4_000_000_000, bytes_accessed=8 << 20, transcendentals=0),
-    )(xp, bcd, rimx, rimbc, conv_x, conv_bc, bias, rate, skip)
-
-
-def gate_kernel(normed_ref, wz_ref, send_ref, y_ref, cc_ref, cum_ref, gain_ref, out_ref, states, incoming, gate, local, ss, sr):
-    place = lax.axis_index("seq")
-    pair, ring, core = seq_place()
-    greet(neighbours(seq_names, pair, ring, core, True))
-    n, width = y_ref.shape
-    bf, f32 = jnp.bfloat16, jnp.float32
-    tall = send_ref.shape[0]
-    every = Gather(lambda pair, ring, core, piece: states.at[(pair * 4 + ring) * 2 + core, piece], lambda piece: send_ref.at[piece],
-                   seq_names, pair, ring, core, ss, sr, 0, [pl.ds(0, 80), pl.ds(80, tall - 80)], True)
-    mine = pltpu.make_async_copy(send_ref, states.at[place], local)
-    every.begin()
-    mine.start()
-
-    def matmul(part):
-        lanes = slice(part * 128, (part + 1) * 128)
-        gate[:, lanes] = jnp.dot(normed_ref[...], wz_ref[:, lanes], preferred_element_type=f32)
-
-    matmul(0)
-    matmul(1)
-    every.second(0)
-    every.second(1)
-    matmul(2)
-    every.forward(0, 0)
-    every.forward(0, 1)
-    matmul(3)
-    matmul(4)
-    every.forward(1, 0)
-    every.forward(1, 1)
-    matmul(5)
-    matmul(6)
-    matmul(7)
-    every.last()
-    every.finish()
-    mine.wait()
-    incoming[...] = jnp.zeros_like(incoming)
-
-    def add(k, _):
-        tail = states[k, N:N + 16, :].astype(f32)
-        decay = tail[0:1] + (tail[1:2] + tail[2:3])
-        incoming[...] = decay * incoming[...] + states[k, 0:N, :].astype(f32)
-        return 0
-
-    lax.fori_loop(0, place, add, 0)
-    low = lax.broadcasted_iota(jnp.int32, (QB, 128), 1) < P_SIZE
-
-    def one(c, _):
-        here = pl.ds(pl.multiple_of(c * QB, QB), QB)
-        cv = cc_ref[here, :]
-        cum = cum_ref[here, :]
-        square = jnp.zeros((QB, 128), f32)
-        for p in range(width // 128):
-            lanes = slice(p * 128, (p + 1) * 128)
-            ct = jnp.where(low, jnp.broadcast_to(cum[:, 2 * p:2 * p + 1], (QB, 128)),
-                           jnp.broadcast_to(cum[:, 2 * p + 1:2 * p + 2], (QB, 128)))
-            carried = jnp.dot(cv, incoming[:, lanes].astype(bf), preferred_element_type=f32)
-            g = gate[here, lanes]
-            value = (y_ref[here, lanes] + jnp.exp(ct) * carried) * (g / (1.0 + jnp.exp(-g)))
-            gate[here, lanes] = value
-            square = square + value * value
-        scale = lax.rsqrt(jnp.sum(square, axis=1, keepdims=True) / width + 1e-05)
-        out_ref[here, :] = (gate[here, :] * scale * gain_ref[...]).astype(bf)
-        return 0
-
-    lax.fori_loop(0, n // QB, one, 0)
-
-
-def run_gate(normed, wz, send, y, cc, cum, gain, cid):
-    n, width = y.shape
-    D = pltpu.SemaphoreType.DMA
-    many = copies_of(2, True)
-    return pl.pallas_call(
-        gate_kernel,
-        out_shape=jax.ShapeDtypeStruct((n, width), jnp.bfloat16),
-        in_specs=[VM] * 7, out_specs=VM,
-        scratch_shapes=[pltpu.VMEM((16,) + send.shape, jnp.bfloat16), pltpu.VMEM((N, width), jnp.float32),
-                        pltpu.VMEM((n, width), jnp.float32), D, D((many,)), D((many,))],
-        compiler_params=pltpu.CompilerParams(collective_id=cid, has_side_effects=True, vmem_limit_bytes=40 << 20),
-    )(normed, wz, send, y, cc, cum, gain)
 
 
 def attention_kernel(x_ref, wq_ref, wk_ref, wv_ref, out_ref, own, kv, q, peak, total, local, ss, sr):
@@ -615,23 +713,12 @@
 
 def on_device(hidden_in, norm_gain, w_z, w_x, w_b, w_c, w_dt, conv_x, conv_b, conv_c, dt_bias, a_rate,
               skip_gain, group_gain, w_out, attn_gain, w_q, w_k, w_v):
-    f32, bf = jnp.float32, jnp.bfloat16
-    n = hidden_in.shape[0]
     w_bcd = jnp.concatenate([w_b, w_c, jnp.pad(w_dt, ((0, 0), (0, 128 - w_dt.shape[1])))], axis=1)
-    w_z_all = lax.all_gather(w_z, "seq", axis=0, tiled=True)
-    w_out_all = lax.all_gather(w_out, "seq")
-    normed, w_x_all, w_bcd_all = run_first(hidden_in, w_x, w_bcd, norm_gain[None, :], 0)
-    bcd = jnp.dot(normed, w_bcd_all, preferred_element_type=f32)
-    xp = jnp.dot(normed, w_x_all, preferred_element_type=f32)
-    route = [(i, i + 1) for i in range(lax.axis_size("seq") - 1)]
-    rims = lax.ppermute(jnp.concatenate([xp[n - 8:], bcd[n - 8:, 0:2 * N]], axis=1), "seq", route)
-    width = xp.shape[1]
-    y, cc, cum, send = run_ssd(
-        xp, bcd, rims[:, 0:width], rims[:, width:], conv_x, jnp.concatenate([conv_b, conv_c], axis=1),
-        padded(dt_bias), padded(a_rate), jnp.repeat(skip_gain, P_SIZE)[None, :])
-    y_normed = run_gate(normed, w_z_all, send, y, cc, cum, group_gain[None, :], 3)
+    y_normed, w_out_all = run_mixer(
+        hidden_in, w_x, w_bcd, w_z, w_out, norm_gain[None, :], conv_x, jnp.concatenate([conv_b, conv_c], axis=1),
+        padded(dt_bias), padded(a_rate), jnp.repeat(skip_gain, P_SIZE)[None, :], group_gain[None, :], 0)
     mixed, normed_two = run_mix(y_normed, w_out_all, hidden_in, attn_gain[None, :], 1)
-    return (mixed, run_attention(normed_two, w_q, w_k, w_v, 4))
+    return (mixed, run_attention(normed_two, w_q, w_k, w_v, 2))
 
 
 def solution(mesh):

time: 327 us -> 278 us (0.85)
  between operations: 14.3 us -> 0.7 us
  Pallas kernels: 274 us -> 264 us
  local copies, waits for them, and re-layouts: 19.9 us -> 10.6 us
  waiting for transfers between devices: 7.09 us -> 0 us
  matrix products: 6.89 us -> 0 us
    unnamed x53 -> x17, local copies, waits for them, and re-layouts: 19.8 us -> 7.93 us
    pallas_call x3 -> x1, Pallas kernels: 139 us -> 132 us  [run_mixer(): pl.pallas_call(mixer_kernel, out_shape=(jax.ShapeDtypeStruct((n, width),...]
    dot_general x2 -> x0, matrix products: 6.89 us -> none  [the longest x1 4.57 us: on_device(): xp = jnp.dot(normed, w_x_all, preferred_element_type=f32)]
    ppermute x1 -> x0, waiting for transfers between devices: 5.69 us -> none  [on_device(): lax.ppermute(jnp.concatenate([xp[n - 8:], bcd[n - 8:, 0:2 * N]], axis=1),...]
    pallas_call x1, Pallas kernels: 57.3 us -> 54 us  [run_attention(): pl.pallas_call(attention_kernel, out_shape=jax.ShapeDtypeStruct((n, width...]
  transfers between devices with their start and end apart: 3 -> 0, of which waited for: 1 -> 0; matrix products, arithmetic and copies ran while one was open for 3% -> 0% of each run, Pallas kernels for 43% -> 0%
where the time goes in v5:
time: 278 us
  Pallas kernels  264 us (95%)
  local copies, waits for them, and re-layouts  10.6 us (4%)
  other arithmetic  2.87 us (1%)
    pallas_call x1, Pallas kernels, run_mixer(): pl.pallas_call(mixer_kernel, out_shape=(jax.ShapeDtypeStruct((n, width),...  132 us
    pallas_call x1, Pallas kernels, run_mix(): pl.pallas_call(mix_kernel, out_shape=(jax.ShapeDtypeStruct((n, width), jn...  77.6 us
    pallas_call x1, Pallas kernels, run_attention(): pl.pallas_call(attention_kernel, out_shape=jax.ShapeDtypeStruct((n, width...  54 us
    unnamed x17, local copies, waits for them, and re-layouts  7.93 us

profile of v5, /device:TPU:8, one launch (start us, length us, event | category | flops | bytes accessed | tf_op | source)
XLA Modules:
  0.0 277.7 jit_solution(5784020854521067046)
XLA Ops:
  0.6 1.3 pad_bitcast_fusion
  1.9 1.3 pad_maximum_fusion.cbc_ref
  3.2 0.7 broadcast_in_dim.21
  3.9 0.7 broadcast_in_dim_reshape.3.skip_ref
  4.6 0.8 copy.21
  5.4 1.6 fusion.1.wb_ref
  7.0 132.0 %shard_map.194 = (bf16[512,1024]{1,0:T(8,128)(2,1)}, bf16[16,1024,256]{2,1,0:T(8,128)(2,1)}) custom-call(bf16[512,512]{1,0:T(8,128)(2,1)} %hidden_ref.1, bf16[256,1024]{1,0:T(8,128)(2,1)} %wx_ref.1, bf16[256,384]{1,0:T(8,128)(2,1)} %fusion.1.wb_ref, bf16[256,1024]{1,0:T(8,128)(2,1)} %wz_ref.1, bf16[1024,256]{1,0:T(8,128)(2,1)} %wo_ref.1, f32[1,4096]{1,0:T(1,128)} %bitcast.8, ...), custom_call_target="tpu_custom_call" | custom-call | tf_op jit(solution)/shard_map/pallas_call | solution.py:453
  139.0 0.0 copy-start.2
  139.0 1.0 copy-done.2
  140.0 0.0 copy-start.3
  140.0 1.2 copy-done.3
  141.3 0.0 copy-start.6
  141.3 0.7 copy-done.6
  142.0 0.0 copy-start
  142.0 0.0 copy-start.4
  142.0 77.6 %shard_map.195 = (f32[512,512]{1,0:T(8,128)S(1)}, bf16[512,4096]{1,0:T(8,128)(2,1)}) custom-call(bf16[512,1024]{1,0:T(8,128)(2,1)S(1)} %copy-done.3, bf16[16,1024,256]{2,1,0:T(8,128)(2,1)} %get-tuple-element.7.w_hbm, bf16[512,512]{1,0:T(8,128)(2,1)S(1)} %copy-done.2, f32[1,4096]{1,0:T(1,128)S(1)} %bitcast.7), custom_call_target="tpu_custom_call" | custom-call | tf_op jit(solution)/shard_map/pallas_call | solution.py:596
  219.6 0.0 copy-done
  219.6 0.0 copy-done.4
  219.6 0.0 copy-done.5
  219.6 0.0 copy-start.1
  219.6 2.2 copy-done.1
  221.8 54.0 %shard_map.196 = f32[512,512]{1,0:T(8,128)S(1)} custom-call(bf16[512,4096]{1,0:T(8,128)(2,1)S(1)} %copy-done.1, bf16[4096,512]{1,0:T(8,128)(2,1)S(1)} %copy-done, bf16[4096,128]{1,0:T(8,128)(2,1)S(1)} %copy-done.4, bf16[4096,128]{1,0:T(8,128)(2,1)S(1)} %copy-done.5), custom_call_target="tpu_custom_call" | custom-call | tf_op jit(solution)/shard_map/pallas_call | solution.py:700
  275.8 1.0 copy.24
  276.8 1.0 copy.25
  (1 shorter events, 0.0 us)
Async XLA Ops:
  139.0 1.0 copy-start.2
  140.0 1.2 copy-start.3
  141.3 0.7 copy-start.6
  142.0 77.6 %copy-start = (bf16[4096,512]{1,0:T(8,128)(2,1)S(1)}, bf16[4096,512]{1,0:T(8,128)(2,1)}, u32[]{:S(2)}) copy-start(bf16[4096,512]{1,0:T(8,128)(2,1)} %wq_ref.1) | copy-start | bytes 12582916
  142.0 77.6 %copy-start.4 = (bf16[4096,128]{1,0:T(8,128)(2,1)S(1)}, bf16[4096,128]{1,0:T(8,128)(2,1)}, u32[]{:S(2)}) copy-start(bf16[4096,128]{1,0:T(8,128)(2,1)} %wk_ref.1) | copy-start | bytes 3145732
  142.0 77.6 %copy-start.5 = (bf16[4096,128]{1,0:T(8,128)(2,1)S(1)}, bf16[4096,128]{1,0:T(8,128)(2,1)}, u32[]{:S(2)}) copy-start(bf16[4096,128]{1,0:T(8,128)(2,1)} %wv_ref.1) | copy-start | bytes 3145732
  219.6 2.2 copy-start.1

commit v6 on v5

--- a/solution.py
+++ b/solution.py
@@ -184,14 +184,19 @@
     return tail[0:1] + (tail[1:2] + tail[2:3])
 
 
-def mixer_kernel(x_ref, wx_ref, wb_ref, wz_ref, wo_ref, norm_ref, cx_ref, cbc_ref, bias_ref, rate_ref, skip_ref, gain_ref,
-                 out_ref, woa, whole, normed, wxa, wba, wza, padx, padbc, bcd, y, gate, state, cc, cumul, tail, mine, theirs,
-                 agg, aggs, turn, half_in, half_out, incoming, local, ts, tr, hs, hr, es, er, bs, br, xs, xr, zs, zr, os, orr, gs, gr):
+def mixer_kernel(x_ref, wx_ref, wb_ref, wc_ref, wdt_ref, wz_ref, wo_ref, norm_ref, cx_ref, cb_ref, cc_ref, bias_ref, rate_ref,
+                 skip_ref, gain_ref,
+                 out_ref, woa, wbc, vectors, wda, whole, normed, wxa, wba, wza, padx, padbc, bcd, y, gate, state, cc, cumul, tail, mine, theirs,
+                 agg, aggs, turn, half_in, half_out, incoming, local, ts, tr, hs, hr, es, er, ds, dr, bs, br, xs, xr, zs, zr, os, orr, gs, gr):
     bf, f32 = jnp.bfloat16, jnp.float32
     mpair, mring = mp_place()
     pair, ring, core = seq_place()
     place = lax.axis_index("seq")
     following, previous = (place + 1) % 16, (place + 15) % 16
+    joined = [pltpu.make_async_copy(wb_ref, wbc.at[:, pl.ds(0, N)], local.at[6]),
+              pltpu.make_async_copy(wc_ref, wbc.at[:, pl.ds(N, N)], local.at[7])]
+    for copy in joined:
+        copy.start()
     greet(neighbours(mp_names, mpair, mring, 0, False) + neighbours(seq_names, pair, ring, core, True)
           + [{"seq": following}, {"seq": previous}])
     n = x_ref.shape[0]
@@ -210,7 +215,12 @@
 
     hidden = Gather(mp_view, lambda piece: x_ref.at[piece], mp_names, mpair, mring, 0, hs, hr, 0, cut(n, 2), False)
     edge = Gather(mp_view, lambda piece: tail, mp_names, mpair, mring, 0, es, er, 0, [pl.ds(n, 16)], False)
-    small = seq_gather(Gather, wide_view(wba), wb_ref, bs, br, 0, cut(depth, 2))
+    small = seq_gather(Gather, wide_view(wba), wbc, bs, br, 0, cut(depth, 2))
+
+    def step_view(pair, ring, core, piece):
+        return wda.at[:, pl.ds(((pair * 4 + ring) * 2 + core) * depth, depth)]
+
+    steps = Gather(step_view, lambda piece: wdt_ref, seq_names, pair, ring, core, ds, dr, 0, [None], True)
     big = seq_gather(Gather, wide_view(wxa), wx_ref, xs, xr, 0, cut(depth, 2))
     fan2 = copies_of(2, True)
     quarters, parts = cut(depth, 4), cut(tall, 4)
@@ -225,7 +235,8 @@
     own_rows = pl.ds(place * depth, depth)
     at_home = [pltpu.make_async_copy(x_ref, whole.at[mpair * 4 + mring, pl.ds(0, n)], local.at[0]),
                pltpu.make_async_copy(wx_ref, wxa.at[own_rows, :], local.at[1]),
-               pltpu.make_async_copy(wb_ref, wba.at[own_rows, :], local.at[2]),
+               pltpu.make_async_copy(wbc, wba.at[own_rows, :], local.at[2]),
+               pltpu.make_async_copy(wdt_ref, wda.at[:, own_rows], local.at[8]),
                pltpu.make_async_copy(wz_ref, wza.at[own_rows, :], local.at[3]),
                pltpu.make_async_copy(wo_ref, woa.at[place], local.at[4])]
 
@@ -236,8 +247,11 @@
         return copy
 
     shifted = to_device(x_ref.at[pl.ds(n - 16, 16)], tail, 0, {"seq": following})
+    hidden.begin()
+    for copy in joined:
+        copy.wait()
     small.begin()
-    hidden.begin()
+    steps.begin()
     big.begin()
     for copy in at_home:
         copy.start()
@@ -249,11 +263,13 @@
         small.second(k)
         hidden.second(k)
         big.second(k)
+    steps.second(0)
     edge.second(0)
     for which in range(2):
         for k in range(2):
             for g in (small, hidden, big):
                 g.forward(which, k)
+        steps.forward(which, 0)
         edge.forward(which, 0)
     z_ring.begin()
     z_pair.begin()
@@ -263,14 +279,22 @@
     home_tail.wait()
     write_normed(whole, norm_ref, normed, 0, n, 32)
     write_normed(whole, norm_ref, normed, n, 16, 16)
+    vectors[...] = jnp.zeros_like(vectors)
+    vectors[0:1, 0:bias_ref.shape[1]] = bias_ref[...]
+    vectors[1:2, 0:rate_ref.shape[1]] = rate_ref[...]
+    bcd[...] = jnp.zeros_like(bcd)
     small.last()
+    steps.last()
     small.finish()
+    steps.finish()
     at_home[2].wait()
+    at_home[3].wait()
     inside = jnp.where(place > 0, 1.0, 0.0)
     product = jnp.dot(normed[...], wba[...], preferred_element_type=f32)
-    bcd[...] = product[0:n, 2 * N:3 * N]
-    padbc[pl.ds(8, n), :] = product[0:n, 0:2 * N]
-    padbc[pl.ds(0, 8), :] = product[n + 8:n + 16, 0:2 * N] * inside
+    bcd[:, 0:bias_ref.shape[1]] = lax.dot_general(
+        normed[0:n, :], wda[...], (((1,), (1,)), ((), ())), preferred_element_type=f32)
+    padbc[pl.ds(8, n), :] = product[0:n]
+    padbc[pl.ds(0, 8), :] = product[n + 8:n + 16] * inside
     z_pair.second(0)
     z_pair.second(1)
     big.last()
@@ -291,22 +315,22 @@
     tri = jnp.where(causal, 1.0, 0.0).astype(f32)
     low = col < P_SIZE
 
-    def conv(pad, taps, start, lanes):
+    def conv(pad, taps, start, lanes, tap_lanes):
         whole_rows = pad[pl.ds(start, QB + 8), lanes]
-        total = taps[0:1, lanes] * whole_rows[5:5 + QB]
+        total = taps[0:1, tap_lanes] * whole_rows[5:5 + QB]
         for j in range(1, 4):
-            total = total + taps[j:j + 1, lanes] * whole_rows[5 + j:5 + j + QB]
+            total = total + taps[j:j + 1, tap_lanes] * whole_rows[5 + j:5 + j + QB]
         return total / (1.0 + jnp.exp(-total))
 
     def one(c, before):
         start = pl.multiple_of(c * QB, QB)
         here = pl.ds(start, QB)
-        bv = conv(padbc, cbc_ref, start, slice(0, N))
-        cv = conv(padbc, cbc_ref, start, slice(N, 2 * N)).astype(bf)
+        bv = conv(padbc, cb_ref, start, slice(0, N), slice(0, N))
+        cv = conv(padbc, cc_ref, start, slice(N, 2 * N), slice(0, N)).astype(bf)
         cc[here, :] = cv
-        raw = bcd[here, :] + bias_ref[...]
+        raw = bcd[here, :] + vectors[0:1, :]
         step = jnp.maximum(raw, 0.0) + jnp.log1p(jnp.exp(-jnp.abs(raw)))
-        decay = -rate_ref[...] * step
+        decay = -vectors[1:2, :] * step
         cum = jnp.dot(tri, decay, precision=lax.Precision.HIGHEST, preferred_element_type=f32)
         cumul[here, :] = cum + before
         cum_t, step_t = cum.T, step.T
@@ -315,7 +339,7 @@
         affinity = jnp.dot(cv, bt, preferred_element_type=f32)
         for p in range(width // 128):
             lanes = slice(p * 128, (p + 1) * 128)
-            xv = conv(padx, cx_ref, start, lanes)
+            xv = conv(padx, cx_ref, start, lanes, lanes)
             mixes, grown, tails, ends = [], [], [], []
             for h in (2 * p, 2 * p + 1):
                 ct = jnp.broadcast_to(cum[:, h:h + 1], (QB, QB))
@@ -332,7 +356,8 @@
             old = state[:, lanes]
             carried = jnp.dot(cv, old.astype(bf), preferred_element_type=f32)
             out = out + jnp.exp(jnp.where(low, grown[0], grown[1])) * carried
-            y[here, lanes] = out + skip_ref[0:1, lanes] * xv
+            skips = [jnp.broadcast_to(skip_ref[:, h:h + 1], (1, QB)) for h in (2 * p, 2 * p + 1)]
+            y[here, lanes] = out + jnp.where(low[0:1], skips[0], skips[1]) * xv
             weighted = (xv * jnp.where(low, tails[0], tails[1])).astype(bf)
             fresh = jnp.dot(bt, weighted, preferred_element_type=f32)
             state[:, lanes] = jnp.exp(jnp.where(low[0:1], ends[0], ends[1])) * old + fresh
@@ -378,7 +403,7 @@
     o_ring.forward(1)
     z_pair.finish()
     z_ring.finish()
-    at_home[3].wait()
+    at_home[4].wait()
 
     def open_gate(part):
         lanes = slice(part * 256, (part + 1) * 256)
@@ -435,12 +460,12 @@
     o_ring.pairs()
     for g in (o_pair, o_ring, hidden, edge, chips):
         g.finish()
-    at_home[4].wait()
+    at_home[5].wait()
     for copy in (shifted, swapped, given):
         copy.wait_send()
 
 
-def run_mixer(x, wx, wb, wz, wo, norm_gain, conv_x, conv_bc, bias, rate, skip, gain, cid):
+def run_mixer(x, wx, wb, wc, wdt, wz, wo, norm_gain, conv_x, conv_b, conv_c, bias, rate, skip, gain, cid):
     n, w = x.shape
     depth, width = wx.shape
     tall, cols = wo.shape
@@ -448,20 +473,21 @@
     bf, f32 = jnp.bfloat16, jnp.float32
     fan2, plain2 = copies_of(2, True), copies_of(2, False)
     pairs = []
-    for size in (3, plain2, copies_of(1, False), fan2, fan2, 2 * fan2, 2 * fan2, plain2):
+    for size in (3, plain2, copies_of(1, False), copies_of(1, True), fan2, fan2, 2 * fan2, 2 * fan2, plain2):
         pairs += [D((size,)), D((size,))]
     return pl.pallas_call(
         mixer_kernel,
         out_shape=(jax.ShapeDtypeStruct((n, width), bf), jax.ShapeDtypeStruct((16, tall, cols), bf)),
-        in_specs=[VM] * 12, out_specs=(VM, VM),
-        scratch_shapes=[V((8, n + 16, w), bf), V((n + 16, 8 * w), bf), V((16 * depth, width), bf), V((16 * depth, wb.shape[1]), bf),
+        in_specs=[VM] * 15, out_specs=(VM, VM),
+        scratch_shapes=[V((depth, 2 * N), bf), V((8, 128), f32), V((16, 16 * depth), bf),
+                        V((8, n + 16, w), bf), V((n + 16, 8 * w), bf), V((16 * depth, width), bf), V((16 * depth, 2 * N), bf),
                         V((16 * depth, width), bf), V((n + 8, width), f32), V((n + 8, 2 * N), f32), V((n, N), f32),
                         V((n, width), f32), V((n, width), f32), V((N, width), f32), V((n, N), bf), V((n, 128), f32),
                         V((16, w), bf), V((N + 16, width), bf), V((N + 16, width), bf), V((N + 16, width // 2), bf),
                         V((8, N + 16, width // 2), bf), V((N, width // 2), bf), V((N, width // 2), bf), V((N, width // 2), f32), V((N, width), f32),
-                        D((6,))] + pairs,
+                        D((9,))] + pairs,
         compiler_params=pltpu.CompilerParams(collective_id=cid, has_side_effects=True, vmem_limit_bytes=63 << 20),
-    )(x, wx, wb, wz, wo, norm_gain, conv_x, conv_bc, bias, rate, skip, gain)
+    )(x, wx, wb, wc, wdt, wz, wo, norm_gain, conv_x, conv_b, conv_c, bias, rate, skip, gain)
 
 
 def mix_kernel(y_ref, w_hbm, hidden_ref, gain_ref, mixed_ref, normed_ref, w, p, tmp, d1, d2, ysrc, ydst, whole, wsem,
@@ -617,36 +643,36 @@
     every = Gather(lambda pair, ring, core, piece: kv.at[(pair * 4 + ring) * 2 + core, piece], lambda piece: own.at[piece],
                    seq_names, pair, ring, core, ss, sr, 0, cut(n, 2), True)
     every.begin()
-    for h in range(heads):
-        q[h] = jnp.dot(x_ref[...], wq_ref[:, h * HD:(h + 1) * HD], preferred_element_type=f32).astype(bf)
+    mine = pltpu.make_async_copy(own, kv.at[place], local)
+    mine.start()
+    for h in range(0, heads, 2):
+        both = jnp.dot(x_ref[...], wq_ref[:, h * HD:(h + 2) * HD], preferred_element_type=f32) * scale
+        q[h] = both[:, 0:HD].astype(bf)
+        q[h + 1] = both[:, HD:2 * HD].astype(bf)
     peak[...] = jnp.full_like(peak, -1e30)
     total[...] = jnp.zeros_like(total)
 
-    def work(block, edge):
-        def head(h, _):
-            keys = block[:, 0:HD]
-            both = jnp.concatenate([block[:, HD:2 * HD], jnp.ones((n, HD), bf)], axis=1)
-            if edge is not None:
-                t = lax.broadcasted_iota(jnp.int32, (n, n), 0)
-                s = lax.broadcasted_iota(jnp.int32, (n, n), 1)
-                allowed = s > t if edge == 0 else s <= t
-            scores = lax.dot_general(q[h], keys, (((1,), (1,)), ((), ())), preferred_element_type=f32) * scale
-            if edge is not None:
+    def work(block, bounds):
+        keys = block[:, 0:HD]
+        both = jnp.concatenate([block[:, HD:2 * HD], jnp.ones((n, HD), bf)], axis=1)
+        if bounds is not None:
+            away = lax.broadcasted_iota(jnp.int32, (n, n), 1) - lax.broadcasted_iota(jnp.int32, (n, n), 0)
+            allowed = (away > bounds[0]) & (away <= bounds[1])
+        for h in range(heads):
+            scores = lax.dot_general(q[h], keys, (((1,), (1,)), ((), ())), preferred_element_type=f32)
+            if bounds is not None:
                 scores = jnp.where(allowed, scores, -1e30)
             old = peak[h]
             new = jnp.maximum(old, jnp.max(scores, axis=1, keepdims=True))
             weights = jnp.exp2(scores - new[:, 0:1])
-            if edge == 0:
+            if bounds is not None:
                 weights = jnp.where(allowed, weights, 0.0)
             shrink = jnp.exp2(old - new)
             peak[h] = new
             total[h] = jnp.concatenate([shrink, shrink], axis=1) * total[h] + jnp.dot(
                 weights.astype(bf), both, preferred_element_type=f32)
-            return 0
-
-        lax.fori_loop(0, heads, head, 0)
-
-    def visit(first, count, chip):
+
+    def visit(count, chip):
         def one(j, _):
             other_pair, other_ring = chip(j // 2)
             which = (other_pair * 4 + other_ring) * 2 + j % 2
@@ -657,33 +683,30 @@
                 work(kv.at[which], None)
             return 0
 
-        lax.fori_loop(first, count, one, 0)
-
-    work(own, 1)
+        lax.fori_loop(0, count, one, 0)
+
     every.second(0)
     every.second(1)
-
-    @pl.when(pair == 1)
-    def _():
-        work(kv.at[ring * 2 + core], 0)
-
     every.forward(0, 0)
     every.forward(0, 1)
-    for copy in every.across[0:4]:
-        copy.wait_recv()
-    mine = pltpu.make_async_copy(own, kv.at[place], local)
-    mine.start()
     mine.wait()
-    visit(0, 4, lambda g: (jnp.where(g == 0, pair, 1 - pair), ring))
+
+    def rim(j, _):
+        @pl.when((j == 0) | (pair == 1))
+        def _():
+            work(kv.at[jnp.where(j == 0, place, ring * 2 + core)], (jnp.where(j == 0, -n, 0), jnp.where(j == 0, 0, n)))
+        return 0
+
+    lax.fori_loop(0, 2, rim, 0)
     every.forward(1, 0)
     every.forward(1, 1)
-    for copy in every.across[4:12]:
+    for copy in every.across[0:12]:
         copy.wait_recv()
-    visit(0, 8, lambda g: (jnp.where(g < 2, pair, 1 - pair), (ring + 1 + 2 * (g % 2)) % 4))
+    visit(12, lambda g: (jnp.where(g % 2 == 0, pair, 1 - pair), (ring + jnp.where(g < 2, 0, jnp.where(g < 4, 1, 3))) % 4))
     every.last()
     for copy in every.across[12:]:
         copy.wait_recv()
-    visit(0, 4, lambda g: (jnp.where(g == 0, pair, 1 - pair), (ring + 2) % 4))
+    visit(4, lambda g: (jnp.where(g == 0, pair, 1 - pair), (ring + 2) % 4))
     for copy in every.started:
         copy.wait_send()
     for h in range(heads):
@@ -707,16 +730,11 @@
     )(x, wq, wk, wv)
 
 
-def padded(vector):
-    return jnp.pad(vector, (0, 128 - vector.shape[0]))[None, :]
-
-
 def on_device(hidden_in, norm_gain, w_z, w_x, w_b, w_c, w_dt, conv_x, conv_b, conv_c, dt_bias, a_rate,
               skip_gain, group_gain, w_out, attn_gain, w_q, w_k, w_v):
-    w_bcd = jnp.concatenate([w_b, w_c, jnp.pad(w_dt, ((0, 0), (0, 128 - w_dt.shape[1])))], axis=1)
     y_normed, w_out_all = run_mixer(
-        hidden_in, w_x, w_bcd, w_z, w_out, norm_gain[None, :], conv_x, jnp.concatenate([conv_b, conv_c], axis=1),
-        padded(dt_bias), padded(a_rate), jnp.repeat(skip_gain, P_SIZE)[None, :], group_gain[None, :], 0)
+        hidden_in, w_x, w_b, w_c, w_dt.T, w_z, w_out, norm_gain[None, :], conv_x, conv_b, conv_c,
+        dt_bias[None, :], a_rate[None, :], skip_gain[None, :], group_gain[None, :], 0)
     mixed, normed_two = run_mix(y_normed, w_out_all, hidden_in, attn_gain[None, :], 1)
     return (mixed, run_attention(normed_two, w_q, w_k, w_v, 2))
 

time: 278 us -> 254 us (0.914)
  Pallas kernels: 264 us -> 246 us
  local copies, waits for them, and re-layouts: 10.6 us -> 7.11 us
  other arithmetic: 2.87 us -> 0 us
    pallas_call x1, Pallas kernels: 54 us -> 38.3 us  [run_attention(): pl.pallas_call(attention_kernel, out_shape=jax.ShapeDtypeStruct((n, width...]
    concatenate x2 -> x0, other arithmetic: 2.87 us -> none  [the longest x1 1.57 us: on_device(): jnp.concatenate([w_b, w_c, jnp.pad(w_dt, ((0, 0), (0, 128 - w_dt.shape[1]...]
    pallas_call x1, Pallas kernels: 132 us -> 129 us  [run_mixer(): pl.pallas_call(mixer_kernel, out_shape=(jax.ShapeDtypeStruct((n, width),...]
    unnamed x17 -> x16, local copies, waits for them, and re-layouts: 7.93 us -> 7.11 us
where the time goes in v6:
time: 254 us
  Pallas kernels  246 us (97%)
  local copies, waits for them, and re-layouts  7.11 us (3%)
    pallas_call x1, Pallas kernels, run_mixer(): pl.pallas_call(mixer_kernel, out_shape=(jax.ShapeDtypeStruct((n, width),...  129 us
    pallas_call x1, Pallas kernels, run_mix(): pl.pallas_call(mix_kernel, out_shape=(jax.ShapeDtypeStruct((n, width), jn...  78.2 us
    pallas_call x1, Pallas kernels, run_attention(): pl.pallas_call(attention_kernel, out_shape=jax.ShapeDtypeStruct((n, width...  38.3 us
    unnamed x16, local copies, waits for them, and re-layouts  7.11 us

profile of v6, /device:TPU:8, one launch (start us, length us, event | category | flops | bytes accessed | tf_op | source)
XLA Modules:
  0.0 253.5 jit_solution(13500156510378398659)
XLA Ops:
  0.6 129.2 %shard_map.194 = (bf16[512,1024]{1,0:T(8,128)(2,1)}, bf16[16,1024,256]{2,1,0:T(8,128)(2,1)}) custom-call(bf16[512,512]{1,0:T(8,128)(2,1)} %hidden_ref.1, bf16[256,1024]{1,0:T(8,128)(2,1)} %wx_ref.1, bf16[256,128]{1,0:T(8,128)(2,1)} %wb_ref.1, bf16[256,128]{1,0:T(8,128)(2,1)} %wc_ref.1, bf16[16,256]{1,0:T(8,128)(2,1)} %bitcast.9, bf16[256,1024]{1,0:T(8,128)(2,1)} %wz_ref.1, ...), custom_call_target="tpu_custom_call" | custom-call | tf_op jit(solution)/shard_map/pallas_call | solution.py:478
  129.8 0.0 copy-start.2
  129.8 1.0 copy-done.2
  130.9 0.0 copy-start.3
  130.9 1.2 copy-done.3
  132.1 0.0 copy-start.6
  132.1 0.7 copy-done.6
  132.8 0.0 copy-start
  132.8 0.0 copy-start.4
  132.8 0.0 copy-start.5
  132.8 78.2 %shard_map.195 = (f32[512,512]{1,0:T(8,128)S(1)}, bf16[512,4096]{1,0:T(8,128)(2,1)}) custom-call(bf16[512,1024]{1,0:T(8,128)(2,1)S(1)} %copy-done.3, bf16[16,1024,256]{2,1,0:T(8,128)(2,1)} %get-tuple-element.7.w_hbm, bf16[512,512]{1,0:T(8,128)(2,1)S(1)} %copy-done.2, f32[1,4096]{1,0:T(1,128)S(1)} %bitcast.7), custom_call_target="tpu_custom_call" | custom-call | tf_op jit(solution)/shard_map/pallas_call | solution.py:622
  211.1 0.0 copy-done
  211.1 0.0 copy-done.4
  211.1 0.0 copy-done.5
  211.1 0.0 copy-start.1
  211.1 2.2 copy-done.1
  213.3 38.3 %shard_map.196 = f32[512,512]{1,0:T(8,128)S(1)} custom-call(bf16[512,4096]{1,0:T(8,128)(2,1)S(1)} %copy-done.1, bf16[4096,512]{1,0:T(8,128)(2,1)S(1)} %copy-done, bf16[4096,128]{1,0:T(8,128)(2,1)S(1)} %copy-done.4, bf16[4096,128]{1,0:T(8,128)(2,1)S(1)} %copy-done.5), custom_call_target="tpu_custom_call" | custom-call | tf_op jit(solution)/shard_map/pallas_call | solution.py:723
  251.6 1.0 copy.23
  252.6 1.0 copy.24
Async XLA Ops:
  129.8 1.0 copy-start.2
  130.9 1.2 copy-start.3
  132.1 0.7 copy-start.6
  132.8 78.3 %copy-start = (bf16[4096,512]{1,0:T(8,128)(2,1)S(1)}, bf16[4096,512]{1,0:T(8,128)(2,1)}, u32[]{:S(2)}) copy-start(bf16[4096,512]{1,0:T(8,128)(2,1)} %wq_ref.1) | copy-start | bytes 12582916
  132.8 78.3 %copy-start.4 = (bf16[4096,128]{1,0:T(8,128)(2,1)S(1)}, bf16[4096,128]{1,0:T(8,128)(2,1)}, u32[]{:S(2)}) copy-start(bf16[4096,128]{1,0:T(8,128)(2,1)} %wk_ref.1) | copy-start | bytes 3145732
  132.8 78.3 %copy-start.5 = (bf16[4096,128]{1,0:T(8,128)(2,1)S(1)}, bf16[4096,128]{1,0:T(8,128)(2,1)}, u32[]{:S(2)}) copy-start(bf16[4096,128]{1,0:T(8,128)(2,1)} %wv_ref.1) | copy-start | bytes 3145732
  211.1 2.2 copy-start.1

commit v7 on v6

--- a/solution.py
+++ b/solution.py
@@ -490,17 +490,20 @@
     )(x, wx, wb, wc, wdt, wz, wo, norm_gain, conv_x, conv_b, conv_c, bias, rate, skip, gain)
 
 
-def mix_kernel(y_ref, w_hbm, hidden_ref, gain_ref, mixed_ref, normed_ref, w, p, tmp, d1, d2, ysrc, ydst, whole, wsem,
-               s1, r1, s2, r2, sraw, rraw, sy, ry, gs, gr):
+def mix_kernel(y_ref, w_hbm, hidden_ref, gain_ref, mixed_ref, normed_ref, w, p, tmp, d1, d2, ysrc, ydst, yb, joint, tmpb, d1b, d2b, whole,
+               wsem, s1, r1, s2, r2, sraw, rraw, sy, ry, syb, ryb, s1b, r1b, s2b, r2b, srb, rrb, gs, gr):
     high, low = mp_place()
     right, left, far = (low + 1) % 4, (low + 3) % 4, (low + 2) % 4
     me = high * 4 + low
     order = (1 - high, high)
     sides = ((right, left), (left, right))
     n = y_ref.shape[0]
-    half, quarter = n // 2, n // 4
+    half = n // 2
+    na, nb = ydst.shape[1], yb.shape[2]
+    ha, hb = na // 2, nb // 2
     f32 = jnp.float32
-    blocks = [pair * 4 + ring for ring in (far, right, left, low) for pair in order]
+    rings = (far, right, left, low)
+    blocks = [pair * 4 + ring for ring in rings for pair in order]
     loads = [pltpu.make_async_copy(w_hbm.at[pl.ds(2 * b, 2)], w.at[pl.ds(2 * b, 2)], wsem.at[i]) for i, b in enumerate(blocks)]
     for load in loads:
         load.start()
@@ -521,20 +524,20 @@
                 y_ref[here, :], w[2 * b + c], preferred_element_type=f32).astype(p.dtype)
 
     def start_first(h, k):
-        return [send(p.at[order[k] * 4 + far, rows(h * half + d * quarter, quarter)], d1.at[h, k, d], high, sides[d][0],
-                     s1.at[h, k, d], r1.at[h, k, d]) for d in range(2)]
+        first[h][k] = [send(p.at[order[k] * 4 + far, rows(h * half + d * ha, ha)], d1.at[h, k, d], high, sides[d][0],
+                            s1.at[h, k, d], r1.at[h, k, d]) for d in range(2)]
 
     def start_raw(h, k, d):
-        return send(p.at[order[k] * 4 + sides[d][0], rows(h * half + (1 - d) * quarter, quarter)],
-                    d2.at[h, k, d, rows((1 - d) * quarter, quarter)], high, sides[d][0], sraw.at[h, k, d], rraw.at[h, k, d])
+        raw[h][k][d] = send(p.at[order[k] * 4 + sides[d][0], rows(h * half + (1 - d) * ha, ha)],
+                            d2.at[h, k, d, rows((1 - d) * ha, ha)], high, sides[d][0], sraw.at[h, k, d], rraw.at[h, k, d])
 
     def pass_on(h, k):
         result = []
         for d in range(2):
             first[h][k][d].wait_recv()
-            here = slice(h * half + d * quarter, h * half + (d + 1) * quarter)
+            here = slice(h * half + d * ha, h * half + (d + 1) * ha)
             tmp[h, k, d] = (d1[h, k, d].astype(f32) + p[order[k] * 4 + sides[d][0], here, :].astype(f32)).astype(tmp.dtype)
-            result.append(send(tmp.at[h, k, d], d2.at[h, k, d, rows(d * quarter, quarter)], high, sides[d][0],
+            result.append(send(tmp.at[h, k, d], d2.at[h, k, d, rows(d * ha, ha)], high, sides[d][0],
                                s2.at[h, k, d], r2.at[h, k, d]))
         second[h][k] = result
 
@@ -542,73 +545,136 @@
         for d in range(2):
             raw[h][k][d].wait_recv()
             second[h][k][d].wait_recv()
-        here = slice(h * half, (h + 1) * half)
+        here = slice(h * half, h * half + na)
         return p[order[k] * 4 + low, here, :].astype(f32) + d2[h, k, 0].astype(f32) + d2[h, k, 1].astype(f32)
 
     def give(h):
         ysrc[h] = total(h, 0).astype(ysrc.dtype)
         across[h] = send(ysrc.at[h], ydst.at[h], 1 - high, low, sy.at[h], ry.at[h])
 
+    def start_pair(h, i):
+        open_pair[h][i] = send(p.at[(1 - high) * 4 + rings[i], rows(h * half + na, nb)], yb.at[h, i], 1 - high, low,
+                               syb.at[h, i], ryb.at[h, i])
+
+    def join(h, i):
+        open_pair[h][i].wait_recv()
+        here = slice(h * half + na, (h + 1) * half)
+        value = p[high * 4 + rings[i], here, :].astype(f32) + yb[h, i].astype(f32)
+        if i < 3:
+            joint[h, i] = value.astype(joint.dtype)
+        return value
+
+    def start_ring(h):
+        join(h, 0)
+        first_b[h] = [send(joint.at[h, 0, rows(d * hb, hb)], d1b.at[h, d], high, sides[d][0], s1b.at[h, d], r1b.at[h, d])
+                      for d in range(2)]
+        for d in range(2):
+            join(h, 1 + d)
+            raw_b[h][d] = send(joint.at[h, 1 + d, rows((1 - d) * hb, hb)], d2b.at[h, d, rows((1 - d) * hb, hb)], high, sides[d][0],
+                               srb.at[h, d], rrb.at[h, d])
+
+    def pass_ring(h):
+        for d in range(2):
+            first_b[h][d].wait_recv()
+            tmpb[h, d] = (d1b[h, d].astype(f32) + joint[h, 1 + d, d * hb:(d + 1) * hb, :].astype(f32)).astype(tmpb.dtype)
+            second_b[h][d] = send(tmpb.at[h, d], d2b.at[h, d, rows(d * hb, hb)], high, sides[d][0], s2b.at[h, d], r2b.at[h, d])
+
+    def keep(start, result):
+        here = slice(start, start + result.shape[0])
+        value = hidden_ref[here, :].astype(f32) + result
+        mixed_ref[here, :] = value
+        whole[me, here, :] = value.astype(whole.dtype)
+
     def close(h):
-        here = slice(h * half, (h + 1) * half)
         own = total(h, 1)
         across[h].wait_recv()
-        result = hidden_ref[here, :].astype(f32) + (own + ydst[h].astype(f32))
-        mixed_ref[here, :] = result
-        whole[me, here, :] = result.astype(whole.dtype)
-        gathers[h].begin()
+        keep(h * half, own + ydst[h].astype(f32))
+        pair_first[h].begin()
+
+    def close_ring(h):
+        own = join(h, 3)
+        for d in range(2):
+            raw_b[h][d].wait_recv()
+            second_b[h][d].wait_recv()
+            own = own + d2b[h, d].astype(f32)
+        keep(h * half + na, own)
+        ring_first[h].begin()
 
     sent = []
-    first, raw, second = [[None, None] for _ in range(2)], [[None, None] for _ in range(2)], [[None, None] for _ in range(2)]
+    first, second = [[None, None] for _ in range(2)], [[None, None] for _ in range(2)]
+    raw = [[[None, None], [None, None]] for _ in range(2)]
     across = [None, None]
+    open_pair = [[None] * 4 for _ in range(2)]
+    first_b, raw_b, second_b = [None, None], [[None, None] for _ in range(2)], [[None, None] for _ in range(2)]
 
     def view(pair, ring, core, piece):
         return whole.at[pair * 4 + ring, piece]
 
-    gathers = [Gather(view, lambda piece: whole.at[me, piece], mp_names, high, low, 0, gs, gr, h * copies_of(2, False),
-                      [pl.ds(h * half, quarter), pl.ds(h * half + quarter, quarter)], False) for h in range(2)]
+    def gather(kind, index, start, size):
+        return kind(view, lambda piece: whole.at[me, piece], mp_names, high, low, 0, gs, gr, index * copies_of(2, False),
+                    [pl.ds(start, size), pl.ds(start + size, size)], False)
+
+    pair_first = [gather(Gather, h, h * half, ha) for h in range(2)]
+    ring_first = [gather(RingFirst, 2 + h, h * half + na, hb) for h in range(2)]
     for h in range(2):
-        raw[h] = [[None, None], [None, None]]
         for i, b in enumerate(blocks):
             if h == 0:
                 loads[i].wait()
             product(h, b)
-            if h == 0 and i < 2:
-                first[0][i] = start_first(0, i)
-            if h == 0 and 2 <= i < 6:
-                raw[0][i % 2][i // 2 - 1] = start_raw(0, i % 2, i // 2 - 1)
+            if h == 0:
+                if i % 2 == 0:
+                    start_pair(0, i // 2)
+                if i < 2:
+                    start_first(0, i)
+                elif i < 6:
+                    start_raw(0, i % 2, i // 2 - 1)
+    for i in range(4):
+        start_pair(1, i)
     pass_on(0, 0)
+    start_ring(0)
     pass_on(0, 1)
     for k in range(2):
-        first[1][k] = start_first(1, k)
+        start_first(1, k)
+    pass_ring(0)
     for k in range(2):
         for d in range(2):
-            raw[1][k][d] = start_raw(1, k, d)
+            start_raw(1, k, d)
     give(0)
     pass_on(1, 0)
+    start_ring(1)
+    close_ring(0)
     pass_on(1, 1)
+    pass_ring(1)
     close(0)
+    ring_first[0].forward(0)
+    ring_first[0].forward(1)
     give(1)
-    early, late = gathers
-    early.second(0)
-    early.second(1)
-    early.forward(0, 0)
-    early.forward(0, 1)
+    for k in range(2):
+        pair_first[0].second(k)
+    for k in range(2):
+        pair_first[0].forward(0, k)
+    close_ring(1)
+    ring_first[0].last()
     close(1)
-    early.forward(1, 0)
-    early.forward(1, 1)
-    late.second(0)
-    late.second(1)
-    late.forward(0, 0)
-    late.forward(0, 1)
-    early.last()
-    late.forward(1, 0)
-    late.forward(1, 1)
+    for k in range(2):
+        pair_first[0].forward(1, k)
+    ring_first[1].forward(0)
+    ring_first[1].forward(1)
+    for k in range(2):
+        pair_first[1].second(k)
+    for k in range(2):
+        pair_first[1].forward(0, k)
+    ring_first[1].last()
+    pair_first[0].last()
+    ring_first[0].pairs()
+    for k in range(2):
+        pair_first[1].forward(1, k)
     write_normed(whole, gain_ref, normed_ref, 0, half, 32)
-    late.last()
+    pair_first[1].last()
+    ring_first[1].pairs()
     write_normed(whole, gain_ref, normed_ref, half, half, 32)
-    early.finish()
-    late.finish()
+    for g in pair_first + ring_first:
+        g.finish()
     for copy in sent:
         copy.wait_send()
 
@@ -618,14 +684,19 @@
     D = pltpu.SemaphoreType.DMA
     bf = jnp.bfloat16
     V = pltpu.VMEM
-    few = 2 * copies_of(2, False)
+    half = n // 2
+    na = half // 8 * 5
+    nb = half - na
+    few = 4 * copies_of(2, False)
     return pl.pallas_call(
         mix_kernel,
         out_shape=(jax.ShapeDtypeStruct((n, width), jnp.float32), jax.ShapeDtypeStruct((n, 8 * width), bf)),
         in_specs=[VM, pl.BlockSpec(memory_space=pl.ANY), VM, VM], out_specs=(VM, VM),
-        scratch_shapes=[V(w.shape, bf), V((8, n, width), bf), V((2, 2, 2, n // 4, width), bf), V((2, 2, 2, n // 4, width), bf),
-                        V((2, 2, 2, n // 2, width), bf), V((2, n // 2, width), bf), V((2, n // 2, width), bf), V((8, n, width), bf),
-                        D((8,))] + [D((2, 2, 2))] * 6 + [D((2,))] * 2 + [D((few,))] * 2,
+        scratch_shapes=[V(w.shape, bf), V((8, n, width), bf), V((2, 2, 2, na // 2, width), bf), V((2, 2, 2, na // 2, width), bf),
+                        V((2, 2, 2, na, width), bf), V((2, na, width), bf), V((2, na, width), bf), V((2, 4, nb, width), bf),
+                        V((2, 3, nb, width), bf), V((2, 2, nb // 2, width), bf), V((2, 2, nb // 2, width), bf),
+                        V((2, 2, nb, width), bf), V((8, n, width), bf), D((8,))]
+        + [D((2, 2, 2))] * 6 + [D((2,))] * 2 + [D((2, 4))] * 2 + [D((2, 2))] * 6 + [D((few,))] * 2,
         compiler_params=pltpu.CompilerParams(collective_id=cid, has_side_effects=True, vmem_limit_bytes=48 << 20),
     )(y, w, hidden, gain)
 
@@ -691,18 +762,25 @@
     every.forward(0, 1)
     mine.wait()
 
+    for copy in every.across[0:4]:
+        copy.wait_recv()
+
     def rim(j, _):
-        @pl.when((j == 0) | (pair == 1))
+        other_core = jnp.where(j % 2 == 0, core, 1 - core)
+        which = (jnp.where(j < 2, pair, 1 - pair) * 4 + ring) * 2 + other_core
+        away = place - which
+
+        @pl.when((away >= 0) & (away <= WINDOW // n))
         def _():
-            work(kv.at[jnp.where(j == 0, place, ring * 2 + core)], (jnp.where(j == 0, -n, 0), jnp.where(j == 0, 0, n)))
+            work(kv.at[which], (jnp.where(away == WINDOW // n, 0, -n), jnp.where(away == 0, 0, n)))
         return 0
 
-    lax.fori_loop(0, 2, rim, 0)
+    lax.fori_loop(0, 4, rim, 0)
     every.forward(1, 0)
     every.forward(1, 1)
-    for copy in every.across[0:12]:
+    for copy in every.across[4:12]:
         copy.wait_recv()
-    visit(12, lambda g: (jnp.where(g % 2 == 0, pair, 1 - pair), (ring + jnp.where(g < 2, 0, jnp.where(g < 4, 1, 3))) % 4))
+    visit(8, lambda g: (jnp.where(g % 2 == 0, pair, 1 - pair), (ring + jnp.where(g < 2, 1, 3)) % 4))
     every.last()
     for copy in every.across[12:]:
         copy.wait_recv()

time: 254 us -> 241 us (0.949)
  Pallas kernels: 246 us -> 233 us
    pallas_call x1, Pallas kernels: 78.2 us -> 66.5 us  [run_mix(): pl.pallas_call(mix_kernel, out_shape=(jax.ShapeDtypeStruct((n, width), jn...]
where the time goes in v7:
time: 241 us
  Pallas kernels  233 us (97%)
  local copies, waits for them, and re-layouts  7.11 us (3%)
    pallas_call x1, Pallas kernels, run_mixer(): pl.pallas_call(mixer_kernel, out_shape=(jax.ShapeDtypeStruct((n, width),...  129 us
    pallas_call x1, Pallas kernels, run_mix(): pl.pallas_call(mix_kernel, out_shape=(jax.ShapeDtypeStruct((n, width), jn...  66.5 us
    pallas_call x1, Pallas kernels, run_attention(): pl.pallas_call(attention_kernel, out_shape=jax.ShapeDtypeStruct((n, width...  37.4 us
    unnamed x16, local copies, waits for them, and re-layouts  7.11 us

profile of v7, /device:TPU:8, one launch (start us, length us, event | category | flops | bytes accessed | tf_op | source)
XLA Modules:
  0.0 240.9 jit_solution(2155726819455108256)
XLA Ops:
  0.6 129.2 %shard_map.194 = (bf16[512,1024]{1,0:T(8,128)(2,1)}, bf16[16,1024,256]{2,1,0:T(8,128)(2,1)}) custom-call(bf16[512,512]{1,0:T(8,128)(2,1)} %hidden_ref.1, bf16[256,1024]{1,0:T(8,128)(2,1)} %wx_ref.1, bf16[256,128]{1,0:T(8,128)(2,1)} %wb_ref.1, bf16[256,128]{1,0:T(8,128)(2,1)} %wc_ref.1, bf16[16,256]{1,0:T(8,128)(2,1)} %bitcast.9, bf16[256,1024]{1,0:T(8,128)(2,1)} %wz_ref.1, ...), custom_call_target="tpu_custom_call" | custom-call | tf_op jit(solution)/shard_map/pallas_call | solution.py:478
  129.8 0.0 copy-start.2
  129.8 1.0 copy-done.2
  130.9 0.0 copy-start.3
  130.9 1.2 copy-done.3
  132.1 0.0 copy-start.6
  132.1 0.7 copy-done.6
  132.8 0.0 copy-start
  132.8 0.0 copy-start.4
  132.8 0.0 copy-start.5
  132.8 66.5 %shard_map.195 = (f32[512,512]{1,0:T(8,128)S(1)}, bf16[512,4096]{1,0:T(8,128)(2,1)}) custom-call(bf16[512,1024]{1,0:T(8,128)(2,1)S(1)} %copy-done.3, bf16[16,1024,256]{2,1,0:T(8,128)(2,1)} %get-tuple-element.7.w_hbm, bf16[512,512]{1,0:T(8,128)(2,1)S(1)} %copy-done.2, f32[1,4096]{1,0:T(1,128)S(1)} %bitcast.7), custom_call_target="tpu_custom_call" | custom-call | tf_op jit(solution)/shard_map/pallas_call | solution.py:691
  199.4 0.0 copy-done
  199.4 0.0 copy-done.4
  199.4 0.0 copy-done.5
  199.4 0.0 copy-start.1
  199.4 2.2 copy-done.1
  201.6 37.4 %shard_map.196 = f32[512,512]{1,0:T(8,128)S(1)} custom-call(bf16[512,4096]{1,0:T(8,128)(2,1)S(1)} %copy-done.1, bf16[4096,512]{1,0:T(8,128)(2,1)S(1)} %copy-done, bf16[4096,128]{1,0:T(8,128)(2,1)S(1)} %copy-done.4, bf16[4096,128]{1,0:T(8,128)(2,1)S(1)} %copy-done.5), custom_call_target="tpu_custom_call" | custom-call | tf_op jit(solution)/shard_map/pallas_call | solution.py:801
  239.0 1.0 copy.23
  240.0 1.0 copy.24
Async XLA Ops:
  129.8 1.0 copy-start.2
  130.9 1.2 copy-start.3
  132.1 0.7 copy-start.6
  132.8 66.6 %copy-start = (bf16[4096,512]{1,0:T(8,128)(2,1)S(1)}, bf16[4096,512]{1,0:T(8,128)(2,1)}, u32[]{:S(2)}) copy-start(bf16[4096,512]{1,0:T(8,128)(2,1)} %wq_ref.1) | copy-start | bytes 12582916
  132.8 66.6 %copy-start.4 = (bf16[4096,128]{1,0:T(8,128)(2,1)S(1)}, bf16[4096,128]{1,0:T(8,128)(2,1)}, u32[]{:S(2)}) copy-start(bf16[4096,128]{1,0:T(8,128)(2,1)} %wk_ref.1) | copy-start | bytes 3145732
  132.8 66.6 %copy-start.5 = (bf16[4096,128]{1,0:T(8,128)(2,1)S(1)}, bf16[4096,128]{1,0:T(8,128)(2,1)}, u32[]{:S(2)}) copy-start(bf16[4096,128]{1,0:T(8,128)(2,1)} %wv_ref.1) | copy-start | bytes 3145732
  199.4 2.2 copy-start.1

commit v8 on v7

--- a/solution.py
+++ b/solution.py
@@ -40,13 +40,16 @@
         if self.fan:
             self.across.append(self.send(src, block, piece, self.pair, self.ring, 1 - self.core))
 
+    def begin_piece(self, k):
+        me, piece = (self.pair, self.ring, self.core), self.pieces[k]
+        src = self.own(piece)
+        self.y[k] = self.send(src, me, piece, 1 - self.pair, self.ring, self.core)
+        self.a[k] = [self.send(src, me, piece, self.pair, to, self.core) for to in (self.right, self.left)]
+        self.over(src, me, piece)
+
     def begin(self):
-        me = (self.pair, self.ring, self.core)
-        for k, piece in enumerate(self.pieces):
-            src = self.own(piece)
-            self.y[k] = self.send(src, me, piece, 1 - self.pair, self.ring, self.core)
-            self.a[k] = [self.send(src, me, piece, self.pair, to, self.core) for to in (self.right, self.left)]
-            self.over(src, me, piece)
+        for k in range(len(self.pieces)):
+            self.begin_piece(k)
 
     def second(self, k):
         piece, block = self.pieces[k], (1 - self.pair, self.ring, self.core)
@@ -230,15 +233,16 @@
     def out_view(pair, ring, core, piece):
         return woa.at[(pair * 4 + ring) * 2 + core, piece]
 
-    o_pair = seq_gather(Gather, out_view, wo_ref, os, orr, 0, parts[0:2])
-    o_ring = seq_gather(RingFirst, out_view, wo_ref, os, orr, fan2, parts[2:4])
+    lead = wo_ref.at[:, pl.ds(0, wo_ref.shape[1] // 2)]
+    o_pair = seq_gather(Gather, out_view, lead, os, orr, 0, parts[0:2])
+    o_ring = seq_gather(RingFirst, out_view, lead, os, orr, fan2, parts[2:4])
     own_rows = pl.ds(place * depth, depth)
     at_home = [pltpu.make_async_copy(x_ref, whole.at[mpair * 4 + mring, pl.ds(0, n)], local.at[0]),
                pltpu.make_async_copy(wx_ref, wxa.at[own_rows, :], local.at[1]),
                pltpu.make_async_copy(wbc, wba.at[own_rows, :], local.at[2]),
                pltpu.make_async_copy(wdt_ref, wda.at[:, own_rows], local.at[8]),
                pltpu.make_async_copy(wz_ref, wza.at[own_rows, :], local.at[3]),
-               pltpu.make_async_copy(wo_ref, woa.at[place], local.at[4])]
+               pltpu.make_async_copy(lead, woa.at[place], local.at[4])]
 
     def to_device(src, dst, index, device):
         copy = pltpu.make_async_remote_copy(src_ref=src, dst_ref=dst, send_sem=ts.at[index], recv_sem=tr.at[index],
@@ -247,30 +251,38 @@
         return copy
 
     shifted = to_device(x_ref.at[pl.ds(n - 16, 16)], tail, 0, {"seq": following})
-    hidden.begin()
     for copy in joined:
         copy.wait()
+    steps.begin()
     small.begin()
-    steps.begin()
-    big.begin()
+    for k in range(2):
+        big.begin_piece(k)
+        hidden.begin_piece(k)
     for copy in at_home:
         copy.start()
     shifted.wait_recv()
     edge.begin()
     home_tail = pltpu.make_async_copy(tail, whole.at[mpair * 4 + mring, pl.ds(n, 16)], local.at[5])
     home_tail.start()
+    steps.second(0)
+    small.second(0)
+    small.second(1)
     for k in range(2):
-        small.second(k)
+        big.second(k)
+        small.forward(0, k)
+        hidden.forward(0, k)
+        big.forward(0, k)
         hidden.second(k)
-        big.second(k)
-    steps.second(0)
+    steps.forward(0, 0)
+    steps.forward(1, 0)
     edge.second(0)
-    for which in range(2):
-        for k in range(2):
-            for g in (small, hidden, big):
-                g.forward(which, k)
-        steps.forward(which, 0)
-        edge.forward(which, 0)
+    edge.forward(0, 0)
+    small.forward(1, 0)
+    small.forward(1, 1)
+    for k in range(2):
+        hidden.forward(1, k)
+        big.forward(1, k)
+    edge.forward(1, 0)
     z_ring.begin()
     z_pair.begin()
     hidden.last()
@@ -477,7 +489,7 @@
         pairs += [D((size,)), D((size,))]
     return pl.pallas_call(
         mixer_kernel,
-        out_shape=(jax.ShapeDtypeStruct((n, width), bf), jax.ShapeDtypeStruct((16, tall, cols), bf)),
+        out_shape=(jax.ShapeDtypeStruct((n, width), bf), jax.ShapeDtypeStruct((16, tall, cols // 2), bf)),
         in_specs=[VM] * 15, out_specs=(VM, VM),
         scratch_shapes=[V((depth, 2 * N), bf), V((8, 128), f32), V((16, 16 * depth), bf),
                         V((8, n + 16, w), bf), V((n + 16, 8 * w), bf), V((16 * depth, width), bf), V((16 * depth, 2 * N), bf),
@@ -490,24 +502,32 @@
     )(x, wx, wb, wc, wdt, wz, wo, norm_gain, conv_x, conv_b, conv_c, bias, rate, skip, gain)
 
 
-def mix_kernel(y_ref, w_hbm, hidden_ref, gain_ref, mixed_ref, normed_ref, w, p, tmp, d1, d2, ysrc, ydst, yb, joint, tmpb, d1b, d2b, whole,
-               wsem, s1, r1, s2, r2, sraw, rraw, sy, ry, syb, ryb, s1b, r1b, s2b, r2b, srb, rrb, gs, gr):
+def mix_kernel(y_ref, w_hbm, wo_ref, hidden_ref, gain_ref, mixed_ref, normed_ref, w, p, tmp, d1, d2, ysrc, ydst, yb, joint, tmpb, d1b, d2b, whole,
+               wsem, s1, r1, s2, r2, sraw, rraw, sy, ry, syb, ryb, s1b, r1b, s2b, r2b, srb, rrb, gs, gr, ls, lr, local):
     high, low = mp_place()
     right, left, far = (low + 1) % 4, (low + 3) % 4, (low + 2) % 4
     me = high * 4 + low
     order = (1 - high, high)
     sides = ((right, left), (left, right))
     n = y_ref.shape[0]
-    half = n // 2
+    cols = w_hbm.shape[2]
+    place = lax.axis_index("seq")
+    spair, sring, score = seq_place()
     na, nb = ydst.shape[1], yb.shape[2]
     ha, hb = na // 2, nb // 2
     f32 = jnp.float32
     rings = (far, right, left, low)
     blocks = [pair * 4 + ring for ring in rings for pair in order]
-    loads = [pltpu.make_async_copy(w_hbm.at[pl.ds(2 * b, 2)], w.at[pl.ds(2 * b, 2)], wsem.at[i]) for i, b in enumerate(blocks)]
+    loads = [pltpu.make_async_copy(w_hbm.at[pl.ds(2 * b, 2)], w.at[0, pl.ds(2 * b, 2)], wsem.at[i]) for i, b in enumerate(blocks)]
     for load in loads:
         load.start()
-    greet(neighbours(mp_names, high, low, 0, False))
+    greet(neighbours(mp_names, high, low, 0, False) + neighbours(seq_names, spair, sring, score, True))
+    trail = wo_ref.at[:, pl.ds(cols, cols)]
+    later = Gather(lambda pair, ring, core, piece: w.at[1, (pair * 4 + ring) * 2 + core, piece], lambda piece: trail.at[piece],
+                   seq_names, spair, sring, score, ls, lr, 0, cut(wo_ref.shape[0], 2), True)
+    later.begin()
+    home = pltpu.make_async_copy(trail, w.at[1, place], local)
+    home.start()
 
     def send(src, dst, pair, ring, ssem, rsem):
         copy = pltpu.make_async_remote_copy(src_ref=src, dst_ref=dst, send_sem=ssem, recv_sem=rsem,
@@ -517,26 +537,23 @@
         return copy
 
     def product(h, b):
-        here = slice(h * half, (h + 1) * half)
-        cols = w.shape[2]
-        for c in range(2):
-            p[b, here, c * cols:(c + 1) * cols] = jnp.dot(
-                y_ref[here, :], w[2 * b + c], preferred_element_type=f32).astype(p.dtype)
+        both = jnp.concatenate([w[h, 2 * b], w[h, 2 * b + 1]], axis=1)
+        p[h, b] = jnp.dot(y_ref[...], both, preferred_element_type=f32).astype(p.dtype)
 
     def start_first(h, k):
-        first[h][k] = [send(p.at[order[k] * 4 + far, rows(h * half + d * ha, ha)], d1.at[h, k, d], high, sides[d][0],
+        first[h][k] = [send(p.at[h, order[k] * 4 + far, rows(d * ha, ha)], d1.at[h, k, d], high, sides[d][0],
                             s1.at[h, k, d], r1.at[h, k, d]) for d in range(2)]
 
     def start_raw(h, k, d):
-        raw[h][k][d] = send(p.at[order[k] * 4 + sides[d][0], rows(h * half + (1 - d) * ha, ha)],
+        raw[h][k][d] = send(p.at[h, order[k] * 4 + sides[d][0], rows((1 - d) * ha, ha)],
                             d2.at[h, k, d, rows((1 - d) * ha, ha)], high, sides[d][0], sraw.at[h, k, d], rraw.at[h, k, d])
 
     def pass_on(h, k):
         result = []
         for d in range(2):
             first[h][k][d].wait_recv()
-            here = slice(h * half + d * ha, h * half + (d + 1) * ha)
-            tmp[h, k, d] = (d1[h, k, d].astype(f32) + p[order[k] * 4 + sides[d][0], here, :].astype(f32)).astype(tmp.dtype)
+            here = slice(d * ha, (d + 1) * ha)
+            tmp[h, k, d] = (d1[h, k, d].astype(f32) + p[h, order[k] * 4 + sides[d][0], here, :].astype(f32)).astype(tmp.dtype)
             result.append(send(tmp.at[h, k, d], d2.at[h, k, d, rows(d * ha, ha)], high, sides[d][0],
                                s2.at[h, k, d], r2.at[h, k, d]))
         second[h][k] = result
@@ -545,21 +562,19 @@
         for d in range(2):
             raw[h][k][d].wait_recv()
             second[h][k][d].wait_recv()
-        here = slice(h * half, h * half + na)
-        return p[order[k] * 4 + low, here, :].astype(f32) + d2[h, k, 0].astype(f32) + d2[h, k, 1].astype(f32)
+        return p[h, order[k] * 4 + low, 0:na, :].astype(f32) + d2[h, k, 0].astype(f32) + d2[h, k, 1].astype(f32)
 
     def give(h):
         ysrc[h] = total(h, 0).astype(ysrc.dtype)
         across[h] = send(ysrc.at[h], ydst.at[h], 1 - high, low, sy.at[h], ry.at[h])
 
     def start_pair(h, i):
-        open_pair[h][i] = send(p.at[(1 - high) * 4 + rings[i], rows(h * half + na, nb)], yb.at[h, i], 1 - high, low,
+        open_pair[h][i] = send(p.at[h, (1 - high) * 4 + rings[i], rows(na, nb)], yb.at[h, i], 1 - high, low,
                                syb.at[h, i], ryb.at[h, i])
 
     def join(h, i):
         open_pair[h][i].wait_recv()
-        here = slice(h * half + na, (h + 1) * half)
-        value = p[high * 4 + rings[i], here, :].astype(f32) + yb[h, i].astype(f32)
+        value = p[h, high * 4 + rings[i], na:n, :].astype(f32) + yb[h, i].astype(f32)
         if i < 3:
             joint[h, i] = value.astype(joint.dtype)
         return value
@@ -579,16 +594,18 @@
             tmpb[h, d] = (d1b[h, d].astype(f32) + joint[h, 1 + d, d * hb:(d + 1) * hb, :].astype(f32)).astype(tmpb.dtype)
             second_b[h][d] = send(tmpb.at[h, d], d2b.at[h, d, rows(d * hb, hb)], high, sides[d][0], s2b.at[h, d], r2b.at[h, d])
 
-    def keep(start, result):
+    def keep(h, start, result):
         here = slice(start, start + result.shape[0])
-        value = hidden_ref[here, :].astype(f32) + result
-        mixed_ref[here, :] = value
-        whole[me, here, :] = value.astype(whole.dtype)
+        for c in range(2):
+            lanes = slice((2 * c + h) * cols, (2 * c + h + 1) * cols)
+            value = hidden_ref[here, lanes].astype(f32) + result[:, c * cols:(c + 1) * cols]
+            mixed_ref[here, lanes] = value
+            whole[h, me, here, c * cols:(c + 1) * cols] = value.astype(whole.dtype)
 
     def close(h):
         own = total(h, 1)
         across[h].wait_recv()
-        keep(h * half, own + ydst[h].astype(f32))
+        keep(h, 0, own + ydst[h].astype(f32))
         pair_first[h].begin()
 
     def close_ring(h):
@@ -597,7 +614,7 @@
             raw_b[h][d].wait_recv()
             second_b[h][d].wait_recv()
             own = own + d2b[h, d].astype(f32)
-        keep(h * half + na, own)
+        keep(h, na, own)
         ring_first[h].begin()
 
     sent = []
@@ -607,38 +624,40 @@
     open_pair = [[None] * 4 for _ in range(2)]
     first_b, raw_b, second_b = [None, None], [[None, None] for _ in range(2)], [[None, None] for _ in range(2)]
 
-    def view(pair, ring, core, piece):
-        return whole.at[pair * 4 + ring, piece]
-
-    def gather(kind, index, start, size):
-        return kind(view, lambda piece: whole.at[me, piece], mp_names, high, low, 0, gs, gr, index * copies_of(2, False),
+    def gather(kind, index, h, start, size):
+        return kind(lambda pair, ring, core, piece: whole.at[h, pair * 4 + ring, piece], lambda piece: whole.at[h, me, piece],
+                    mp_names, high, low, 0, gs, gr, index * copies_of(2, False),
                     [pl.ds(start, size), pl.ds(start + size, size)], False)
 
-    pair_first = [gather(Gather, h, h * half, ha) for h in range(2)]
-    ring_first = [gather(RingFirst, 2 + h, h * half + na, hb) for h in range(2)]
-    for h in range(2):
+    pair_first = [gather(Gather, h, h, 0, ha) for h in range(2)]
+    ring_first = [gather(RingFirst, 2 + h, h, na, hb) for h in range(2)]
+    def issue(h):
         for i, b in enumerate(blocks):
             if h == 0:
                 loads[i].wait()
             product(h, b)
-            if h == 0:
-                if i % 2 == 0:
-                    start_pair(0, i // 2)
-                if i < 2:
-                    start_first(0, i)
-                elif i < 6:
-                    start_raw(0, i % 2, i // 2 - 1)
-    for i in range(4):
-        start_pair(1, i)
+            if i % 2 == 0:
+                start_pair(h, i // 2)
+            if i < 2:
+                start_first(h, i)
+            elif i < 6:
+                start_raw(h, i % 2, i // 2 - 1)
+
+    issue(0)
     pass_on(0, 0)
+    later.second(0)
+    later.second(1)
+    later.forward(0, 0)
+    later.forward(0, 1)
     start_ring(0)
     pass_on(0, 1)
-    for k in range(2):
-        start_first(1, k)
     pass_ring(0)
-    for k in range(2):
-        for d in range(2):
-            start_raw(1, k, d)
+    later.forward(1, 0)
+    later.forward(1, 1)
+    later.last()
+    later.finish()
+    home.wait()
+    issue(1)
     give(0)
     pass_on(1, 0)
     start_ring(1)
@@ -669,36 +688,55 @@
     ring_first[0].pairs()
     for k in range(2):
         pair_first[1].forward(1, k)
-    write_normed(whole, gain_ref, normed_ref, 0, half, 32)
     pair_first[1].last()
     ring_first[1].pairs()
-    write_normed(whole, gain_ref, normed_ref, half, half, 32)
+    wide = whole.shape[3]
+
+    def norm(c, _):
+        piece = rows(pl.multiple_of(c * 32, 32), 32)
+        square = jnp.zeros((32, wide), f32)
+        for b in range(8):
+            for h in range(2):
+                value = whole[h, b, piece, :].astype(f32)
+                square = square + value * value
+        scale = lax.rsqrt(jnp.sum(square, axis=1, keepdims=True) / (16 * wide) + 1e-05)
+        for b in range(8):
+            for h in range(2):
+                for q in range(2):
+                    start = b * 2 * wide + (2 * q + h) * cols
+                    normed_ref[piece, start:start + cols] = (
+                        whole[h, b, piece, q * cols:(q + 1) * cols].astype(f32) * scale
+                        * gain_ref[:, start:start + cols]).astype(normed_ref.dtype)
+        return 0
+
+    lax.fori_loop(0, n // 32, norm, 0)
     for g in pair_first + ring_first:
         g.finish()
     for copy in sent:
         copy.wait_send()
 
 
-def run_mix(y, w, hidden, gain, cid):
+def run_mix(y, w, wo, hidden, gain, cid):
     n, width = hidden.shape
     D = pltpu.SemaphoreType.DMA
     bf = jnp.bfloat16
     V = pltpu.VMEM
-    half = n // 2
-    na = half // 8 * 5
-    nb = half - na
+    na = n // 8 * 5
+    nb = n - na
+    lanes = width // 2
     few = 4 * copies_of(2, False)
+    fan2 = copies_of(2, True)
     return pl.pallas_call(
         mix_kernel,
         out_shape=(jax.ShapeDtypeStruct((n, width), jnp.float32), jax.ShapeDtypeStruct((n, 8 * width), bf)),
-        in_specs=[VM, pl.BlockSpec(memory_space=pl.ANY), VM, VM], out_specs=(VM, VM),
-        scratch_shapes=[V(w.shape, bf), V((8, n, width), bf), V((2, 2, 2, na // 2, width), bf), V((2, 2, 2, na // 2, width), bf),
-                        V((2, 2, 2, na, width), bf), V((2, na, width), bf), V((2, na, width), bf), V((2, 4, nb, width), bf),
-                        V((2, 3, nb, width), bf), V((2, 2, nb // 2, width), bf), V((2, 2, nb // 2, width), bf),
-                        V((2, 2, nb, width), bf), V((8, n, width), bf), D((8,))]
-        + [D((2, 2, 2))] * 6 + [D((2,))] * 2 + [D((2, 4))] * 2 + [D((2, 2))] * 6 + [D((few,))] * 2,
+        in_specs=[VM, pl.BlockSpec(memory_space=pl.ANY), VM, VM, VM], out_specs=(VM, VM),
+        scratch_shapes=[V((2,) + w.shape, bf), V((2, 8, n, lanes), bf), V((2, 2, 2, na // 2, lanes), bf),
+                        V((2, 2, 2, na // 2, lanes), bf), V((2, 2, 2, na, lanes), bf), V((2, na, lanes), bf), V((2, na, lanes), bf),
+                        V((2, 4, nb, lanes), bf), V((2, 3, nb, lanes), bf), V((2, 2, nb // 2, lanes), bf),
+                        V((2, 2, nb // 2, lanes), bf), V((2, 2, nb, lanes), bf), V((2, 8, n, lanes), bf), D((8,))]
+        + [D((2, 2, 2))] * 6 + [D((2,))] * 2 + [D((2, 4))] * 2 + [D((2, 2))] * 6 + [D((few,))] * 2 + [D((fan2,))] * 2 + [D],
         compiler_params=pltpu.CompilerParams(collective_id=cid, has_side_effects=True, vmem_limit_bytes=48 << 20),
-    )(y, w, hidden, gain)
+    )(y, w, wo, hidden, gain)
 
 
 def attention_kernel(x_ref, wq_ref, wk_ref, wv_ref, out_ref, own, kv, q, peak, total, local, ss, sr):
@@ -810,10 +848,10 @@
 
 def on_device(hidden_in, norm_gain, w_z, w_x, w_b, w_c, w_dt, conv_x, conv_b, conv_c, dt_bias, a_rate,
               skip_gain, group_gain, w_out, attn_gain, w_q, w_k, w_v):
-    y_normed, w_out_all = run_mixer(
+    y_normed, w_out_half = run_mixer(
         hidden_in, w_x, w_b, w_c, w_dt.T, w_z, w_out, norm_gain[None, :], conv_x, conv_b, conv_c,
         dt_bias[None, :], a_rate[None, :], skip_gain[None, :], group_gain[None, :], 0)
-    mixed, normed_two = run_mix(y_normed, w_out_all, hidden_in, attn_gain[None, :], 1)
+    mixed, normed_two = run_mix(y_normed, w_out_half, w_out, hidden_in, attn_gain[None, :], 1)
     return (mixed, run_attention(normed_two, w_q, w_k, w_v, 2))
 
 

time: 241 us -> 239 us (level)
  Pallas kernels: 233 us -> 229 us
    pallas_call x1, Pallas kernels: 129 us -> 115 us  [run_mixer(): pl.pallas_call(mixer_kernel, out_shape=(jax.ShapeDtypeStruct((n, width),...]
    pallas_call x1, Pallas kernels: 66.5 us -> 77.7 us  [run_mix(): pl.pallas_call(mix_kernel, out_shape=(jax.ShapeDtypeStruct((n, width), jn...]
    unnamed x16 -> x18, local copies, waits for them, and re-layouts: 7.11 us -> 8.52 us
where the time goes in v8:
time: 239 us; the launch traced here: 238 us
  Pallas kernels  229 us (96%)
  local copies, waits for them, and re-layouts  8.52 us (4%)
    pallas_call x1, Pallas kernels, run_mixer(): pl.pallas_call(mixer_kernel, out_shape=(jax.ShapeDtypeStruct((n, width),...  115 us
    pallas_call x1, Pallas kernels, run_mix(): pl.pallas_call(mix_kernel, out_shape=(jax.ShapeDtypeStruct((n, width), jn...  77.7 us
    pallas_call x1, Pallas kernels, run_attention(): pl.pallas_call(attention_kernel, out_shape=jax.ShapeDtypeStruct((n, width...  36.6 us
    unnamed x18, local copies, waits for them, and re-layouts  8.52 us

profile of v8, /device:TPU:8, one launch (start us, length us, event | category | flops | bytes accessed | tf_op | source)
XLA Modules:
  0.0 238.0 jit_solution(17464523169866658361)
XLA Ops:
  0.6 114.5 %shard_map.194 = (bf16[512,1024]{1,0:T(8,128)(2,1)}, bf16[16,1024,128]{2,1,0:T(8,128)(2,1)}) custom-call(bf16[512,512]{1,0:T(8,128)(2,1)} %hidden_ref.1, bf16[256,1024]{1,0:T(8,128)(2,1)} %wx_ref.1, bf16[256,128]{1,0:T(8,128)(2,1)} %wb_ref.1, bf16[256,128]{1,0:T(8,128)(2,1)} %wc_ref.1, bf16[16,256]{1,0:T(8,128)(2,1)} %bitcast.9, bf16[256,1024]{1,0:T(8,128)(2,1)} %wz_ref.1, ...), custom_call_target="tpu_custom_call" | custom-call | tf_op jit(solution)/shard_map/pallas_call | solution.py:490
  115.1 0.0 copy-start
  115.2 0.0 copy-start.2
  115.2 1.2 copy-done.2
  116.4 0.0 copy-start.3
  116.4 1.3 copy-done.3
  117.6 0.0 copy-start.4
  117.6 1.2 copy-done.4
  118.8 0.0 copy-start.7
  118.8 0.7 copy-done.7
  119.6 0.0 copy-start.5
  119.6 0.0 copy-start.6
  119.6 77.7 %shard_map.195 = (f32[512,512]{1,0:T(8,128)S(1)}, bf16[512,4096]{1,0:T(8,128)(2,1)}) custom-call(bf16[512,1024]{1,0:T(8,128)(2,1)S(1)} %copy-done.4, bf16[16,1024,128]{2,1,0:T(8,128)(2,1)} %get-tuple-element.7.w_hbm, bf16[1024,256]{1,0:T(8,128)(2,1)S(1)} %copy-done.3, bf16[512,512]{1,0:T(8,128)(2,1)S(1)} %copy-done.2, f32[1,4096]{1,0:T(1,128)S(1)} %bitcast.7), custom_call_target="tpu_custom_call" | custom-call | tf_op jit(solution)/shard_map/pallas_call | solution.py:729
  197.2 0.0 copy-done
  197.2 0.0 copy-done.5
  197.2 0.0 copy-done.6
  197.3 0.0 copy-start.1
  197.3 2.2 copy-done.1
  199.4 36.6 %shard_map.196 = f32[512,512]{1,0:T(8,128)S(1)} custom-call(bf16[512,4096]{1,0:T(8,128)(2,1)S(1)} %copy-done.1, bf16[4096,512]{1,0:T(8,128)(2,1)S(1)} %copy-done, bf16[4096,128]{1,0:T(8,128)(2,1)S(1)} %copy-done.5, bf16[4096,128]{1,0:T(8,128)(2,1)S(1)} %copy-done.6), custom_call_target="tpu_custom_call" | custom-call | tf_op jit(solution)/shard_map/pallas_call | solution.py:839
  236.1 1.0 copy.23
  237.0 1.0 copy.24
Async XLA Ops:
  115.1 82.1 %copy-start = (bf16[4096,512]{1,0:T(8,128)(2,1)S(1)}, bf16[4096,512]{1,0:T(8,128)(2,1)}, u32[]{:S(2)}) copy-start(bf16[4096,512]{1,0:T(8,128)(2,1)} %wq_ref.1) | copy-start | bytes 12582916
  115.2 1.2 copy-start.2
  116.4 1.3 copy-start.3
  117.6 1.2 copy-start.4
  118.8 0.7 copy-start.7
  119.6 77.7 %copy-start.5 = (bf16[4096,128]{1,0:T(8,128)(2,1)S(1)}, bf16[4096,128]{1,0:T(8,128)(2,1)}, u32[]{:S(2)}) copy-start(bf16[4096,128]{1,0:T(8,128)(2,1)} %wk_ref.1) | copy-start | bytes 3145732
  119.6 77.7 %copy-start.6 = (bf16[4096,128]{1,0:T(8,128)(2,1)S(1)}, bf16[4096,128]{1,0:T(8,128)(2,1)}, u32[]{:S(2)}) copy-start(bf16[4096,128]{1,0:T(8,128)(2,1)} %wv_ref.1) | copy-start | bytes 3145732
  197.3 2.2 copy-start.1

commit v9 on v8

--- a/solution.py
+++ b/solution.py
@@ -7,6 +7,7 @@
 
 MESH = pl.DeviceIdType.MESH
 VM = pl.BlockSpec(memory_space=pltpu.VMEM)
+ANY = pl.BlockSpec(memory_space=pl.ANY)
 P_SIZE = 64
 N = 128
 HD = 128
@@ -502,7 +503,7 @@
     )(x, wx, wb, wc, wdt, wz, wo, norm_gain, conv_x, conv_b, conv_c, bias, rate, skip, gain)
 
 
-def mix_kernel(y_ref, w_hbm, wo_ref, hidden_ref, gain_ref, mixed_ref, normed_ref, w, p, tmp, d1, d2, ysrc, ydst, yb, joint, tmpb, d1b, d2b, whole,
+def mix_kernel(y_hbm, w_hbm, wo_ref, hidden_hbm, gain_hbm, mixed_ref, normed_ref, y_ref, gain_ref, hidden_ref, w, p, tmp, d1, d2, ysrc, ydst, yb, joint, tmpb, d1b, d2b, whole,
                wsem, s1, r1, s2, r2, sraw, rraw, sy, ry, syb, ryb, s1b, r1b, s2b, r2b, srb, rrb, gs, gr, ls, lr, local):
     high, low = mp_place()
     right, left, far = (low + 1) % 4, (low + 3) % 4, (low + 2) % 4
@@ -519,6 +520,8 @@
     rings = (far, right, left, low)
     blocks = [pair * 4 + ring for ring in rings for pair in order]
     loads = [pltpu.make_async_copy(w_hbm.at[pl.ds(2 * b, 2)], w.at[0, pl.ds(2 * b, 2)], wsem.at[i]) for i, b in enumerate(blocks)]
+    arriving = pltpu.make_async_copy(y_hbm, y_ref, local.at[2])
+    arriving.start()
     for load in loads:
         load.start()
     greet(neighbours(mp_names, high, low, 0, False) + neighbours(seq_names, spair, sring, score, True))
@@ -526,8 +529,12 @@
     later = Gather(lambda pair, ring, core, piece: w.at[1, (pair * 4 + ring) * 2 + core, piece], lambda piece: trail.at[piece],
                    seq_names, spair, sring, score, ls, lr, 0, cut(wo_ref.shape[0], 2), True)
     later.begin()
-    home = pltpu.make_async_copy(trail, w.at[1, place], local)
+    home = pltpu.make_async_copy(trail, w.at[1, place], local.at[0])
     home.start()
+    fetched = [pltpu.make_async_copy(hidden_hbm, hidden_ref, local.at[1]), pltpu.make_async_copy(gain_hbm, gain_ref, local.at[3])]
+    for copy in fetched:
+        copy.start()
+    arriving.wait()
 
     def send(src, dst, pair, ring, ssem, rsem):
         copy = pltpu.make_async_remote_copy(src_ref=src, dst_ref=dst, send_sem=ssem, recv_sem=rsem,
@@ -652,31 +659,34 @@
     start_ring(0)
     pass_on(0, 1)
     pass_ring(0)
+    give(0)
     later.forward(1, 0)
     later.forward(1, 1)
+    for copy in fetched:
+        copy.wait()
+    close_ring(0)
+    close(0)
     later.last()
-    later.finish()
+    ring_first[0].forward(0)
+    ring_first[0].forward(1)
+    for copy in later.across:
+        copy.wait_recv()
     home.wait()
     issue(1)
-    give(0)
+    for k in range(2):
+        pair_first[0].second(k)
     pass_on(1, 0)
     start_ring(1)
-    close_ring(0)
     pass_on(1, 1)
     pass_ring(1)
-    close(0)
-    ring_first[0].forward(0)
-    ring_first[0].forward(1)
-    give(1)
-    for k in range(2):
-        pair_first[0].second(k)
     for k in range(2):
         pair_first[0].forward(0, k)
+    ring_first[0].last()
+    give(1)
     close_ring(1)
-    ring_first[0].last()
-    close(1)
     for k in range(2):
         pair_first[0].forward(1, k)
+    close(1)
     ring_first[1].forward(0)
     ring_first[1].forward(1)
     for k in range(2):
@@ -712,7 +722,7 @@
     lax.fori_loop(0, n // 32, norm, 0)
     for g in pair_first + ring_first:
         g.finish()
-    for copy in sent:
+    for copy in sent + later.started:
         copy.wait_send()
 
 
@@ -729,31 +739,39 @@
     return pl.pallas_call(
         mix_kernel,
         out_shape=(jax.ShapeDtypeStruct((n, width), jnp.float32), jax.ShapeDtypeStruct((n, 8 * width), bf)),
-        in_specs=[VM, pl.BlockSpec(memory_space=pl.ANY), VM, VM, VM], out_specs=(VM, VM),
-        scratch_shapes=[V((2,) + w.shape, bf), V((2, 8, n, lanes), bf), V((2, 2, 2, na // 2, lanes), bf),
+        in_specs=[ANY] * 5, out_specs=(VM, VM),
+        scratch_shapes=[V(y.shape, bf), V(gain.shape, jnp.float32), V((n, width), bf), V((2,) + w.shape, bf), V((2, 8, n, lanes), bf), V((2, 2, 2, na // 2, lanes), bf),
                         V((2, 2, 2, na // 2, lanes), bf), V((2, 2, 2, na, lanes), bf), V((2, na, lanes), bf), V((2, na, lanes), bf),
                         V((2, 4, nb, lanes), bf), V((2, 3, nb, lanes), bf), V((2, 2, nb // 2, lanes), bf),
                         V((2, 2, nb // 2, lanes), bf), V((2, 2, nb, lanes), bf), V((2, 8, n, lanes), bf), D((8,))]
-        + [D((2, 2, 2))] * 6 + [D((2,))] * 2 + [D((2, 4))] * 2 + [D((2, 2))] * 6 + [D((few,))] * 2 + [D((fan2,))] * 2 + [D],
-        compiler_params=pltpu.CompilerParams(collective_id=cid, has_side_effects=True, vmem_limit_bytes=48 << 20),
+        + [D((2, 2, 2))] * 6 + [D((2,))] * 2 + [D((2, 4))] * 2 + [D((2, 2))] * 6 + [D((few,))] * 2 + [D((fan2,))] * 2 + [D((4,))],
+        compiler_params=pltpu.CompilerParams(collective_id=cid, has_side_effects=True, vmem_limit_bytes=63 << 20),
     )(y, w, wo, hidden, gain)
 
 
-def attention_kernel(x_ref, wq_ref, wk_ref, wv_ref, out_ref, own, kv, q, peak, total, local, ss, sr):
+def attention_kernel(x_hbm, wq_hbm, wk_hbm, wv_hbm, out_ref, x_ref, wq_ref, wk_ref, wv_ref, wsem, own, kv, q, peak, total, local, ss, sr):
     place = lax.axis_index("seq")
     pair, ring, core = seq_place()
+    loads = [pltpu.make_async_copy(src, dst, wsem.at[i])
+             for i, (src, dst) in enumerate(((x_hbm, x_ref), (wk_hbm, wk_ref), (wv_hbm, wv_ref), (wq_hbm, wq_ref)))]
+    for load in loads:
+        load.start()
     greet(neighbours(seq_names, pair, ring, core, True))
     n = x_ref.shape[0]
     heads = q.shape[0]
     bf, f32 = jnp.bfloat16, jnp.float32
     scale = HD ** -0.5 * 1.4426950408889634
+    loads[0].wait()
+    loads[1].wait()
     own[:, 0:HD] = jnp.dot(x_ref[...], wk_ref[...], preferred_element_type=f32).astype(bf)
+    loads[2].wait()
     own[:, HD:2 * HD] = jnp.dot(x_ref[...], wv_ref[...], preferred_element_type=f32).astype(bf)
     every = Gather(lambda pair, ring, core, piece: kv.at[(pair * 4 + ring) * 2 + core, piece], lambda piece: own.at[piece],
                    seq_names, pair, ring, core, ss, sr, 0, cut(n, 2), True)
     every.begin()
     mine = pltpu.make_async_copy(own, kv.at[place], local)
     mine.start()
+    loads[3].wait()
     for h in range(0, heads, 2):
         both = jnp.dot(x_ref[...], wq_ref[:, h * HD:(h + 2) * HD], preferred_element_type=f32) * scale
         q[h] = both[:, 0:HD].astype(bf)
@@ -839,10 +857,11 @@
     return pl.pallas_call(
         attention_kernel,
         out_shape=jax.ShapeDtypeStruct((n, width), f32),
-        in_specs=[VM] * 4, out_specs=VM,
-        scratch_shapes=[pltpu.VMEM((n, 2 * HD), bf), pltpu.VMEM((16, n, 2 * HD), bf), pltpu.VMEM((heads, n, HD), bf),
+        in_specs=[ANY] * 4, out_specs=VM,
+        scratch_shapes=[pltpu.VMEM(x.shape, bf), pltpu.VMEM(wq.shape, bf), pltpu.VMEM(wk.shape, bf), pltpu.VMEM(wv.shape, bf), D((4,)),
+                        pltpu.VMEM((n, 2 * HD), bf), pltpu.VMEM((16, n, 2 * HD), bf), pltpu.VMEM((heads, n, HD), bf),
                         pltpu.VMEM((heads, n, HD), f32), pltpu.VMEM((heads, n, 2 * HD), f32), D, D((many,)), D((many,))],
-        compiler_params=pltpu.CompilerParams(collective_id=cid, has_side_effects=True, vmem_limit_bytes=40 << 20),
+        compiler_params=pltpu.CompilerParams(collective_id=cid, has_side_effects=True, vmem_limit_bytes=63 << 20),
     )(x, wq, wk, wv)
 
 

time: 239 us -> 237 us (level)
  local copies, waits for them, and re-layouts: 8.52 us -> 4.52 us
    pallas_call x1, Pallas kernels: 36.6 us -> 42 us  [run_attention(): pl.pallas_call(attention_kernel, out_shape=jax.ShapeDtypeStruct((n, width...]
    unnamed x18 -> x2, local copies, waits for them, and re-layouts: 8.52 us -> 4.52 us
    pallas_call x1, Pallas kernels: 77.7 us -> 74.8 us  [run_mix(): pl.pallas_call(mix_kernel, out_shape=(jax.ShapeDtypeStruct((n, width), jn...]
where the time goes in v9:
time: 237 us
  Pallas kernels  231 us (97%)
  local copies, waits for them, and re-layouts  4.52 us (2%)
    pallas_call x1, Pallas kernels, run_mixer(): pl.pallas_call(mixer_kernel, out_shape=(jax.ShapeDtypeStruct((n, width),...  115 us
    pallas_call x1, Pallas kernels, run_mix(): pl.pallas_call(mix_kernel, out_shape=(jax.ShapeDtypeStruct((n, width), jn...  74.8 us
    pallas_call x1, Pallas kernels, run_attention(): pl.pallas_call(attention_kernel, out_shape=jax.ShapeDtypeStruct((n, width...  42 us

profile of v9, /device:TPU:8, one launch (start us, length us, event | category | flops | bytes accessed | tf_op | source)
XLA Modules:
  0.0 236.5 jit_solution(12067972479970166638)
XLA Ops:
  0.6 114.5 %shard_map.194 = (bf16[512,1024]{1,0:T(8,128)(2,1)}, bf16[16,1024,128]{2,1,0:T(8,128)(2,1)}) custom-call(bf16[512,512]{1,0:T(8,128)(2,1)} %hidden_hbm.1, bf16[256,1024]{1,0:T(8,128)(2,1)} %wx_ref.1, bf16[256,128]{1,0:T(8,128)(2,1)} %wb_ref.1, bf16[256,128]{1,0:T(8,128)(2,1)} %wc_ref.1, bf16[16,256]{1,0:T(8,128)(2,1)} %bitcast.9, bf16[256,1024]{1,0:T(8,128)(2,1)} %wz_ref.1, ...), custom_call_target="tpu_custom_call" | custom-call | tf_op jit(solution)/shard_map/pallas_call | solution.py:491
  115.2 74.8 %shard_map.195 = (f32[512,512]{1,0:T(8,128)}, bf16[512,4096]{1,0:T(8,128)(2,1)}) custom-call(bf16[512,1024]{1,0:T(8,128)(2,1)} %get-tuple-element.6.y_hbm, bf16[16,1024,128]{2,1,0:T(8,128)(2,1)} %get-tuple-element.7.w_hbm, bf16[1024,256]{1,0:T(8,128)(2,1)} %wo_ref.3, bf16[512,512]{1,0:T(8,128)(2,1)} %hidden_hbm.1, f32[1,4096]{1,0:T(1,128)} %bitcast.8), custom_call_target="tpu_custom_call" | custom-call | tf_op jit(solution)/shard_map/pallas_call | solution.py:739
  190.0 42.0 %shard_map.196 = f32[512,512]{1,0:T(8,128)} custom-call(bf16[512,4096]{1,0:T(8,128)(2,1)} %get-tuple-element.9.x_hbm, bf16[4096,512]{1,0:T(8,128)(2,1)} %wq_hbm.1, bf16[4096,128]{1,0:T(8,128)(2,1)} %wk_hbm.1, bf16[4096,128]{1,0:T(8,128)(2,1)} %wv_hbm.1), custom_call_target="tpu_custom_call" | custom-call | tf_op jit(solution)/shard_map/pallas_call | solution.py:857
  232.0 2.3 copy.23
  234.3 2.3 copy.24

commit v10 on v9

--- a/solution.py
+++ b/solution.py
@@ -7,7 +7,7 @@
 
 MESH = pl.DeviceIdType.MESH
 VM = pl.BlockSpec(memory_space=pltpu.VMEM)
-ANY = pl.BlockSpec(memory_space=pl.ANY)
+FAR = pl.BlockSpec(memory_space=pltpu.HBM)
 P_SIZE = 64
 N = 128
 HD = 128
@@ -739,39 +739,34 @@
     return pl.pallas_call(
         mix_kernel,
         out_shape=(jax.ShapeDtypeStruct((n, width), jnp.float32), jax.ShapeDtypeStruct((n, 8 * width), bf)),
-        in_specs=[ANY] * 5, out_specs=(VM, VM),
+        in_specs=[FAR] * 5, out_specs=(VM, VM),
         scratch_shapes=[V(y.shape, bf), V(gain.shape, jnp.float32), V((n, width), bf), V((2,) + w.shape, bf), V((2, 8, n, lanes), bf), V((2, 2, 2, na // 2, lanes), bf),
                         V((2, 2, 2, na // 2, lanes), bf), V((2, 2, 2, na, lanes), bf), V((2, na, lanes), bf), V((2, na, lanes), bf),
                         V((2, 4, nb, lanes), bf), V((2, 3, nb, lanes), bf), V((2, 2, nb // 2, lanes), bf),
                         V((2, 2, nb // 2, lanes), bf), V((2, 2, nb, lanes), bf), V((2, 8, n, lanes), bf), D((8,))]
         + [D((2, 2, 2))] * 6 + [D((2,))] * 2 + [D((2, 4))] * 2 + [D((2, 2))] * 6 + [D((few,))] * 2 + [D((fan2,))] * 2 + [D((4,))],
-        compiler_params=pltpu.CompilerParams(collective_id=cid, has_side_effects=True, vmem_limit_bytes=63 << 20),
+        compiler_params=pltpu.CompilerParams(collective_id=cid, has_side_effects=True, vmem_limit_bytes=44 << 20),
     )(y, w, wo, hidden, gain)
 
 
-def attention_kernel(x_hbm, wq_hbm, wk_hbm, wv_hbm, out_ref, x_ref, wq_ref, wk_ref, wv_ref, wsem, own, kv, q, peak, total, local, ss, sr):
+def attention_kernel(x_hbm, wq_ref, wk_ref, wv_ref, out_ref, x_ref, xsem, own, kv, q, peak, total, local, ss, sr):
     place = lax.axis_index("seq")
     pair, ring, core = seq_place()
-    loads = [pltpu.make_async_copy(src, dst, wsem.at[i])
-             for i, (src, dst) in enumerate(((x_hbm, x_ref), (wk_hbm, wk_ref), (wv_hbm, wv_ref), (wq_hbm, wq_ref)))]
-    for load in loads:
-        load.start()
+    load = pltpu.make_async_copy(x_hbm, x_ref, xsem)
+    load.start()
     greet(neighbours(seq_names, pair, ring, core, True))
     n = x_ref.shape[0]
     heads = q.shape[0]
     bf, f32 = jnp.bfloat16, jnp.float32
     scale = HD ** -0.5 * 1.4426950408889634
-    loads[0].wait()
-    loads[1].wait()
+    load.wait()
     own[:, 0:HD] = jnp.dot(x_ref[...], wk_ref[...], preferred_element_type=f32).astype(bf)
-    loads[2].wait()
     own[:, HD:2 * HD] = jnp.dot(x_ref[...], wv_ref[...], preferred_element_type=f32).astype(bf)
     every = Gather(lambda pair, ring, core, piece: kv.at[(pair * 4 + ring) * 2 + core, piece], lambda piece: own.at[piece],
                    seq_names, pair, ring, core, ss, sr, 0, cut(n, 2), True)
     every.begin()
     mine = pltpu.make_async_copy(own, kv.at[place], local)
     mine.start()
-    loads[3].wait()
     for h in range(0, heads, 2):
         both = jnp.dot(x_ref[...], wq_ref[:, h * HD:(h + 2) * HD], preferred_element_type=f32) * scale
         q[h] = both[:, 0:HD].astype(bf)
@@ -857,11 +852,11 @@
     return pl.pallas_call(
         attention_kernel,
         out_shape=jax.ShapeDtypeStruct((n, width), f32),
-        in_specs=[ANY] * 4, out_specs=VM,
-        scratch_shapes=[pltpu.VMEM(x.shape, bf), pltpu.VMEM(wq.shape, bf), pltpu.VMEM(wk.shape, bf), pltpu.VMEM(wv.shape, bf), D((4,)),
+        in_specs=[FAR, VM, VM, VM], out_specs=VM,
+        scratch_shapes=[pltpu.VMEM(x.shape, bf), D,
                         pltpu.VMEM((n, 2 * HD), bf), pltpu.VMEM((16, n, 2 * HD), bf), pltpu.VMEM((heads, n, HD), bf),
                         pltpu.VMEM((heads, n, HD), f32), pltpu.VMEM((heads, n, 2 * HD), f32), D, D((many,)), D((many,))],
-        compiler_params=pltpu.CompilerParams(collective_id=cid, has_side_effects=True, vmem_limit_bytes=63 << 20),
+        compiler_params=pltpu.CompilerParams(collective_id=cid, has_side_effects=True, vmem_limit_bytes=40 << 20),
     )(x, wq, wk, wv)
 
 

time: 237 us -> 232 us (0.979)
  Pallas kernels: 231 us -> 225 us
    pallas_call x1, Pallas kernels: 42 us -> 37.8 us  [run_attention(): pl.pallas_call(attention_kernel, out_shape=jax.ShapeDtypeStruct((n, width...]
    unnamed x2 -> x16, local copies, waits for them, and re-layouts: 4.52 us -> 6.34 us
where the time goes in v10:
time: 232 us
  Pallas kernels  225 us (97%)
  local copies, waits for them, and re-layouts  6.34 us (3%)
    pallas_call x1, Pallas kernels, run_mixer(): pl.pallas_call(mixer_kernel, out_shape=(jax.ShapeDtypeStruct((n, width),...  114 us
    pallas_call x1, Pallas kernels, run_mix(): pl.pallas_call(mix_kernel, out_shape=(jax.ShapeDtypeStruct((n, width), jn...  72.7 us
    pallas_call x1, Pallas kernels, run_attention(): pl.pallas_call(attention_kernel, out_shape=jax.ShapeDtypeStruct((n, width...  37.8 us
    unnamed x16, local copies, waits for them, and re-layouts  6.34 us

profile of v10, /device:TPU:8, one launch (start us, length us, event | category | flops | bytes accessed | tf_op | source)
XLA Modules:
  0.0 232.1 jit_solution(7646851626145718434)
XLA Ops:
  0.6 114.5 %shard_map.194 = (bf16[512,1024]{1,0:T(8,128)(2,1)}, bf16[16,1024,128]{2,1,0:T(8,128)(2,1)}) custom-call(bf16[512,512]{1,0:T(8,128)(2,1)} %hidden_hbm.1, bf16[256,1024]{1,0:T(8,128)(2,1)} %wx_ref.1, bf16[256,128]{1,0:T(8,128)(2,1)} %wb_ref.1, bf16[256,128]{1,0:T(8,128)(2,1)} %wc_ref.1, bf16[16,256]{1,0:T(8,128)(2,1)} %bitcast.9, bf16[256,1024]{1,0:T(8,128)(2,1)} %wz_ref.1, ...), custom_call_target="tpu_custom_call" | custom-call | tf_op jit(solution)/shard_map/pallas_call | solution.py:491
  115.1 0.0 copy-start
  115.1 0.0 copy-start.1
  115.2 1.2 copy-done.1
  116.3 0.0 copy-start.2
  116.3 1.3 copy-done.2
  117.6 0.0 copy-start.3
  117.6 1.2 copy-done.3
  118.8 0.0 copy-start.6
  118.8 0.7 copy-done.6
  119.5 0.0 copy-start.4
  119.5 0.0 copy-start.5
  119.5 72.7 %shard_map.195 = (f32[512,512]{1,0:T(8,128)S(1)}, bf16[512,4096]{1,0:T(8,128)(2,1)S(1)}) custom-call(bf16[512,1024]{1,0:T(8,128)(2,1)S(1)} %copy-done.3, bf16[16,1024,128]{2,1,0:T(8,128)(2,1)} %get-tuple-element.7.w_hbm, bf16[1024,256]{1,0:T(8,128)(2,1)S(1)} %copy-done.2, bf16[512,512]{1,0:T(8,128)(2,1)S(1)} %copy-done.1, f32[1,4096]{1,0:T(1,128)S(1)} %bitcast.7), custom_call_target="tpu_custom_call" | custom-call | tf_op jit(solution)/shard_map/pallas_call | solution.py:739
  192.3 0.0 copy-done
  192.3 0.0 copy-done.4
  192.3 0.0 copy-done.5
  192.3 37.8 %shard_map.196 = f32[512,512]{1,0:T(8,128)S(1)} custom-call(bf16[512,4096]{1,0:T(8,128)(2,1)S(1)} %get-tuple-element.9.x_hbm, bf16[4096,512]{1,0:T(8,128)(2,1)S(1)} %copy-done, bf16[4096,128]{1,0:T(8,128)(2,1)S(1)} %copy-done.4, bf16[4096,128]{1,0:T(8,128)(2,1)S(1)} %copy-done.5), custom_call_target="tpu_custom_call" | custom-call | tf_op jit(solution)/shard_map/pallas_call | solution.py:852
  230.1 1.0 copy.23
  231.1 1.0 copy.24
Async XLA Ops:
  115.1 77.1 %copy-start = (bf16[4096,512]{1,0:T(8,128)(2,1)S(1)}, bf16[4096,512]{1,0:T(8,128)(2,1)}, u32[]{:S(2)}) copy-start(bf16[4096,512]{1,0:T(8,128)(2,1)} %wq_ref.1) | copy-start | bytes 12582916
  115.1 1.2 copy-start.1
  116.3 1.3 copy-start.2
  117.6 1.2 copy-start.3
  118.8 0.7 copy-start.6
  119.5 72.7 %copy-start.4 = (bf16[4096,128]{1,0:T(8,128)(2,1)S(1)}, bf16[4096,128]{1,0:T(8,128)(2,1)}, u32[]{:S(2)}) copy-start(bf16[4096,128]{1,0:T(8,128)(2,1)} %wk_ref.1) | copy-start | bytes 3145732
  119.5 72.7 %copy-start.5 = (bf16[4096,128]{1,0:T(8,128)(2,1)S(1)}, bf16[4096,128]{1,0:T(8,128)(2,1)}, u32[]{:S(2)}) copy-start(bf16[4096,128]{1,0:T(8,128)(2,1)} %wv_ref.1) | copy-start | bytes 3145732
